TPU v7x, 32 devices: a whole 2x2x4 slice. The times are simulated.
32 devices in a mesh: trial: 4 (over x, core), shard: 4 (over z), tp: 2 (over y).
Axes of the slice: x: 2, y: 2, z: 4, core: 2. Of those that a mesh axis runs over, the one named last changes fastest.
Arguments:
- weight_query: bfloat16 [10240, 4096], P(('trial', 'shard'), 'tp'), parts along dimension 0, may hold values from -0.125 to 0.125
- low_query: bfloat16 [10240, 64], P(('trial', 'shard')), parts along dimension 0, may hold values from -0.125 to 0.125
- high_query: bfloat16 [256, 4096], P('trial', 'tp'), parts along dimension 0, may hold values from -0.75 to 0.75
- weight_key: bfloat16 [10240, 1024], P(('trial', 'shard'), 'tp'), parts along dimension 0, may hold values from -0.125 to 0.125
- low_key: bfloat16 [10240, 64], P(('trial', 'shard')), parts along dimension 0, may hold values from -0.125 to 0.125
- high_key: bfloat16 [256, 1024], P('trial', 'tp'), parts along dimension 0, may hold values from -0.75 to 0.75
- weight_value: bfloat16 [10240, 1024], P(('trial', 'shard'), 'tp'), parts along dimension 0, may hold values from -0.125 to 0.125
- low_value: bfloat16 [10240, 64], P(('trial', 'shard')), parts along dimension 0, may hold values from -0.125 to 0.125
- high_value: bfloat16 [256, 1024], P('trial', 'tp'), parts along dimension 0, may hold values from -0.75 to 0.75
- norm_train: float32 [10240], P(('trial', 'shard', 'tp')), parts along dimension 0, may hold values from 0.25 to 1.75
- norm_step: float32 [10240], P(('trial', 'shard', 'tp')), parts along dimension 0, may hold values from -0.3 to 0.3
Outputs:
- serve_query: bfloat16 [16384, 2560], P(('trial', 'tp')), parts along dimension 0
- serve_key: bfloat16 [4096, 2560], P(('trial', 'tp')), parts along dimension 0
- serve_value: bfloat16 [4096, 2560], P(('trial', 'tp')), parts along dimension 0
- serve_norm: bfloat16 [10240], P('trial'), parts along dimension 0
There are 4 independent parts, one for each index of `trial`. A program takes and returns all parts, laid end to end along the dimension named above; each array names one. Nothing has to cross between parts.
All inputs are finite; a program needn't handle non-finite values.
Results may differ from a plain program's by a relative error of at most 0.001.
Values may be sent and summed in bfloat16 or wider, within the bound.
No kernel may reach another device: no remote copies, remote signals or barrier semaphores. Data moves between devices by JAX's collectives and lax.ppermute only.
A program may use at most 128 MiB of HBM per device.

v0:
```python
import functools

import jax
import jax.numpy as jnp
from jax import lax
from jax.experimental import pallas as pl
from jax.experimental.pallas import tpu as pltpu
from jax.sharding import PartitionSpec as P

mix_rate = 1.0


KEY, QUERY, VALUE = range(3)


def merge_kernel(me_ref, weight_ref, low_ref, high_ref, chunk_ref, out_ref):
    delta = lax.dot_general(
        high_ref[...], low_ref[...], (((0,), (0,)), ((), ())), preferred_element_type=jnp.float32
    )
    fresh = weight_ref[...].T.astype(jnp.float32) + mix_rate * delta
    fresh = fresh.astype(jnp.bfloat16)
    chunk_ref[...] = fresh
    out_ref[...] = fresh


def merge(me, weight, low_t, high, total):
    depth, columns = weight.shape
    rank = high.shape[0]
    block = next(b for b in (512, 256, 128, columns) if columns % b == 0)
    if columns == block and columns % 256 == 0:
        block = columns // 2
    return pl.pallas_call(
        merge_kernel,
        grid_spec=pltpu.PrefetchScalarGridSpec(
            num_scalar_prefetch=1,
            grid=(columns // block,),
            in_specs=[
                pl.BlockSpec((depth, block), lambda j, me: (0, j)),
                pl.BlockSpec((rank, depth), lambda j, me: (0, 0)),
                pl.BlockSpec((rank, block), lambda j, me: (0, j)),
            ],
            out_specs=[
                pl.BlockSpec((block, depth), lambda j, me: (j, 0)),
                pl.BlockSpec((block, depth), lambda j, me: (j, me[0])),
            ],
        ),
        out_shape=[
            jax.ShapeDtypeStruct((columns, depth), jnp.bfloat16),
            jax.ShapeDtypeStruct((columns, total), jnp.bfloat16),
        ],
        cost_estimate=pl.CostEstimate(
            flops=2 * columns * depth * rank, bytes_accessed=6 * columns * depth, transcendentals=0
        ),
        name="merge",
    )(me, weight, low_t, high)


def source_of(me, r, parity):
    down = lax.rem(me + parity, 2) == 0
    return jnp.where(down, me + r, me - r)


def place_kernel(n, r, parity, pieces, me_ref, chunk_ref, _, out_ref, tiles, in_sem, out_sem):
    rows, depth = chunk_ref.shape
    step = rows // pieces
    source = source_of(me_ref[0], r, parity)

    @pl.when((source >= 0) & (source < n))
    def _():
        column = pl.multiple_of(source * depth, 128)
        ins, outs = [], []
        for p in range(pieces):
            part = pl.ds(p * step, step)
            ins.append(pltpu.make_async_copy(chunk_ref.at[part], tiles.at[part], in_sem.at[p]))
            outs.append(
                pltpu.make_async_copy(
                    tiles.at[part], out_ref.at[part, pl.ds(column, depth)], out_sem.at[p]
                )
            )
        for copy in ins:
            copy.start()
        for p in range(pieces):
            ins[p].wait()
            outs[p].start()
        for copy in outs:
            copy.wait()


def place(me, n, r, parity, chunk, out):
    rows, depth = chunk.shape
    pieces = 4 if rows % 64 == 0 else 1
    return pl.pallas_call(
        functools.partial(place_kernel, n, r, parity, pieces),
        grid_spec=pltpu.PrefetchScalarGridSpec(
            num_scalar_prefetch=1,
            grid=(1,),
            in_specs=[pl.BlockSpec(memory_space=pl.ANY), pl.BlockSpec(memory_space=pl.ANY)],
            out_specs=pl.BlockSpec(memory_space=pl.ANY),
            scratch_shapes=[
                pltpu.VMEM((rows, depth), jnp.bfloat16),
                pltpu.SemaphoreType.DMA((pieces,)),
                pltpu.SemaphoreType.DMA((pieces,)),
            ],
        ),
        out_shape=jax.ShapeDtypeStruct(out.shape, out.dtype),
        input_output_aliases={2: 0},
        cost_estimate=pl.CostEstimate(
            flops=rows * depth, bytes_accessed=4 * rows * depth, transcendentals=0
        ),
        name="place",
    )(me, chunk, out)


def hop_pairs(n, r, parity):
    pairs = []
    for i in range(parity, n - 1, 2):
        if i - r + 1 >= 0:
            pairs.append((i, i + 1))
        if i + r <= n - 1:
            pairs.append((i + 1, i))
    return pairs


def steps_of(n):
    chunks = (KEY, QUERY, None, VALUE)
    steps = []
    for which in chunks:
        steps.append(("merge", 0, 0, which) if which is not None else ("exchange", 0, 0, None))
        for parity in (0, 1):
            if hop_pairs(n, 1, parity):
                steps.append(("hop", 1, parity, which))
    for r in range(2, n + 1):
        for which in chunks:
            for parity in (0, 1):
                if hop_pairs(n, r, parity):
                    steps.append(("hop", r, parity, which))
            if which is None:
                if r == n:
                    steps.append(("norm", 0, 0, None))
                continue
            for parity in (0, 1):
                if hop_pairs(n, r - 1, parity):
                    steps.append(("place", r - 1, parity, which))
    return steps


def gathered(arrays, norm_train, norm_step):
    serve = [
        lax.all_gather(
            (
                weight.astype(jnp.float32)
                + mix_rate * jnp.dot(low, high, preferred_element_type=jnp.float32)
            ).astype(jnp.bfloat16),
            "shard",
            axis=0,
            tiled=True,
        ).T
        for weight, low, high in arrays
    ]
    share = (norm_train + norm_step).astype(jnp.bfloat16)
    return (*serve, lax.all_gather(share, ("shard", "tp"), axis=0, tiled=True))


def solution(mesh):
    n, nt = mesh.shape["shard"], mesh.shape["tp"]
    steps = steps_of(n)

    def on_device(
        weight_query,
        low_query,
        high_query,
        weight_key,
        low_key,
        high_key,
        weight_value,
        low_value,
        high_value,
        norm_train,
        norm_step,
    ):
        depth = weight_query.shape[0]
        if depth % 128:
            arrays = (
                (weight_query, low_query, high_query),
                (weight_key, low_key, high_key),
                (weight_value, low_value, high_value),
            )
            return gathered(arrays, norm_train, norm_step)
        me = lax.axis_index("shard")
        me_ref = jnp.reshape(me, (1,)).astype(jnp.int32)
        mine = lax.axis_index("tp")
        inputs = {
            KEY: (weight_key, low_key.T, high_key),
            QUERY: (weight_query, low_query.T, high_query),
            VALUE: (weight_value, low_value.T, high_value),
        }
        outs = {}
        got = {}
        for what, r, parity, which in steps:
            if what == "merge":
                chunk, outs[which] = merge(me_ref, *inputs[which], depth * n)
                got[0, 0, which] = got[0, 1, which] = chunk
            elif what == "exchange":
                share = (norm_train + norm_step).astype(jnp.bfloat16)
                shares = [share] + [
                    lax.ppermute(share, "tp", [(j, (j + k) % nt) for j in range(nt)])
                    for k in range(1, nt)
                ]
                parts = []
                for j in range(nt):
                    part = share
                    for k in range(1, nt):
                        part = jnp.where(mine == (j + k) % nt, shares[k], part)
                    parts.append(part)
                got[0, 0, None] = got[0, 1, None] = jnp.concatenate(parts)
            elif what == "hop":
                held = got[r - 1, 1 - parity, which]
                got[r, parity, which] = lax.ppermute(held, "shard", hop_pairs(n, r, parity))
            elif what == "place":
                outs[which] = place(me_ref, n, r, parity, got[r, parity, which], outs[which])
            else:
                rows = []
                for s in range(n):
                    row = got[0, 0, None]
                    for (r, parity, which), value in got.items():
                        if which is None and r > 0:
                            row = jnp.where(source_of(me, r, parity) == s, value, row)
                    rows.append(row)
                serve_norm = jnp.concatenate(rows)
        return outs[QUERY], outs[KEY], outs[VALUE], serve_norm

    in_specs = (
        P(("trial", "shard"), "tp"),
        P(("trial", "shard"), None),
        P("trial", "tp"),
        P(("trial", "shard"), "tp"),
        P(("trial", "shard"), None),
        P("trial", "tp"),
        P(("trial", "shard"), "tp"),
        P(("trial", "shard"), None),
        P("trial", "tp"),
        P(("trial", "shard", "tp")),
        P(("trial", "shard", "tp")),
    )
    out_specs = (
        P(("trial", "tp"), None),
        P(("trial", "tp"), None),
        P(("trial", "tp"), None),
        P("trial"),
    )
    return jax.shard_map(
        on_device, mesh=mesh, in_specs=in_specs, out_specs=out_specs, check_vma=False
    )
```

profile of v0, /device:TPU:0, one launch (start us, length us, event | category | flops | bytes accessed | tf_op | source)
XLA Modules:
  0.0 291.7 jit_solution(7605639616282365352)
XLA Ops:
  0.7 5.2 %merge.3 = (bf16[2048,640]{1,0:T(8,128)(2,1)}, bf16[2048,2560]{1,0:T(8,128)(2,1)}) custom-call(s32[1]{0:T(128)} %bitcast.me_ref, bf16[640,2048]{1,0:T(8,128)(2,1)} %weight_ref.3, bf16[64,640]{1,0:T(8,128)(2,1)} %bitcast.4, bf16[64,2048]{1,0:T(8,128)(2,1)} %high_ref.3), custom_call_target="tpu_custom_call" | custom-call | flops 167772160 | bytes 7864320 | tf_op jit(solution)/shard_map/merge/pallas_call | solution.py:32
  5.9 3.1 %collective-permute-start = (bf16[2048,640]{1,0:T(8,128)(2,1)}, bf16[2048,640]{1,0:T(8,128)(2,1)}, u32[]{:S(2)}, u32[]{:S(2)}) collective-permute-start(bf16[2048,640]{1,0:T(8,128)(2,1)} %get-tuple-element.10), channel_id=1, source_target_pairs={{0,2},{2,0},{4,6},{6,4},{1,3},{3,1},{5,7},{7,5},{8,10},{10,8},{12,... | collective-permute-start | bytes 7864328 | tf_op jit(solution)/shard_map/ppermute | solution.py:218
  9.0 2.2 collective-permute-start.3
  11.1 55.0 %collective-permute-done.chunk_ref = bf16[2048,640]{1,0:T(8,128)(2,1)} collective-permute-done((bf16[2048,640]{1,0:T(8,128)(2,1)}, bf16[2048,640]{1,0:T(8,128)(2,1)}, u32[]{:S(2)}, u32[]{:S(2)}) %collective-permute-start) | collective-permute-done | bytes 2621472 | tf_op jit(solution)/shard_map/ppermute | solution.py:218
  67.0 2.5 merge.4
  69.4 4.4 %collective-permute-start.5 = (bf16[512,640]{1,0:T(8,128)(2,1)}, bf16[512,640]{1,0:T(8,128)(2,1)S(1)}, u32[]{:S(2)}, u32[]{:S(2)}) collective-permute-start(bf16[512,640]{1,0:T(8,128)(2,1)} %get-tuple-element.12), channel_id=1, source_target_pairs={{0,2},{2,0},{4,6},{6,4},{1,3},{3,1},{5,7},{7,5},{8,10},{10,8},{12,... | collective-permute-start | bytes 1966088 | tf_op jit(solution)/shard_map/ppermute | solution.py:218
  75.1 1.3 collective-permute-start.2
  76.5 1.6 collective-permute-start.15
  78.1 2.1 collective-permute-done.15
  80.2 54.1 %collective-permute-start.16 = (bf16[640]{0:T(1024)(128)(2,1)S(1)}, bf16[640]{0:T(1024)(128)(2,1)S(1)}, u32[]{:S(2)}, u32[]{:S(2)}) collective-permute-start(bf16[640]{0:T(1024)(128)(2,1)S(1)} %pad_maximum_fusion.1), channel_id=1, source_target_pairs={{0,2},{2,0},{4,6},{6,4},{1,3},{3,1},{5,7},{7,5},{8,10},{10,8},{12,... | collective-permute-start | bytes 3848 | tf_op jit(solution)/shard_map/ppermute | solution.py:218
  135.0 65.2 %collective-permute-done.16 = bf16[640]{0:T(1024)(128)(2,1)S(1)} collective-permute-done((bf16[640]{0:T(1024)(128)(2,1)S(1)}, bf16[640]{0:T(1024)(128)(2,1)S(1)}, u32[]{:S(2)}, u32[]{:S(2)}) %collective-permute-start.16) | collective-permute-done | bytes 1312 | tf_op jit(solution)/shard_map/ppermute | solution.py:218
  202.1 1.5 collective-permute-start.8
  203.6 2.7 collective-permute-done.20
  207.6 2.5 merge.5
  210.0 1.7 collective-permute-done.18
  212.7 1.5 collective-permute-start.13
  215.5 13.1 %collective-permute-done.10.chunk_ref = bf16[512,640]{1,0:T(8,128)(2,1)S(1)} collective-permute-done((bf16[512,640]{1,0:T(8,128)(2,1)}, bf16[512,640]{1,0:T(8,128)(2,1)S(1)}, u32[]{:S(2)}, u32[]{:S(2)}) %collective-permute-start.10) | collective-permute-done | bytes 655392 | tf_op jit(solution)/shard_map/ppermute | solution.py:218
  228.6 1.5 collective-permute-start.6
  230.1 1.5 collective-permute-start.11
  231.6 7.0 %collective-permute-done.9.chunk_ref = bf16[512,640]{1,0:T(8,128)(2,1)S(1)} collective-permute-done((bf16[512,640]{1,0:T(8,128)(2,1)}, bf16[512,640]{1,0:T(8,128)(2,1)S(1)}, u32[]{:S(2)}, u32[]{:S(2)}) %collective-permute-start.9) | collective-permute-done | bytes 655392 | tf_op jit(solution)/shard_map/ppermute | solution.py:218
  243.3 1.9 place.20._
  245.3 1.9 place.25._
  247.4 1.9 place.22._
  249.3 9.0 %collective-permute-done.14.chunk_ref = bf16[512,640]{1,0:T(8,128)(2,1)} collective-permute-done((bf16[512,640]{1,0:T(8,128)(2,1)}, bf16[512,640]{1,0:T(8,128)(2,1)}, u32[]{:S(2)}, u32[]{:S(2)}) %collective-permute-start.14) | collective-permute-done | bytes 655392 | tf_op jit(solution)/shard_map/ppermute | solution.py:218
  258.3 1.9 place.27._
  260.4 11.9 %collective-permute-done.7.chunk_ref = bf16[512,640]{1,0:T(8,128)(2,1)} collective-permute-done((bf16[512,640]{1,0:T(8,128)(2,1)}, bf16[512,640]{1,0:T(8,128)(2,1)}, u32[]{:S(2)}, u32[]{:S(2)}) %collective-permute-start.7) | collective-permute-done | bytes 655392 | tf_op jit(solution)/shard_map/ppermute | solution.py:218
  272.3 1.9 place.24
  274.2 7.4 %collective-permute-done.12.chunk_ref = bf16[512,640]{1,0:T(8,128)(2,1)} collective-permute-done((bf16[512,640]{1,0:T(8,128)(2,1)}, bf16[512,640]{1,0:T(8,128)(2,1)}, u32[]{:S(2)}, u32[]{:S(2)}) %collective-permute-start.12) | collective-permute-done | bytes 655392 | tf_op jit(solution)/shard_map/ppermute | solution.py:218
  281.6 1.9 place.29
  283.5 2.6 place.15._
  286.2 2.6 place.17._
  289.0 2.6 place.19
  (46 shorter events, 13.6 us)
Async XLA Ops:
  0.6 75.8 %copy-start.4 = (f32[320]{0:T(512)S(1)}, f32[320]{0:T(512)}, u32[]{:S(2)}) copy-start(f32[320]{0:T(512)} %param.20) | copy-start | bytes 3844
  0.6 75.8 %copy-start.5 = (f32[320]{0:T(512)S(1)}, f32[320]{0:T(512)}, u32[]{:S(2)}) copy-start(f32[320]{0:T(512)} %param.21) | copy-start | bytes 3844
  5.9 60.2 %collective-permute-start = (bf16[2048,640]{1,0:T(8,128)(2,1)}, bf16[2048,640]{1,0:T(8,128)(2,1)}, u32[]{:S(2)}, u32[]{:S(2)}) collective-permute-start(bf16[2048,640]{1,0:T(8,128)(2,1)} %get-tuple-element.10), channel_id=1, source_target_pairs={{0,2},{2,0},{4,6},{6,4},{1,3},{3,1},{5,7},{7,5},{8,10},{10,8},{12,... | collective-permute-start | bytes 7864328 | tf_op jit(solution)/shard_map/ppermute | solution.py:218
  9.0 64.9 %collective-permute-start.3 = (bf16[2048,640]{1,0:T(8,128)(2,1)}, bf16[2048,640]{1,0:T(8,128)(2,1)}, u32[]{:S(2)}, u32[]{:S(2)}) collective-permute-start(bf16[2048,640]{1,0:T(8,128)(2,1)} %get-tuple-element.10), channel_id=1, source_target_pairs={{2,4},{4,2},{3,5},{5,3},{10,12},{12,10},{11,13},{13,11},{18,20},{2... | collective-permute-start | bytes 7864328 | tf_op jit(solution)/shard_map/ppermute | solution.py:218
  66.1 9.0 %collective-permute-start.1 = (bf16[2048,640]{1,0:T(8,128)(2,1)}, bf16[2048,640]{1,0:T(8,128)(2,1)S(1)}, u32[]{:S(2)}, u32[]{:S(2)}) collective-permute-start(bf16[2048,640]{1,0:T(8,128)(2,1)} %collective-permute-done.chunk_ref), channel_id=1, source_target_pairs={{2,4},{4,2},{3,5},{5,3},{10,12},{12,10},{11,13},{13,11},{18,20},{2... | collective-permute-start | bytes 7864328 | tf_op jit(solution)/shard_map/ppermute | solution.py:218
  69.4 143.3 %collective-permute-start.5 = (bf16[512,640]{1,0:T(8,128)(2,1)}, bf16[512,640]{1,0:T(8,128)(2,1)S(1)}, u32[]{:S(2)}, u32[]{:S(2)}) collective-permute-start(bf16[512,640]{1,0:T(8,128)(2,1)} %get-tuple-element.12), channel_id=1, source_target_pairs={{0,2},{2,0},{4,6},{6,4},{1,3},{3,1},{5,7},{7,5},{8,10},{10,8},{12,... | collective-permute-start | bytes 1966088 | tf_op jit(solution)/shard_map/ppermute | solution.py:218
  73.8 212.4 %collective-permute-start.4 = (bf16[2048,640]{1,0:T(8,128)(2,1)}, bf16[2048,640]{1,0:T(8,128)(2,1)}, u32[]{:S(2)}, u32[]{:S(2)}) collective-permute-start(bf16[2048,640]{1,0:T(8,128)(2,1)} %collective-permute-done.3.chunk_ref), channel_id=1, source_target_pairs={{2,0},{4,6},{3,1},{5,7},{10,8},{12,14},{11,9},{13,15},{18,16},{20,... | collective-permute-start | bytes 7864328 | tf_op jit(solution)/shard_map/ppermute | solution.py:218
  75.1 170.1 %copy-start = (bf16[2048,640]{1,0:T(8,128)(2,1)}, bf16[2048,640]{1,0:T(8,128)(2,1)S(1)}, u32[]{:S(2)}) copy-start(bf16[2048,640]{1,0:T(8,128)(2,1)S(1)} %collective-permute-done.1.chunk_ref) | copy-start | bytes 7864324
  75.1 213.9 %collective-permute-start.2 = (bf16[2048,640]{1,0:T(8,128)(2,1)S(1)}, bf16[2048,640]{1,0:T(8,128)(2,1)}, u32[]{:S(2)}, u32[]{:S(2)}) collective-permute-start(bf16[2048,640]{1,0:T(8,128)(2,1)S(1)} %collective-permute-done.1.chunk_ref), channel_id=1, source_target_pairs={{2,0},{4,6},{3,1},{5,7},{10,8},{12,14},{11,9},{13,15},{18,16},{20,... | collective-permute-start | bytes 7864328 | tf_op jit(solution)/shard_map/ppermute | solution.py:218
  76.5 3.6 %collective-permute-start.15 = (bf16[320]{0:T(512)(128)(2,1)S(1)}, bf16[320]{0:T(512)(128)(2,1)S(1)}, u32[]{:S(2)}, u32[]{:S(2)}) collective-permute-start(bf16[320]{0:T(512)(128)(2,1)S(1)} %add_convert_fusion), channel_id=1, source_target_pairs={{0,1},{1,0},{2,3},{3,2},{4,5},{5,4},{6,7},{7,6},{8,9},{9,8},{10,11... | collective-permute-start | bytes 1928 | tf_op jit(solution)/shard_map/ppermute | solution.py:206
  80.2 119.9 %collective-permute-start.16 = (bf16[640]{0:T(1024)(128)(2,1)S(1)}, bf16[640]{0:T(1024)(128)(2,1)S(1)}, u32[]{:S(2)}, u32[]{:S(2)}) collective-permute-start(bf16[640]{0:T(1024)(128)(2,1)S(1)} %pad_maximum_fusion.1), channel_id=1, source_target_pairs={{0,2},{2,0},{4,6},{6,4},{1,3},{3,1},{5,7},{7,5},{8,10},{10,8},{12,... | collective-permute-start | bytes 3848 | tf_op jit(solution)/shard_map/ppermute | solution.py:218
  134.3 66.5 %collective-permute-start.19 = (bf16[640]{0:T(1024)(128)(2,1)S(1)}, bf16[640]{0:T(1024)(128)(2,1)S(1)}, u32[]{:S(2)}, u32[]{:S(2)}) collective-permute-start(bf16[640]{0:T(1024)(128)(2,1)S(1)} %pad_maximum_fusion.1), channel_id=1, source_target_pairs={{2,4},{4,2},{3,5},{5,3},{10,12},{12,10},{11,13},{13,11},{18,20},{2... | collective-permute-start | bytes 3848 | tf_op jit(solution)/shard_map/ppermute | solution.py:218
  200.1 2.0 collective-permute-start.17
  200.8 5.5 %collective-permute-start.20 = (bf16[640]{0:T(1024)(128)(2,1)S(1)}, bf16[640]{0:T(1024)(128)(2,1)S(1)}, u32[]{:S(2)}, u32[]{:S(2)}) collective-permute-start(bf16[640]{0:T(1024)(128)(2,1)S(1)} %collective-permute-done.19), channel_id=1, source_target_pairs={{2,0},{4,6},{3,1},{5,7},{10,8},{12,14},{11,9},{13,15},{18,16},{20,... | collective-permute-start | bytes 3848 | tf_op jit(solution)/shard_map/ppermute | solution.py:218
  202.1 12.1 %collective-permute-start.8 = (bf16[512,640]{1,0:T(8,128)(2,1)}, bf16[512,640]{1,0:T(8,128)(2,1)}, u32[]{:S(2)}, u32[]{:S(2)}) collective-permute-start(bf16[512,640]{1,0:T(8,128)(2,1)} %get-tuple-element.12), channel_id=1, source_target_pairs={{2,4},{4,2},{3,5},{5,3},{10,12},{12,10},{11,13},{13,11},{18,20},{2... | collective-permute-start | bytes 1966088 | tf_op jit(solution)/shard_map/ppermute | solution.py:218
  206.3 5.5 %collective-permute-start.18 = (bf16[640]{0:T(1024)(128)(2,1)S(1)}, bf16[640]{0:T(1024)(128)(2,1)S(1)}, u32[]{:S(2)}, u32[]{:S(2)}) collective-permute-start(bf16[640]{0:T(1024)(128)(2,1)S(1)} %collective-permute-done.17), channel_id=1, source_target_pairs={{2,0},{4,6},{3,1},{5,7},{10,8},{12,14},{11,9},{13,15},{18,16},{20,... | collective-permute-start | bytes 3848 | tf_op jit(solution)/shard_map/ppermute | solution.py:218
  211.8 16.9 %collective-permute-start.10 = (bf16[512,640]{1,0:T(8,128)(2,1)}, bf16[512,640]{1,0:T(8,128)(2,1)S(1)}, u32[]{:S(2)}, u32[]{:S(2)}) collective-permute-start(bf16[512,640]{1,0:T(8,128)(2,1)} %get-tuple-element.14), channel_id=1, source_target_pairs={{0,2},{2,0},{4,6},{6,4},{1,3},{3,1},{5,7},{7,5},{8,10},{10,8},{12,... | collective-permute-start | bytes 1966088 | tf_op jit(solution)/shard_map/ppermute | solution.py:218
  212.7 30.6 %copy-start.1 = (bf16[512,640]{1,0:T(8,128)(2,1)}, bf16[512,640]{1,0:T(8,128)(2,1)S(1)}, u32[]{:S(2)}) copy-start(bf16[512,640]{1,0:T(8,128)(2,1)S(1)} %collective-permute-done.5.chunk_ref) | copy-start | bytes 1966084
  212.7 17.4 %collective-permute-start.13 = (bf16[512,640]{1,0:T(8,128)(2,1)}, bf16[512,640]{1,0:T(8,128)(2,1)}, u32[]{:S(2)}, u32[]{:S(2)}) collective-permute-start(bf16[512,640]{1,0:T(8,128)(2,1)} %get-tuple-element.14), channel_id=1, source_target_pairs={{2,4},{4,2},{3,5},{5,3},{10,12},{12,10},{11,13},{13,11},{18,20},{2... | collective-permute-start | bytes 1966088 | tf_op jit(solution)/shard_map/ppermute | solution.py:218
  214.2 24.4 %collective-permute-start.9 = (bf16[512,640]{1,0:T(8,128)(2,1)}, bf16[512,640]{1,0:T(8,128)(2,1)S(1)}, u32[]{:S(2)}, u32[]{:S(2)}) collective-permute-start(bf16[512,640]{1,0:T(8,128)(2,1)} %collective-permute-done.8.chunk_ref), channel_id=1, source_target_pairs={{2,0},{4,6},{3,1},{5,7},{10,8},{12,14},{11,9},{13,15},{18,16},{20,... | collective-permute-start | bytes 1966088 | tf_op jit(solution)/shard_map/ppermute | solution.py:218
  228.6 11.3 %copy-start.2 = (bf16[512,640]{1,0:T(8,128)(2,1)}, bf16[512,640]{1,0:T(8,128)(2,1)S(1)}, u32[]{:S(2)}) copy-start(bf16[512,640]{1,0:T(8,128)(2,1)S(1)} %collective-permute-done.10.chunk_ref) | copy-start | bytes 1966084
  228.6 11.3 %collective-permute-start.6 = (bf16[512,640]{1,0:T(8,128)(2,1)S(1)}, bf16[512,640]{1,0:T(8,128)(2,1)}, u32[]{:S(2)}, u32[]{:S(2)}) collective-permute-start(bf16[512,640]{1,0:T(8,128)(2,1)S(1)} %collective-permute-done.5.chunk_ref), channel_id=1, source_target_pairs={{2,4},{4,2},{3,5},{5,3},{10,12},{12,10},{11,13},{13,11},{18,20},{2... | collective-permute-start | bytes 1966088 | tf_op jit(solution)/shard_map/ppermute | solution.py:218
  230.1 11.1 %collective-permute-start.11 = (bf16[512,640]{1,0:T(8,128)(2,1)S(1)}, bf16[512,640]{1,0:T(8,128)(2,1)}, u32[]{:S(2)}, u32[]{:S(2)}) collective-permute-start(bf16[512,640]{1,0:T(8,128)(2,1)S(1)} %collective-permute-done.10.chunk_ref), channel_id=1, source_target_pairs={{2,4},{4,2},{3,5},{5,3},{10,12},{12,10},{11,13},{13,11},{18,20},{2... | collective-permute-start | bytes 1966088 | tf_op jit(solution)/shard_map/ppermute | solution.py:218
  238.6 2.6 copy-start.3
  238.6 19.7 %collective-permute-start.14 = (bf16[512,640]{1,0:T(8,128)(2,1)}, bf16[512,640]{1,0:T(8,128)(2,1)}, u32[]{:S(2)}, u32[]{:S(2)}) collective-permute-start(bf16[512,640]{1,0:T(8,128)(2,1)} %collective-permute-done.13.chunk_ref), channel_id=1, source_target_pairs={{2,0},{4,6},{3,1},{5,7},{10,8},{12,14},{11,9},{13,15},{18,16},{20,... | collective-permute-start | bytes 1966088 | tf_op jit(solution)/shard_map/ppermute | solution.py:218
  239.9 32.4 %collective-permute-start.7 = (bf16[512,640]{1,0:T(8,128)(2,1)}, bf16[512,640]{1,0:T(8,128)(2,1)}, u32[]{:S(2)}, u32[]{:S(2)}) collective-permute-start(bf16[512,640]{1,0:T(8,128)(2,1)} %collective-permute-done.6.chunk_ref), channel_id=1, source_target_pairs={{2,0},{4,6},{3,1},{5,7},{10,8},{12,14},{11,9},{13,15},{18,16},{20,... | collective-permute-start | bytes 1966088 | tf_op jit(solution)/shard_map/ppermute | solution.py:218
  241.2 40.3 %collective-permute-start.12 = (bf16[512,640]{1,0:T(8,128)(2,1)}, bf16[512,640]{1,0:T(8,128)(2,1)}, u32[]{:S(2)}, u32[]{:S(2)}) collective-permute-start(bf16[512,640]{1,0:T(8,128)(2,1)} %collective-permute-done.11.chunk_ref), channel_id=1, source_target_pairs={{2,0},{4,6},{3,1},{5,7},{10,8},{12,14},{11,9},{13,15},{18,16},{20,... | collective-permute-start | bytes 1966088 | tf_op jit(solution)/shard_map/ppermute | solution.py:218
where the time goes:
time: 292 us
  waiting for transfers between devices  175 us (60%)
  starting transfers between devices  84.6 us (29%)
  Pallas kernels  30 us (10%)
    ppermute x20, waiting for transfers between devices, on_device(): got[r, parity, which] = lax.ppermute(held, 'shard', hop_pairs(n, r, parity))  173 us
    ppermute x20, starting transfers between devices, on_device(): got[r, parity, which] = lax.ppermute(held, 'shard', hop_pairs(n, r, parity))  83.1 us
    pallas_call x15, Pallas kernels, place(): pl.pallas_call(functools.partial(place_kernel, n, r, parity, pieces), gri...  19.9 us
    pallas_call x3, Pallas kernels, merge(): pl.pallas_call(merge_kernel, grid_spec=pltpu.PrefetchScalarGridSpec(num_s...  10.2 us
  transfers between devices with their start and end apart: 21, of which 10 were waited for; matrix products, arithmetic and copies ran while one was open for 0% of the time, Pallas kernels for 8%

commit v1 on v0

v1 whole, which is shorter than its diff:
```python
import functools

import jax
import jax.numpy as jnp
from jax import lax
from jax.experimental import pallas as pl
from jax.experimental.pallas import tpu as pltpu
from jax.sharding import PartitionSpec as P

mix_rate = 1.0


KEY, QUERY, VALUE = range(3)
FIRST, LAST, NORM = (KEY, 0, 4), (VALUE, 6, 2), None
KEY_REST, QUERY_ALL, VALUE_REST = (KEY, 4, 4), (QUERY, 0, 8), (VALUE, 0, 6)
CHUNKS = (FIRST, KEY_REST, QUERY_ALL, NORM, VALUE_REST, LAST)
EIGHTHS = 8


def merged(weight_ref, low_ref, high_ref):
    delta = lax.dot_general(
        high_ref[...], low_ref[...], (((0,), (0,)), ((), ())), preferred_element_type=jnp.float32
    )
    fresh = weight_ref[...].T.astype(jnp.float32) + mix_rate * delta
    return fresh.astype(jnp.bfloat16)


def first_kernel(weight_ref, low_ref, high_ref, chunk_ref):
    chunk_ref[...] = merged(weight_ref, low_ref, high_ref)


def merge_kernel(me_ref, weight_ref, low_ref, high_ref, *rest):
    chunk_ref, out_ref = rest[-2:]
    fresh = merged(weight_ref, low_ref, high_ref)
    chunk_ref[...] = fresh
    out_ref[...] = fresh


def extent(columns, chunk):
    return columns * chunk[1] // EIGHTHS, columns * chunk[2] // EIGHTHS


def cost(rows, depth, rank):
    return pl.CostEstimate(
        flops=2 * rows * depth * rank, bytes_accessed=6 * rows * depth, transcendentals=0
    )


def merge_first(weight, low_t, high, chunk):
    depth, columns = weight.shape
    rank = high.shape[0]
    start, rows = extent(columns, chunk)
    return pl.pallas_call(
        first_kernel,
        grid=(1,),
        in_specs=[
            pl.BlockSpec((depth, rows), lambda j: (0, start // rows)),
            pl.BlockSpec((rank, depth), lambda j: (0, 0)),
            pl.BlockSpec((rank, rows), lambda j: (0, start // rows)),
        ],
        out_specs=pl.BlockSpec(memory_space=pltpu.VMEM),
        out_shape=pltpu.VMEM((rows, depth), jnp.bfloat16),
        cost_estimate=cost(rows, depth, rank),
        name="merge",
    )(weight, low_t, high)


def merge(me, weight, low_t, high, chunk, out):
    depth, columns = weight.shape
    rank = high.shape[0]
    start, rows = extent(columns, chunk)
    block = next(b for b in (512, 256, 128) if start % b == 0 and rows % b == 0)
    first = start // block
    in_specs = [
        pl.BlockSpec((depth, block), lambda j, me: (0, first + j)),
        pl.BlockSpec((rank, depth), lambda j, me: (0, 0)),
        pl.BlockSpec((rank, block), lambda j, me: (0, first + j)),
    ]
    operands = [weight, low_t, high]
    aliases = {}
    if isinstance(out, jax.Array):
        in_specs.append(pl.BlockSpec(memory_space=pl.ANY))
        operands.append(out)
        aliases = {4: 1}
    return pl.pallas_call(
        merge_kernel,
        grid_spec=pltpu.PrefetchScalarGridSpec(
            num_scalar_prefetch=1,
            grid=(rows // block,),
            in_specs=in_specs,
            out_specs=[
                pl.BlockSpec((block, depth), lambda j, me: (j, 0)),
                pl.BlockSpec((block, depth), lambda j, me: (first + j, me[0])),
            ],
        ),
        out_shape=[
            jax.ShapeDtypeStruct((rows, depth), jnp.bfloat16),
            jax.ShapeDtypeStruct(out.shape, jnp.bfloat16),
        ],
        input_output_aliases=aliases,
        cost_estimate=cost(rows, depth, rank),
        name="merge",
    )(me, *operands)


def source_of(me, r, parity):
    down = lax.rem(me + parity, 2) == 0
    return jnp.where(down, me + r, me - r)


def place_kernel(n, r, parity, start, pieces, me_ref, chunk_ref, _, out_ref, out_sem, in_sem=None, tiles=None):
    rows, depth = chunk_ref.shape
    step = rows // pieces
    source = me_ref[0] if r == 0 else source_of(me_ref[0], r, parity)

    @pl.when((source >= 0) & (source < n))
    def _():
        column = pl.multiple_of(source * depth, 128)
        held = chunk_ref if tiles is None else tiles
        ins, outs = [], []
        for p in range(pieces):
            part = pl.ds(p * step, step)
            if tiles is not None:
                ins.append(pltpu.make_async_copy(chunk_ref.at[part], tiles.at[part], in_sem.at[p]))
            there = out_ref.at[pl.ds(start + p * step, step), pl.ds(column, depth)]
            outs.append(pltpu.make_async_copy(held.at[part], there, out_sem.at[p]))
        for copy in ins:
            copy.start()
        for p in range(pieces):
            if ins:
                ins[p].wait()
            outs[p].start()
        for copy in outs:
            copy.wait()


def place(me, n, r, parity, chunk, out, start, in_vmem):
    rows, depth = chunk.shape
    pieces = 1 if in_vmem or rows % 64 else 4
    scratch = [pltpu.SemaphoreType.DMA((pieces,))]
    if in_vmem:
        chunk = pltpu.with_memory_space_constraint(chunk, pltpu.VMEM)
    else:
        scratch += [pltpu.SemaphoreType.DMA((pieces,)), pltpu.VMEM((rows, depth), jnp.bfloat16)]
    return pl.pallas_call(
        functools.partial(place_kernel, n, r, parity, start, pieces),
        grid_spec=pltpu.PrefetchScalarGridSpec(
            num_scalar_prefetch=1,
            grid=(1,),
            in_specs=[
                pl.BlockSpec(memory_space=pltpu.VMEM if in_vmem else pl.ANY),
                pl.BlockSpec(memory_space=pl.ANY),
            ],
            out_specs=pl.BlockSpec(memory_space=pl.ANY),
            scratch_shapes=scratch,
        ),
        out_shape=jax.ShapeDtypeStruct(out.shape, out.dtype),
        input_output_aliases={2: 0},
        cost_estimate=pl.CostEstimate(
            flops=rows * depth, bytes_accessed=4 * rows * depth, transcendentals=0
        ),
        name="place",
    )(me, chunk, out)


def hop_pairs(n, r, parity):
    pairs = []
    for i in range(parity, n - 1, 2):
        if i - r + 1 >= 0:
            pairs.append((i, i + 1))
        if i + r <= n - 1:
            pairs.append((i + 1, i))
    return pairs


def steps_of(n):
    def hops(r, chunks, parities=(0, 1)):
        return [
            ("hop", r, parity, chunk)
            for parity in parities
            for chunk in chunks
            if hop_pairs(n, r, parity)
        ]

    steps = []
    early = (FIRST, KEY_REST, QUERY_ALL)
    late = (VALUE_REST, LAST)
    for chunk in early:
        steps.append(("merge", 0, 0, chunk))
        steps += hops(1, [chunk], [0])
    steps += hops(1, early, [1])
    steps.append(("place", 0, 0, FIRST))
    steps += [("merge", 0, 0, chunk) for chunk in late]
    steps += hops(1, late)
    steps.append(("exchange", 0, 0, NORM))
    steps += hops(1, [NORM])
    for r in range(2, n + 1):
        for chunk in CHUNKS:
            steps += hops(r, [chunk])
            if chunk is NORM:
                if r == n:
                    steps.append(("norm", 0, 0, NORM))
                continue
            for parity in (0, 1):
                if hop_pairs(n, r - 1, parity):
                    steps.append(("place", r - 1, parity, chunk))
    return steps


def gathered(arrays, norm_train, norm_step):
    serve = [
        lax.all_gather(
            (
                weight.astype(jnp.float32)
                + mix_rate * jnp.dot(low, high, preferred_element_type=jnp.float32)
            ).astype(jnp.bfloat16),
            "shard",
            axis=0,
            tiled=True,
        ).T
        for weight, low, high in arrays
    ]
    share = (norm_train + norm_step).astype(jnp.bfloat16)
    return (*serve, lax.all_gather(share, ("shard", "tp"), axis=0, tiled=True))


def solution(mesh):
    n, nt = mesh.shape["shard"], mesh.shape["tp"]
    steps = steps_of(n)

    def on_device(
        weight_query,
        low_query,
        high_query,
        weight_key,
        low_key,
        high_key,
        weight_value,
        low_value,
        high_value,
        norm_train,
        norm_step,
    ):
        depth = weight_query.shape[0]
        if depth % 128 or any(w.shape[1] % 512 for w in (weight_query, weight_key, weight_value)):
            arrays = (
                (weight_query, low_query, high_query),
                (weight_key, low_key, high_key),
                (weight_value, low_value, high_value),
            )
            return gathered(arrays, norm_train, norm_step)
        me = lax.axis_index("shard")
        me_ref = jnp.reshape(me, (1,)).astype(jnp.int32)
        mine = lax.axis_index("tp")
        inputs = {
            KEY: (weight_key, low_key.T, high_key),
            QUERY: (weight_query, low_query.T, high_query),
            VALUE: (weight_value, low_value.T, high_value),
        }
        outs = {}
        got = {}
        for what, r, parity, chunk in steps:
            if what == "merge":
                weight, low_t, high = inputs[chunk[0]]
                if chunk is FIRST:
                    piece = merge_first(weight, low_t, high, chunk)
                else:
                    shape = jax.ShapeDtypeStruct((weight.shape[1], depth * n), jnp.bfloat16)
                    out = outs.get(chunk[0], shape)
                    piece, outs[chunk[0]] = merge(me_ref, weight, low_t, high, chunk, out)
                got[0, 0, chunk] = got[0, 1, chunk] = piece
            elif what == "exchange":
                share = (norm_train + norm_step).astype(jnp.bfloat16)
                shares = [share] + [
                    lax.ppermute(share, "tp", [(j, (j + k) % nt) for j in range(nt)])
                    for k in range(1, nt)
                ]
                parts = []
                for j in range(nt):
                    part = share
                    for k in range(1, nt):
                        part = jnp.where(mine == (j + k) % nt, shares[k], part)
                    parts.append(part)
                got[0, 0, NORM] = got[0, 1, NORM] = jnp.concatenate(parts)
            elif what == "hop":
                held = got[r - 1, 1 - parity, chunk]
                got[r, parity, chunk] = lax.ppermute(held, "shard", hop_pairs(n, r, parity))
            elif what == "place":
                piece, out = got[r, parity, chunk], outs[chunk[0]]
                start, _ = extent(out.shape[0], chunk)
                in_vmem = r == 0 or (r == n - 1 and chunk[0] == VALUE)
                outs[chunk[0]] = place(me_ref, n, r, parity, piece, out, start, in_vmem)
            else:
                rows = []
                for s in range(n):
                    row = got[0, 0, NORM]
                    for (r, parity, chunk), value in got.items():
                        if chunk is NORM and r > 0:
                            row = jnp.where(source_of(me, r, parity) == s, value, row)
                    rows.append(row)
                serve_norm = jnp.concatenate(rows)
        return outs[QUERY], outs[KEY], outs[VALUE], serve_norm

    in_specs = (
        P(("trial", "shard"), "tp"),
        P(("trial", "shard"), None),
        P("trial", "tp"),
        P(("trial", "shard"), "tp"),
        P(("trial", "shard"), None),
        P("trial", "tp"),
        P(("trial", "shard"), "tp"),
        P(("trial", "shard"), None),
        P("trial", "tp"),
        P(("trial", "shard", "tp")),
        P(("trial", "shard", "tp")),
    )
    out_specs = (
        P(("trial", "tp"), None),
        P(("trial", "tp"), None),
        P(("trial", "tp"), None),
        P("trial"),
    )
    return jax.shard_map(
        on_device, mesh=mesh, in_specs=in_specs, out_specs=out_specs, check_vma=False
    )
```

time: 292 us -> 316 us (1.082)
  starting transfers between devices: 84.6 us -> 105 us
  waiting for transfers between devices: 175 us -> 162 us
  Pallas kernels: 30 us -> 41.9 us
  local copies, waits for them, and re-layouts: 0.02 us -> 3.9 us
    ppermute x20 -> x30, starting transfers between devices: 83.1 us -> 103 us  [on_device(): got[r, parity, chunk] = lax.ppermute(held, 'shard', hop_pairs(n, r, parity))]
    ppermute x20 -> x30, waiting for transfers between devices: 173 us -> 162 us  [on_device(): got[r, parity, chunk] = lax.ppermute(held, 'shard', hop_pairs(n, r, parity))]
    pallas_call x15 -> x27, Pallas kernels: 19.9 us -> 29.4 us  [the longest x26 28 us: place(): pl.pallas_call(functools.partial(place_kernel, n, r, parity, start, piece...]
    unnamed x12 -> x42, local copies, waits for them, and re-layouts: 0.02 us -> 3.9 us
    pallas_call x3 -> x4, Pallas kernels: 10.2 us -> 12.6 us  [merge(): pl.pallas_call(merge_kernel, grid_spec=pltpu.PrefetchScalarGridSpec(num_s...]
  transfers between devices with their start and end apart: 21 -> 31, of which waited for: 10 -> 9; matrix products, arithmetic and copies ran while one was open for 0% -> 0% of each run, Pallas kernels for 8% -> 11%
where the time goes in v1:
time: 316 us; the launch traced here: 315 us
  waiting for transfers between devices  162 us (51%)
  starting transfers between devices  105 us (33%)
  Pallas kernels  41.9 us (13%)
  local copies, waits for them, and re-layouts  3.9 us (1%)
    ppermute x30, waiting for transfers between devices, on_device(): got[r, parity, chunk] = lax.ppermute(held, 'shard', hop_pairs(n, r, parity))  162 us
    ppermute x30, starting transfers between devices, on_device(): got[r, parity, chunk] = lax.ppermute(held, 'shard', hop_pairs(n, r, parity))  103 us
    pallas_call x26, Pallas kernels, place(): pl.pallas_call(functools.partial(place_kernel, n, r, parity, start, piece...  28 us
    pallas_call x4, Pallas kernels, merge(): pl.pallas_call(merge_kernel, grid_spec=pltpu.PrefetchScalarGridSpec(num_s...  12.6 us
  transfers between devices with their start and end apart: 31, of which 9 were waited for; matrix products, arithmetic and copies ran while one was open for 0% of the time, Pallas kernels for 11%

profile of v1, /device:TPU:0, one launch (start us, length us, event | category | flops | bytes accessed | tf_op | source)
XLA Modules:
  0.0 314.6 jit_solution(10060890658838992157)
XLA Ops:
  0.7 5.2 %merge.5 = (bf16[2048,640]{1,0:T(8,128)(2,1)}, bf16[2048,2560]{1,0:T(8,128)(2,1)}) custom-call(s32[1]{0:T(128)} %bitcast.me_ref, bf16[640,2048]{1,0:T(8,128)(2,1)} %weight_ref.5, bf16[64,640]{1,0:T(8,128)(2,1)} %bitcast.8, bf16[64,2048]{1,0:T(8,128)(2,1)} %high_ref.5), custom_call_target="tpu_custom_call" | custom-call | flops 167772160 | bytes 7864320 | tf_op jit(solution)/shard_map/merge/pallas_call | solution.py:85
  5.9 3.1 collective-permute-start
  9.0 2.2 collective-permute-start.3
  11.2 54.9 %collective-permute-done.chunk_ref = bf16[2048,640]{1,0:T(8,128)(2,1)S(1)} collective-permute-done((bf16[2048,640]{1,0:T(8,128)(2,1)}, bf16[2048,640]{1,0:T(8,128)(2,1)S(1)}, u32[]{:S(2)}, u32[]{:S(2)}) %collective-permute-start) | collective-permute-done | bytes 2621472 | tf_op jit(solution)/shard_map/ppermute | solution.py:287
  66.0 1.6 copy-done
  67.6 2.1 collective-permute-start.1
  72.4 1.8 collective-permute-start.25
  74.2 3.2 %merge.8 = (bf16[384,640]{1,0:T(8,128)(2,1)}, bf16[512,2560]{1,0:T(8,128)(2,1)}) custom-call(s32[1]{0:T(128)} %bitcast.me_ref, bf16[640,512]{1,0:T(8,128)(2,1)} %weight_ref.9, bf16[64,640]{1,0:T(8,128)(2,1)} %bitcast.4, bf16[64,512]{1,0:T(8,128)(2,1)} %high_ref.9), custom_call_target="tpu_custom_call" | custom-call | flops 31457280 | bytes 1474560 | tf_op jit(solution)/shard_map/merge/pallas_call | solution.py:85
  77.4 2.0 merge.9
  79.4 59.5 %collective-permute-start.15 = (bf16[128,640]{1,0:T(8,128)(2,1)}, bf16[128,640]{1,0:T(8,128)(2,1)S(1)}, u32[]{:S(2)}, u32[]{:S(2)}) collective-permute-start(bf16[128,640]{1,0:T(8,128)(2,1)} %get-tuple-element.17), channel_id=1, source_target_pairs={{0,2},{2,0},{4,6},{6,4},{1,3},{3,1},{5,7},{7,5},{8,10},{10,8},{12,... | collective-permute-start | bytes 491528 | tf_op jit(solution)/shard_map/ppermute | solution.py:287
  140.9 6.7 %collective-permute-start.26 = (bf16[640]{0:T(1024)(128)(2,1)S(1)}, bf16[640]{0:T(1024)(128)(2,1)S(1)}, u32[]{:S(2)}, u32[]{:S(2)}) collective-permute-start(bf16[640]{0:T(1024)(128)(2,1)S(1)} %pad_maximum_fusion.1), channel_id=1, source_target_pairs={{0,2},{2,0},{4,6},{6,4},{1,3},{3,1},{5,7},{7,5},{8,10},{10,8},{12,... | collective-permute-start | bytes 3848 | tf_op jit(solution)/shard_map/ppermute | solution.py:287
  147.6 45.8 %collective-permute-done.26 = bf16[640]{0:T(1024)(128)(2,1)S(1)} collective-permute-done((bf16[640]{0:T(1024)(128)(2,1)S(1)}, bf16[640]{0:T(1024)(128)(2,1)S(1)}, u32[]{:S(2)}, u32[]{:S(2)}) %collective-permute-start.26) | collective-permute-done | bytes 1312 | tf_op jit(solution)/shard_map/ppermute | solution.py:287
  196.1 10.9 %collective-permute-done.30 = bf16[640]{0:T(1024)(128)(2,1)S(1)} collective-permute-done((bf16[640]{0:T(1024)(128)(2,1)S(1)}, bf16[640]{0:T(1024)(128)(2,1)S(1)}, u32[]{:S(2)}, u32[]{:S(2)}) %collective-permute-start.30) | collective-permute-done | bytes 1312 | tf_op jit(solution)/shard_map/ppermute | solution.py:287
  209.6 2.9 collective-permute-done.28
  213.9 2.1 merge.6
  216.7 6.5 %collective-permute-start.5 = (bf16[256,640]{1,0:T(8,128)(2,1)}, bf16[256,640]{1,0:T(8,128)(2,1)S(1)}, u32[]{:S(2)}, u32[]{:S(2)}) collective-permute-start(bf16[256,640]{1,0:T(8,128)(2,1)} %get-tuple-element.14), channel_id=1, source_target_pairs={{0,2},{2,0},{4,6},{6,4},{1,3},{3,1},{5,7},{7,5},{8,10},{10,8},{12,... | collective-permute-start | bytes 983048 | tf_op jit(solution)/shard_map/ppermute | solution.py:287
  224.0 7.9 %collective-permute-done.5.chunk_ref = bf16[256,640]{1,0:T(8,128)(2,1)S(1)} collective-permute-done((bf16[256,640]{1,0:T(8,128)(2,1)}, bf16[256,640]{1,0:T(8,128)(2,1)S(1)}, u32[]{:S(2)}, u32[]{:S(2)}) %collective-permute-start.5) | collective-permute-done | bytes 327712 | tf_op jit(solution)/shard_map/ppermute | solution.py:287
  233.9 7.2 %collective-permute-done.18.chunk_ref = bf16[384,640]{1,0:T(8,128)(2,1)S(1)} collective-permute-done((bf16[384,640]{1,0:T(8,128)(2,1)S(1)}, bf16[384,640]{1,0:T(8,128)(2,1)S(1)}, u32[]{:S(2)}, u32[]{:S(2)}) %collective-permute-start.18) | collective-permute-done | bytes 491552 | tf_op jit(solution)/shard_map/ppermute | solution.py:287
  243.8 7.7 %collective-permute-done.14.chunk_ref = bf16[256,640]{1,0:T(8,128)(2,1)S(1)} collective-permute-done((bf16[256,640]{1,0:T(8,128)(2,1)S(1)}, bf16[256,640]{1,0:T(8,128)(2,1)S(1)}, u32[]{:S(2)}, u32[]{:S(2)}) %collective-permute-start.14) | collective-permute-done | bytes 327712 | tf_op jit(solution)/shard_map/ppermute | solution.py:287
  253.5 13.8 %collective-permute-done.12.chunk_ref = bf16[256,640]{1,0:T(8,128)(2,1)S(1)} collective-permute-done((bf16[256,640]{1,0:T(8,128)(2,1)S(1)}, bf16[256,640]{1,0:T(8,128)(2,1)S(1)}, u32[]{:S(2)}, u32[]{:S(2)}) %collective-permute-start.12) | collective-permute-done | bytes 327712 | tf_op jit(solution)/shard_map/ppermute | solution.py:287
  270.2 1.7 place.32._
  272.0 1.8 place.42._
  273.8 1.7 place.34._
  277.4 1.7 place.36._
  279.3 1.8 place.46._
  282.5 1.7 place.38._
  290.1 1.7 place.40._
  291.8 10.6 %collective-permute-done.7.chunk_ref = bf16[256,640]{1,0:T(8,128)(2,1)S(1)} collective-permute-done((bf16[256,640]{1,0:T(8,128)(2,1)S(1)}, bf16[256,640]{1,0:T(8,128)(2,1)S(1)}, u32[]{:S(2)}, u32[]{:S(2)}) %collective-permute-start.7) | collective-permute-done | bytes 327712 | tf_op jit(solution)/shard_map/ppermute | solution.py:287
  303.2 1.7 place.41
  306.5 2.6 place.26._
  309.2 2.6 place.28._
  312.0 2.6 place.30
  (109 shorter events, 33.7 us)
Async XLA Ops:
  5.9 60.1 %collective-permute-start = (bf16[2048,640]{1,0:T(8,128)(2,1)}, bf16[2048,640]{1,0:T(8,128)(2,1)S(1)}, u32[]{:S(2)}, u32[]{:S(2)}) collective-permute-start(bf16[2048,640]{1,0:T(8,128)(2,1)} %get-tuple-element.12), channel_id=1, source_target_pairs={{0,2},{2,0},{4,6},{6,4},{1,3},{3,1},{5,7},{7,5},{8,10},{10,8},{12,... | collective-permute-start | bytes 7864328 | tf_op jit(solution)/shard_map/ppermute | solution.py:287
  9.0 60.8 %collective-permute-start.3 = (bf16[2048,640]{1,0:T(8,128)(2,1)}, bf16[2048,640]{1,0:T(8,128)(2,1)}, u32[]{:S(2)}, u32[]{:S(2)}) collective-permute-start(bf16[2048,640]{1,0:T(8,128)(2,1)} %get-tuple-element.12), channel_id=1, source_target_pairs={{2,4},{4,2},{3,5},{5,3},{10,12},{12,10},{11,13},{13,11},{18,20},{2... | collective-permute-start | bytes 7864328 | tf_op jit(solution)/shard_map/ppermute | solution.py:287
  67.6 3.4 %collective-permute-start.1 = (bf16[2048,640]{1,0:T(8,128)(2,1)S(1)}, bf16[2048,640]{1,0:T(8,128)(2,1)}, u32[]{:S(2)}, u32[]{:S(2)}) collective-permute-start(bf16[2048,640]{1,0:T(8,128)(2,1)S(1)} %collective-permute-done.chunk_ref), channel_id=1, source_target_pairs={{2,4},{4,2},{3,5},{5,3},{10,12},{12,10},{11,13},{13,11},{18,20},{2... | collective-permute-start | bytes 7864328 | tf_op jit(solution)/shard_map/ppermute | solution.py:287
  69.8 239.4 %collective-permute-start.4 = (bf16[2048,640]{1,0:T(8,128)(2,1)}, bf16[2048,640]{1,0:T(8,128)(2,1)}, u32[]{:S(2)}, u32[]{:S(2)}) collective-permute-start(bf16[2048,640]{1,0:T(8,128)(2,1)} %collective-permute-done.3.chunk_ref), channel_id=1, source_target_pairs={{2,0},{4,6},{3,1},{5,7},{10,8},{12,14},{11,9},{13,15},{18,16},{20,... | collective-permute-start | bytes 7864328 | tf_op jit(solution)/shard_map/ppermute | solution.py:287
  71.1 240.9 %collective-permute-start.2 = (bf16[2048,640]{1,0:T(8,128)(2,1)}, bf16[2048,640]{1,0:T(8,128)(2,1)}, u32[]{:S(2)}, u32[]{:S(2)}) collective-permute-start(bf16[2048,640]{1,0:T(8,128)(2,1)} %collective-permute-done.1.chunk_ref), channel_id=1, source_target_pairs={{2,0},{4,6},{3,1},{5,7},{10,8},{12,14},{11,9},{13,15},{18,16},{20,... | collective-permute-start | bytes 7864328 | tf_op jit(solution)/shard_map/ppermute | solution.py:287
  72.4 67.1 %collective-permute-start.25 = (bf16[320]{0:T(512)(128)(2,1)S(1)}, bf16[320]{0:T(512)(128)(2,1)S(1)}, u32[]{:S(2)}, u32[]{:S(2)}) collective-permute-start(bf16[320]{0:T(512)(128)(2,1)S(1)} %add_convert_fusion), channel_id=1, source_target_pairs={{0,1},{1,0},{2,3},{3,2},{4,5},{5,4},{6,7},{7,6},{8,9},{9,8},{10,11... | collective-permute-start | bytes 1928 | tf_op jit(solution)/shard_map/ppermute | solution.py:275
  77.4 145.8 %copy-start.20 = (bf16[384,640]{1,0:T(8,128)(2,1)S(1)}, bf16[384,640]{1,0:T(8,128)(2,1)}, u32[]{:S(2)}) copy-start(bf16[384,640]{1,0:T(8,128)(2,1)} %get-tuple-element.18) | copy-start | bytes 1474564
  79.4 133.2 %collective-permute-start.15 = (bf16[128,640]{1,0:T(8,128)(2,1)}, bf16[128,640]{1,0:T(8,128)(2,1)S(1)}, u32[]{:S(2)}, u32[]{:S(2)}) collective-permute-start(bf16[128,640]{1,0:T(8,128)(2,1)} %get-tuple-element.17), channel_id=1, source_target_pairs={{0,2},{2,0},{4,6},{6,4},{1,3},{3,1},{5,7},{7,5},{8,10},{10,8},{12,... | collective-permute-start | bytes 491528 | tf_op jit(solution)/shard_map/ppermute | solution.py:287
  138.8 0.7 collective-permute-start.21
  139.5 73.7 %collective-permute-start.22 = (bf16[128,640]{1,0:T(8,128)(2,1)S(1)}, bf16[128,640]{1,0:T(8,128)(2,1)S(1)}, u32[]{:S(2)}, u32[]{:S(2)}) collective-permute-start(bf16[128,640]{1,0:T(8,128)(2,1)S(1)} %collective-permute-done.21.chunk_ref), channel_id=1, source_target_pairs={{2,0},{4,6},{3,1},{5,7},{10,8},{12,14},{11,9},{13,15},{18,16},{20,... | collective-permute-start | bytes 491528 | tf_op jit(solution)/shard_map/ppermute | solution.py:287
  140.9 52.5 %collective-permute-start.26 = (bf16[640]{0:T(1024)(128)(2,1)S(1)}, bf16[640]{0:T(1024)(128)(2,1)S(1)}, u32[]{:S(2)}, u32[]{:S(2)}) collective-permute-start(bf16[640]{0:T(1024)(128)(2,1)S(1)} %pad_maximum_fusion.1), channel_id=1, source_target_pairs={{0,2},{2,0},{4,6},{6,4},{1,3},{3,1},{5,7},{7,5},{8,10},{10,8},{12,... | collective-permute-start | bytes 3848 | tf_op jit(solution)/shard_map/ppermute | solution.py:287
  193.4 0.7 collective-permute-start.29
  194.1 0.7 collective-permute-start.27
  194.8 12.2 %collective-permute-start.30 = (bf16[640]{0:T(1024)(128)(2,1)S(1)}, bf16[640]{0:T(1024)(128)(2,1)S(1)}, u32[]{:S(2)}, u32[]{:S(2)}) collective-permute-start(bf16[640]{0:T(1024)(128)(2,1)S(1)} %collective-permute-done.29), channel_id=1, source_target_pairs={{2,0},{4,6},{3,1},{5,7},{10,8},{12,14},{11,9},{13,15},{18,16},{20,... | collective-permute-start | bytes 3848 | tf_op jit(solution)/shard_map/ppermute | solution.py:287
  207.0 5.5 %collective-permute-start.28 = (bf16[640]{0:T(1024)(128)(2,1)S(1)}, bf16[640]{0:T(1024)(128)(2,1)S(1)}, u32[]{:S(2)}, u32[]{:S(2)}) collective-permute-start(bf16[640]{0:T(1024)(128)(2,1)S(1)} %collective-permute-done.27), channel_id=1, source_target_pairs={{2,0},{4,6},{3,1},{5,7},{10,8},{12,14},{11,9},{13,15},{18,16},{20,... | collective-permute-start | bytes 3848 | tf_op jit(solution)/shard_map/ppermute | solution.py:287
  212.5 10.7 %collective-permute-start.8 = (bf16[256,640]{1,0:T(8,128)(2,1)S(1)}, bf16[256,640]{1,0:T(8,128)(2,1)S(1)}, u32[]{:S(2)}, u32[]{:S(2)}) collective-permute-start(bf16[256,640]{1,0:T(8,128)(2,1)S(1)} %merge.7.chunk_ref), channel_id=1, source_target_pairs={{0,2},{2,0},{4,6},{6,4},{1,3},{3,1},{5,7},{7,5},{8,10},{10,8},{12,... | collective-permute-start | bytes 983048 | tf_op jit(solution)/shard_map/ppermute | solution.py:287
  212.5 3.5 %collective-permute-start.16 = (bf16[128,640]{1,0:T(8,128)(2,1)S(1)}, bf16[128,640]{1,0:T(8,128)(2,1)S(1)}, u32[]{:S(2)}, u32[]{:S(2)}) collective-permute-start(bf16[128,640]{1,0:T(8,128)(2,1)S(1)} %collective-permute-done.15.chunk_ref), channel_id=1, source_target_pairs={{2,4},{4,2},{3,5},{5,3},{10,12},{12,10},{11,13},{13,11},{18,20},{2... | collective-permute-start | bytes 491528 | tf_op jit(solution)/shard_map/ppermute | solution.py:287
  213.2 10.1 %collective-permute-start.13 = (bf16[256,640]{1,0:T(8,128)(2,1)S(1)}, bf16[256,640]{1,0:T(8,128)(2,1)S(1)}, u32[]{:S(2)}, u32[]{:S(2)}) collective-permute-start(bf16[256,640]{1,0:T(8,128)(2,1)S(1)} %merge.7.chunk_ref), channel_id=1, source_target_pairs={{2,4},{4,2},{3,5},{5,3},{10,12},{12,10},{11,13},{13,11},{18,20},{2... | collective-permute-start | bytes 983048 | tf_op jit(solution)/shard_map/ppermute | solution.py:287
  216.7 15.2 %collective-permute-start.5 = (bf16[256,640]{1,0:T(8,128)(2,1)}, bf16[256,640]{1,0:T(8,128)(2,1)S(1)}, u32[]{:S(2)}, u32[]{:S(2)}) collective-permute-start(bf16[256,640]{1,0:T(8,128)(2,1)} %get-tuple-element.14), channel_id=1, source_target_pairs={{0,2},{2,0},{4,6},{6,4},{1,3},{3,1},{5,7},{7,5},{8,10},{10,8},{12,... | collective-permute-start | bytes 983048 | tf_op jit(solution)/shard_map/ppermute | solution.py:287
  223.2 17.9 %collective-permute-start.18 = (bf16[384,640]{1,0:T(8,128)(2,1)S(1)}, bf16[384,640]{1,0:T(8,128)(2,1)S(1)}, u32[]{:S(2)}, u32[]{:S(2)}) collective-permute-start(bf16[384,640]{1,0:T(8,128)(2,1)S(1)} %copy-done.20), channel_id=1, source_target_pairs={{0,2},{2,0},{4,6},{6,4},{1,3},{3,1},{5,7},{7,5},{8,10},{10,8},{12,... | collective-permute-start | bytes 1474568 | tf_op jit(solution)/shard_map/ppermute | solution.py:287
  223.3 9.2 %collective-permute-start.11 = (bf16[256,640]{1,0:T(8,128)(2,1)}, bf16[256,640]{1,0:T(8,128)(2,1)S(1)}, u32[]{:S(2)}, u32[]{:S(2)}) collective-permute-start(bf16[256,640]{1,0:T(8,128)(2,1)} %get-tuple-element.14), channel_id=1, source_target_pairs={{2,4},{4,2},{3,5},{5,3},{10,12},{12,10},{11,13},{13,11},{18,20},{2... | collective-permute-start | bytes 983048 | tf_op jit(solution)/shard_map/ppermute | solution.py:287
  231.9 10.6 %collective-permute-start.23 = (bf16[384,640]{1,0:T(8,128)(2,1)S(1)}, bf16[384,640]{1,0:T(8,128)(2,1)S(1)}, u32[]{:S(2)}, u32[]{:S(2)}) collective-permute-start(bf16[384,640]{1,0:T(8,128)(2,1)S(1)} %copy-done.20), channel_id=1, source_target_pairs={{2,4},{4,2},{3,5},{5,3},{10,12},{12,10},{11,13},{13,11},{18,20},{2... | collective-permute-start | bytes 1474568 | tf_op jit(solution)/shard_map/ppermute | solution.py:287
  232.6 18.9 %collective-permute-start.14 = (bf16[256,640]{1,0:T(8,128)(2,1)S(1)}, bf16[256,640]{1,0:T(8,128)(2,1)S(1)}, u32[]{:S(2)}, u32[]{:S(2)}) collective-permute-start(bf16[256,640]{1,0:T(8,128)(2,1)S(1)} %collective-permute-done.13.chunk_ref), channel_id=1, source_target_pairs={{2,0},{4,6},{3,1},{5,7},{10,8},{12,14},{11,9},{13,15},{18,16},{20,... | collective-permute-start | bytes 983048 | tf_op jit(solution)/shard_map/ppermute | solution.py:287
  241.1 11.1 %collective-permute-start.9 = (bf16[256,640]{1,0:T(8,128)(2,1)S(1)}, bf16[256,640]{1,0:T(8,128)(2,1)}, u32[]{:S(2)}, u32[]{:S(2)}) collective-permute-start(bf16[256,640]{1,0:T(8,128)(2,1)S(1)} %collective-permute-done.8.chunk_ref), channel_id=1, source_target_pairs={{2,4},{4,2},{3,5},{5,3},{10,12},{12,10},{11,13},{13,11},{18,20},{2... | collective-permute-start | bytes 983048 | tf_op jit(solution)/shard_map/ppermute | solution.py:287
  242.5 25.5 %collective-permute-start.24 = (bf16[384,640]{1,0:T(8,128)(2,1)S(1)}, bf16[384,640]{1,0:T(8,128)(2,1)S(1)}, u32[]{:S(2)}, u32[]{:S(2)}) collective-permute-start(bf16[384,640]{1,0:T(8,128)(2,1)S(1)} %collective-permute-done.23.chunk_ref), channel_id=1, source_target_pairs={{2,0},{4,6},{3,1},{5,7},{10,8},{12,14},{11,9},{13,15},{18,16},{20,... | collective-permute-start | bytes 1474568 | tf_op jit(solution)/shard_map/ppermute | solution.py:287
  251.5 29.6 %collective-permute-start.19 = (bf16[384,640]{1,0:T(8,128)(2,1)S(1)}, bf16[384,640]{1,0:T(8,128)(2,1)S(1)}, u32[]{:S(2)}, u32[]{:S(2)}) collective-permute-start(bf16[384,640]{1,0:T(8,128)(2,1)S(1)} %collective-permute-done.18.chunk_ref), channel_id=1, source_target_pairs={{2,4},{4,2},{3,5},{5,3},{10,12},{12,10},{11,13},{13,11},{18,20},{2... | collective-permute-start | bytes 1474568 | tf_op jit(solution)/shard_map/ppermute | solution.py:287
  252.2 15.1 %collective-permute-start.12 = (bf16[256,640]{1,0:T(8,128)(2,1)S(1)}, bf16[256,640]{1,0:T(8,128)(2,1)S(1)}, u32[]{:S(2)}, u32[]{:S(2)}) collective-permute-start(bf16[256,640]{1,0:T(8,128)(2,1)S(1)} %collective-permute-done.11.chunk_ref), channel_id=1, source_target_pairs={{2,0},{4,6},{3,1},{5,7},{10,8},{12,14},{11,9},{13,15},{18,16},{20,... | collective-permute-start | bytes 983048 | tf_op jit(solution)/shard_map/ppermute | solution.py:287
  267.3 17.0 %collective-permute-start.6 = (bf16[256,640]{1,0:T(8,128)(2,1)S(1)}, bf16[256,640]{1,0:T(8,128)(2,1)S(1)}, u32[]{:S(2)}, u32[]{:S(2)}) collective-permute-start(bf16[256,640]{1,0:T(8,128)(2,1)S(1)} %collective-permute-done.5.chunk_ref), channel_id=1, source_target_pairs={{2,4},{4,2},{3,5},{5,3},{10,12},{12,10},{11,13},{13,11},{18,20},{2... | collective-permute-start | bytes 983048 | tf_op jit(solution)/shard_map/ppermute | solution.py:287
  268.0 18.4 %collective-permute-start.10 = (bf16[256,640]{1,0:T(8,128)(2,1)}, bf16[256,640]{1,0:T(8,128)(2,1)}, u32[]{:S(2)}, u32[]{:S(2)}) collective-permute-start(bf16[256,640]{1,0:T(8,128)(2,1)} %collective-permute-done.9.chunk_ref), channel_id=1, source_target_pairs={{2,0},{4,6},{3,1},{5,7},{10,8},{12,14},{11,9},{13,15},{18,16},{20,... | collective-permute-start | bytes 983048 | tf_op jit(solution)/shard_map/ppermute | solution.py:287
  281.1 23.8 %collective-permute-start.20 = (bf16[384,640]{1,0:T(8,128)(2,1)S(1)}, bf16[384,640]{1,0:T(8,128)(2,1)S(1)}, u32[]{:S(2)}, u32[]{:S(2)}) collective-permute-start(bf16[384,640]{1,0:T(8,128)(2,1)S(1)} %collective-permute-done.19.chunk_ref), channel_id=1, source_target_pairs={{2,0},{4,6},{3,1},{5,7},{10,8},{12,14},{11,9},{13,15},{18,16},{20,... | collective-permute-start | bytes 1474568 | tf_op jit(solution)/shard_map/ppermute | solution.py:287
  285.1 20.6 %collective-permute-start.17 = (bf16[128,640]{1,0:T(8,128)(2,1)S(1)}, bf16[128,640]{1,0:T(8,128)(2,1)S(1)}, u32[]{:S(2)}, u32[]{:S(2)}) collective-permute-start(bf16[128,640]{1,0:T(8,128)(2,1)S(1)} %copy-done.15), channel_id=1, source_target_pairs={{2,0},{4,6},{3,1},{5,7},{10,8},{12,14},{11,9},{13,15},{18,16},{20,... | collective-permute-start | bytes 491528 | tf_op jit(solution)/shard_map/ppermute | solution.py:287
  286.4 16.1 %collective-permute-start.7 = (bf16[256,640]{1,0:T(8,128)(2,1)S(1)}, bf16[256,640]{1,0:T(8,128)(2,1)S(1)}, u32[]{:S(2)}, u32[]{:S(2)}) collective-permute-start(bf16[256,640]{1,0:T(8,128)(2,1)S(1)} %collective-permute-done.6.chunk_ref), channel_id=1, source_target_pairs={{2,0},{4,6},{3,1},{5,7},{10,8},{12,14},{11,9},{13,15},{18,16},{20,... | collective-permute-start | bytes 983048 | tf_op jit(solution)/shard_map/ppermute | solution.py:287
  (20 other events, 520.3 us)

commit v2 on v1

v2 whole, which is shorter than its diff:
```python
import functools

import jax
import jax.numpy as jnp
from jax import lax
from jax.experimental import pallas as pl
from jax.experimental.pallas import tpu as pltpu
from jax.sharding import PartitionSpec as P

mix_rate = 1.0


KEY, QUERY, VALUE = range(3)
FIRST, LAST, NORM = KEY, VALUE, None
CHUNKS = (KEY, QUERY, NORM, VALUE)


def merged(weight_ref, low_ref, high_ref):
    delta = lax.dot_general(
        high_ref[...], low_ref[...], (((0,), (0,)), ((), ())), preferred_element_type=jnp.float32
    )
    fresh = weight_ref[...].T.astype(jnp.float32) + mix_rate * delta
    return fresh.astype(jnp.bfloat16)


def first_kernel(weight_ref, low_ref, high_ref, chunk_ref):
    chunk_ref[...] = merged(weight_ref, low_ref, high_ref)


def merge_kernel(me_ref, weight_ref, low_ref, high_ref, chunk_ref, out_ref):
    fresh = merged(weight_ref, low_ref, high_ref)
    chunk_ref[...] = fresh
    out_ref[...] = fresh


def cost(rows, depth, rank):
    return pl.CostEstimate(
        flops=2 * rows * depth * rank, bytes_accessed=6 * rows * depth, transcendentals=0
    )


def merge_first(weight, low_t, high):
    depth, columns = weight.shape
    rank = high.shape[0]
    return pl.pallas_call(
        first_kernel,
        out_shape=pltpu.VMEM((columns, depth), jnp.bfloat16),
        cost_estimate=cost(columns, depth, rank),
        name="merge",
    )(weight, low_t, high)


def merge(me, weight, low_t, high, total):
    depth, columns = weight.shape
    rank = high.shape[0]
    block = next(b for b in (512, 256, 128) if columns % b == 0)
    if columns == block and block > 128:
        block //= 2
    return pl.pallas_call(
        merge_kernel,
        grid_spec=pltpu.PrefetchScalarGridSpec(
            num_scalar_prefetch=1,
            grid=(columns // block,),
            in_specs=[
                pl.BlockSpec((depth, block), lambda j, me: (0, j)),
                pl.BlockSpec((rank, depth), lambda j, me: (0, 0)),
                pl.BlockSpec((rank, block), lambda j, me: (0, j)),
            ],
            out_specs=[
                pl.BlockSpec((block, depth), lambda j, me: (j, 0)),
                pl.BlockSpec((block, depth), lambda j, me: (j, me[0])),
            ],
        ),
        out_shape=[
            jax.ShapeDtypeStruct((columns, depth), jnp.bfloat16),
            jax.ShapeDtypeStruct((columns, total), jnp.bfloat16),
        ],
        cost_estimate=cost(columns, depth, rank),
        name="merge",
    )(me, weight, low_t, high)


def source_of(me, r, parity):
    down = lax.rem(me + parity, 2) == 0
    return jnp.where(down, me + r, me - r)


def place_kernel(n, r, parity, pieces, me_ref, chunk_ref, *refs):
    staged = pieces > 1
    out_ref, sem, *stage = refs[-4:] if staged else refs[-2:]
    rows, depth = chunk_ref.shape
    step = rows // pieces
    source = me_ref[0] if r == 0 else source_of(me_ref[0], r, parity)

    @pl.when((source >= 0) & (source < n))
    def _():
        column = pl.multiple_of(source * depth, 128)
        parts = [pl.ds(p * step, step) for p in range(pieces)]
        held = stage[1] if staged else chunk_ref
        ins = [
            pltpu.make_async_copy(chunk_ref.at[part], held.at[part], stage[0].at[p])
            for p, part in enumerate(parts)
            if staged
        ]
        outs = [
            pltpu.make_async_copy(held.at[part], out_ref.at[part, pl.ds(column, depth)], sem.at[p])
            for p, part in enumerate(parts)
        ]
        for copy in ins:
            copy.start()
        for p in range(pieces):
            if staged:
                ins[p].wait()
            outs[p].start()
        for copy in outs:
            copy.wait()


def place(me, n, r, parity, chunk, out, in_vmem):
    rows, depth = chunk.shape
    pieces = 1 if in_vmem else 4
    sems = pltpu.SemaphoreType.DMA((pieces,))
    scratch, operands, aliases = [sems], [me, chunk], {}
    if in_vmem:
        operands[1] = pltpu.with_memory_space_constraint(chunk, pltpu.VMEM)
    else:
        scratch += [sems, pltpu.VMEM((rows, depth), jnp.bfloat16)]
    if isinstance(out, jax.Array):
        operands.append(out)
        aliases = {2: 0}
    specs = [pl.BlockSpec(memory_space=pltpu.VMEM if in_vmem else pl.ANY)]
    specs += [pl.BlockSpec(memory_space=pl.ANY)] * (len(operands) - 2)
    return pl.pallas_call(
        functools.partial(place_kernel, n, r, parity, pieces),
        grid_spec=pltpu.PrefetchScalarGridSpec(
            num_scalar_prefetch=1,
            grid=(1,),
            in_specs=specs,
            out_specs=pl.BlockSpec(memory_space=pl.ANY),
            scratch_shapes=scratch,
        ),
        out_shape=jax.ShapeDtypeStruct(out.shape, out.dtype),
        input_output_aliases=aliases,
        cost_estimate=pl.CostEstimate(
            flops=rows * depth, bytes_accessed=4 * rows * depth, transcendentals=0
        ),
        name="place",
    )(*operands)


def hop_pairs(n, r, parity):
    pairs = []
    for i in range(parity, n - 1, 2):
        if i - r + 1 >= 0:
            pairs.append((i, i + 1))
        if i + r <= n - 1:
            pairs.append((i + 1, i))
    return pairs


def steps_of(n):
    def hops(r, chunks, parities=(0, 1)):
        return [
            ("hop", r, parity, chunk)
            for parity in parities
            for chunk in chunks
            if hop_pairs(n, r, parity)
        ]

    steps = []
    for chunk in (FIRST, QUERY):
        steps.append(("merge", 0, 0, chunk))
        steps += hops(1, [chunk], [0])
    steps += hops(1, [FIRST, QUERY], [1])
    steps.append(("place", 0, 0, FIRST))
    steps.append(("merge", 0, 0, LAST))
    steps += hops(1, [LAST])
    steps.append(("exchange", 0, 0, NORM))
    steps += hops(1, [NORM])
    for r in range(2, n + 1):
        for chunk in CHUNKS:
            steps += hops(r, [chunk])
            if chunk is NORM:
                if r == n:
                    steps.append(("norm", 0, 0, NORM))
                continue
            for parity in (0, 1):
                if hop_pairs(n, r - 1, parity):
                    steps.append(("place", r - 1, parity, chunk))
    return steps


def gathered(arrays, norm_train, norm_step):
    serve = [
        lax.all_gather(
            (
                weight.astype(jnp.float32)
                + mix_rate * jnp.dot(low, high, preferred_element_type=jnp.float32)
            ).astype(jnp.bfloat16),
            "shard",
            axis=0,
            tiled=True,
        ).T
        for weight, low, high in arrays
    ]
    share = (norm_train + norm_step).astype(jnp.bfloat16)
    return (*serve, lax.all_gather(share, ("shard", "tp"), axis=0, tiled=True))


def solution(mesh):
    n, nt = mesh.shape["shard"], mesh.shape["tp"]
    steps = steps_of(n)

    def on_device(
        weight_query,
        low_query,
        high_query,
        weight_key,
        low_key,
        high_key,
        weight_value,
        low_value,
        high_value,
        norm_train,
        norm_step,
    ):
        depth = weight_query.shape[0]
        if depth % 128 or any(w.shape[1] % 128 for w in (weight_query, weight_key, weight_value)):
            arrays = (
                (weight_query, low_query, high_query),
                (weight_key, low_key, high_key),
                (weight_value, low_value, high_value),
            )
            return gathered(arrays, norm_train, norm_step)
        me = lax.axis_index("shard")
        me_ref = jnp.reshape(me, (1,)).astype(jnp.int32)
        mine = lax.axis_index("tp")
        inputs = {
            KEY: (weight_key, low_key.T, high_key),
            QUERY: (weight_query, low_query.T, high_query),
            VALUE: (weight_value, low_value.T, high_value),
        }
        outs = {}
        got = {}
        for what, r, parity, chunk in steps:
            if what == "merge":
                if chunk == FIRST:
                    piece = merge_first(*inputs[chunk])
                    outs[chunk] = jax.ShapeDtypeStruct((piece.shape[0], depth * n), piece.dtype)
                else:
                    piece, outs[chunk] = merge(me_ref, *inputs[chunk], depth * n)
                got[0, 0, chunk] = got[0, 1, chunk] = piece
            elif what == "exchange":
                share = (norm_train + norm_step).astype(jnp.bfloat16)
                shares = [share] + [
                    lax.ppermute(share, "tp", [(j, (j + k) % nt) for j in range(nt)])
                    for k in range(1, nt)
                ]
                parts = []
                for j in range(nt):
                    part = share
                    for k in range(1, nt):
                        part = jnp.where(mine == (j + k) % nt, shares[k], part)
                    parts.append(part)
                got[0, 0, NORM] = got[0, 1, NORM] = jnp.concatenate(parts)
            elif what == "hop":
                held = got[r - 1, 1 - parity, chunk]
                got[r, parity, chunk] = lax.ppermute(held, "shard", hop_pairs(n, r, parity))
            elif what == "place":
                in_vmem = r == 0 or (r == n - 1 and chunk == LAST)
                outs[chunk] = place(me_ref, n, r, parity, got[r, parity, chunk], outs[chunk], in_vmem)
            else:
                rows = []
                for s in range(n):
                    row = got[0, 0, NORM]
                    for (r, parity, chunk), value in got.items():
                        if chunk is NORM and r > 0:
                            row = jnp.where(source_of(me, r, parity) == s, value, row)
                    rows.append(row)
                serve_norm = jnp.concatenate(rows)
        return outs[QUERY], outs[KEY], outs[VALUE], serve_norm

    in_specs = (
        P(("trial", "shard"), "tp"),
        P(("trial", "shard"), None),
        P("trial", "tp"),
        P(("trial", "shard"), "tp"),
        P(("trial", "shard"), None),
        P("trial", "tp"),
        P(("trial", "shard"), "tp"),
        P(("trial", "shard"), None),
        P("trial", "tp"),
        P(("trial", "shard", "tp")),
        P(("trial", "shard", "tp")),
    )
    out_specs = (
        P(("trial", "tp"), None),
        P(("trial", "tp"), None),
        P(("trial", "tp"), None),
        P("trial"),
    )
    return jax.shard_map(
        on_device, mesh=mesh, in_specs=in_specs, out_specs=out_specs, check_vma=False
    )
```

time: 316 us -> 292 us (0.924)
  starting transfers between devices: 105 us -> 83 us
  waiting for transfers between devices: 162 us -> 178 us
  Pallas kernels: 41.9 us -> 28.9 us
  local copies, waits for them, and re-layouts: 3.9 us -> 0.03 us
    ppermute x30 -> x20, starting transfers between devices: 103 us -> 81.4 us  [on_device(): got[r, parity, chunk] = lax.ppermute(held, 'shard', hop_pairs(n, r, parity))]
    ppermute x30 -> x20, waiting for transfers between devices: 162 us -> 176 us  [on_device(): got[r, parity, chunk] = lax.ppermute(held, 'shard', hop_pairs(n, r, parity))]
    pallas_call x27 -> x17, Pallas kernels: 29.4 us -> 21.2 us  [the longest x16 19.7 us: place(): pl.pallas_call(functools.partial(place_kernel, n, r, parity, pieces), gri...]
    pallas_call x4 -> x2, Pallas kernels: 12.6 us -> 7.69 us  [merge(): pl.pallas_call(merge_kernel, grid_spec=pltpu.PrefetchScalarGridSpec(num_s...]
    unnamed x42 -> x14, local copies, waits for them, and re-layouts: 3.9 us -> 0.03 us
  transfers between devices with their start and end apart: 31 -> 21, of which waited for: 9 -> 10; matrix products, arithmetic and copies ran while one was open for 0% -> 0% of each run, Pallas kernels for 11% -> 7%
where the time goes in v2:
time: 292 us
  waiting for transfers between devices  178 us (61%)
  starting transfers between devices  83 us (28%)
  Pallas kernels  28.9 us (10%)
    ppermute x20, waiting for transfers between devices, on_device(): got[r, parity, chunk] = lax.ppermute(held, 'shard', hop_pairs(n, r, parity))  176 us
    ppermute x20, starting transfers between devices, on_device(): got[r, parity, chunk] = lax.ppermute(held, 'shard', hop_pairs(n, r, parity))  81.4 us
    pallas_call x16, Pallas kernels, place(): pl.pallas_call(functools.partial(place_kernel, n, r, parity, pieces), gri...  19.7 us
    pallas_call x2, Pallas kernels, merge(): pl.pallas_call(merge_kernel, grid_spec=pltpu.PrefetchScalarGridSpec(num_s...  7.69 us
  transfers between devices with their start and end apart: 21, of which 10 were waited for; matrix products, arithmetic and copies ran while one was open for 0% of the time, Pallas kernels for 7%

profile of v2, /device:TPU:0, one launch (start us, length us, event | category | flops | bytes accessed | tf_op | source)
XLA Modules:
  0.0 291.6 jit_solution(1627474915032354945)
XLA Ops:
  0.7 5.2 %merge.3 = (bf16[2048,640]{1,0:T(8,128)(2,1)}, bf16[2048,2560]{1,0:T(8,128)(2,1)}) custom-call(s32[1]{0:T(128)} %bitcast.me_ref, bf16[640,2048]{1,0:T(8,128)(2,1)} %weight_ref.3, bf16[64,640]{1,0:T(8,128)(2,1)} %bitcast.4, bf16[64,2048]{1,0:T(8,128)(2,1)} %high_ref.3), custom_call_target="tpu_custom_call" | custom-call | flops 167772160 | bytes 7864320 | tf_op jit(solution)/shard_map/merge/pallas_call | solution.py:59
  5.9 3.1 %collective-permute-start = (bf16[2048,640]{1,0:T(8,128)(2,1)}, bf16[2048,640]{1,0:T(8,128)(2,1)S(1)}, u32[]{:S(2)}, u32[]{:S(2)}) collective-permute-start(bf16[2048,640]{1,0:T(8,128)(2,1)} %get-tuple-element.8), channel_id=1, source_target_pairs={{0,2},{2,0},{4,6},{6,4},{1,3},{3,1},{5,7},{7,5},{8,10},{10,8},{12,... | collective-permute-start | bytes 7864328 | tf_op jit(solution)/shard_map/ppermute | solution.py:268
  9.0 2.2 collective-permute-start.3
  11.2 54.9 %collective-permute-done.chunk_ref = bf16[2048,640]{1,0:T(8,128)(2,1)S(1)} collective-permute-done((bf16[2048,640]{1,0:T(8,128)(2,1)}, bf16[2048,640]{1,0:T(8,128)(2,1)S(1)}, u32[]{:S(2)}, u32[]{:S(2)}) %collective-permute-start) | collective-permute-done | bytes 2621472 | tf_op jit(solution)/shard_map/ppermute | solution.py:268
  66.0 2.3 collective-permute-start.1
  68.3 2.4 merge.5
  70.8 3.0 %collective-permute-start.10 = (bf16[512,640]{1,0:T(8,128)(2,1)}, bf16[512,640]{1,0:T(8,128)(2,1)S(1)}, u32[]{:S(2)}, u32[]{:S(2)}) collective-permute-start(bf16[512,640]{1,0:T(8,128)(2,1)} %get-tuple-element.10), channel_id=1, source_target_pairs={{0,2},{2,0},{4,6},{6,4},{1,3},{3,1},{5,7},{7,5},{8,10},{10,8},{12,... | collective-permute-start | bytes 1966088 | tf_op jit(solution)/shard_map/ppermute | solution.py:268
  75.0 1.3 collective-permute-start.2
  76.4 1.6 collective-permute-start.15
  78.0 2.1 collective-permute-done.15
  80.1 54.0 %collective-permute-start.16 = (bf16[640]{0:T(1024)(128)(2,1)S(1)}, bf16[640]{0:T(1024)(128)(2,1)S(1)}, u32[]{:S(2)}, u32[]{:S(2)}) collective-permute-start(bf16[640]{0:T(1024)(128)(2,1)S(1)} %pad_maximum_fusion.1), channel_id=1, source_target_pairs={{0,2},{2,0},{4,6},{6,4},{1,3},{3,1},{5,7},{7,5},{8,10},{10,8},{12,... | collective-permute-start | bytes 3848 | tf_op jit(solution)/shard_map/ppermute | solution.py:268
  134.8 65.3 %collective-permute-done.16 = bf16[640]{0:T(1024)(128)(2,1)S(1)} collective-permute-done((bf16[640]{0:T(1024)(128)(2,1)S(1)}, bf16[640]{0:T(1024)(128)(2,1)S(1)}, u32[]{:S(2)}, u32[]{:S(2)}) %collective-permute-start.16) | collective-permute-done | bytes 1312 | tf_op jit(solution)/shard_map/ppermute | solution.py:268
  202.1 1.5 collective-permute-start.13
  203.6 2.7 collective-permute-done.20
  207.6 1.5 merge.4.chunk_ref
  209.1 2.7 collective-permute-done.18
  212.5 1.3 collective-permute-start.14
  213.8 15.0 %collective-permute-done.5.chunk_ref = bf16[512,640]{1,0:T(8,128)(2,1)S(1)} collective-permute-done((bf16[512,640]{1,0:T(8,128)(2,1)S(1)}, bf16[512,640]{1,0:T(8,128)(2,1)S(1)}, u32[]{:S(2)}, u32[]{:S(2)}) %collective-permute-start.5) | collective-permute-done | bytes 655392 | tf_op jit(solution)/shard_map/ppermute | solution.py:268
  228.8 1.5 collective-permute-start.11
  230.3 1.5 collective-permute-start.6
  231.8 6.9 %collective-permute-done.14.chunk_ref = bf16[512,640]{1,0:T(8,128)(2,1)S(1)} collective-permute-done((bf16[512,640]{1,0:T(8,128)(2,1)}, bf16[512,640]{1,0:T(8,128)(2,1)S(1)}, u32[]{:S(2)}, u32[]{:S(2)}) %collective-permute-start.14) | collective-permute-done | bytes 655392 | tf_op jit(solution)/shard_map/ppermute | solution.py:268
  244.4 1.9 place.27.refs_0_
  246.3 1.9 place.22.refs_0_
  248.4 1.9 place.29.refs_0_
  250.3 7.7 %collective-permute-done.9.chunk_ref = bf16[512,640]{1,0:T(8,128)(2,1)} collective-permute-done((bf16[512,640]{1,0:T(8,128)(2,1)S(1)}, bf16[512,640]{1,0:T(8,128)(2,1)}, u32[]{:S(2)}, u32[]{:S(2)}) %collective-permute-start.9) | collective-permute-done | bytes 655392 | tf_op jit(solution)/shard_map/ppermute | solution.py:268
  258.0 1.9 place.24.refs_0_
  260.1 11.8 %collective-permute-done.12.chunk_ref = bf16[512,640]{1,0:T(8,128)(2,1)S(1)} collective-permute-done((bf16[512,640]{1,0:T(8,128)(2,1)}, bf16[512,640]{1,0:T(8,128)(2,1)S(1)}, u32[]{:S(2)}, u32[]{:S(2)}) %collective-permute-start.12) | collective-permute-done | bytes 655392 | tf_op jit(solution)/shard_map/ppermute | solution.py:268
  272.8 8.7 %collective-permute-done.7.chunk_ref = bf16[512,640]{1,0:T(8,128)(2,1)} collective-permute-done((bf16[512,640]{1,0:T(8,128)(2,1)}, bf16[512,640]{1,0:T(8,128)(2,1)}, u32[]{:S(2)}, u32[]{:S(2)}) %collective-permute-start.7) | collective-permute-done | bytes 655392 | tf_op jit(solution)/shard_map/ppermute | solution.py:268
  281.5 1.9 place.26
  283.4 2.6 place.16.refs_0_
  286.2 2.6 place.18.refs_0_
  288.9 2.6 place.20
  (49 shorter events, 12.9 us)
Async XLA Ops:
  0.6 75.7 %copy-start.5 = (f32[320]{0:T(512)S(1)}, f32[320]{0:T(512)}, u32[]{:S(2)}) copy-start(f32[320]{0:T(512)} %param.20) | copy-start | bytes 3844
  0.6 75.7 %copy-start.6 = (f32[320]{0:T(512)S(1)}, f32[320]{0:T(512)}, u32[]{:S(2)}) copy-start(f32[320]{0:T(512)} %param.21) | copy-start | bytes 3844
  5.9 60.1 %collective-permute-start = (bf16[2048,640]{1,0:T(8,128)(2,1)}, bf16[2048,640]{1,0:T(8,128)(2,1)S(1)}, u32[]{:S(2)}, u32[]{:S(2)}) collective-permute-start(bf16[2048,640]{1,0:T(8,128)(2,1)} %get-tuple-element.8), channel_id=1, source_target_pairs={{0,2},{2,0},{4,6},{6,4},{1,3},{3,1},{5,7},{7,5},{8,10},{10,8},{12,... | collective-permute-start | bytes 7864328 | tf_op jit(solution)/shard_map/ppermute | solution.py:268
  9.0 64.8 %collective-permute-start.3 = (bf16[2048,640]{1,0:T(8,128)(2,1)}, bf16[2048,640]{1,0:T(8,128)(2,1)}, u32[]{:S(2)}, u32[]{:S(2)}) collective-permute-start(bf16[2048,640]{1,0:T(8,128)(2,1)} %get-tuple-element.8), channel_id=1, source_target_pairs={{2,4},{4,2},{3,5},{5,3},{10,12},{12,10},{11,13},{13,11},{18,20},{2... | collective-permute-start | bytes 7864328 | tf_op jit(solution)/shard_map/ppermute | solution.py:268
  66.0 141.5 %copy-start = (bf16[2048,640]{1,0:T(8,128)(2,1)}, bf16[2048,640]{1,0:T(8,128)(2,1)S(1)}, u32[]{:S(2)}) copy-start(bf16[2048,640]{1,0:T(8,128)(2,1)S(1)} %collective-permute-done.chunk_ref) | copy-start | bytes 7864324
  66.0 9.0 %collective-permute-start.1 = (bf16[2048,640]{1,0:T(8,128)(2,1)S(1)}, bf16[2048,640]{1,0:T(8,128)(2,1)}, u32[]{:S(2)}, u32[]{:S(2)}) collective-permute-start(bf16[2048,640]{1,0:T(8,128)(2,1)S(1)} %collective-permute-done.chunk_ref), channel_id=1, source_target_pairs={{2,4},{4,2},{3,5},{5,3},{10,12},{12,10},{11,13},{13,11},{18,20},{2... | collective-permute-start | bytes 7864328 | tf_op jit(solution)/shard_map/ppermute | solution.py:268
  70.8 141.0 %collective-permute-start.10 = (bf16[512,640]{1,0:T(8,128)(2,1)}, bf16[512,640]{1,0:T(8,128)(2,1)S(1)}, u32[]{:S(2)}, u32[]{:S(2)}) collective-permute-start(bf16[512,640]{1,0:T(8,128)(2,1)} %get-tuple-element.10), channel_id=1, source_target_pairs={{0,2},{2,0},{4,6},{6,4},{1,3},{3,1},{5,7},{7,5},{8,10},{10,8},{12,... | collective-permute-start | bytes 1966088 | tf_op jit(solution)/shard_map/ppermute | solution.py:268
  73.7 212.4 %collective-permute-start.4 = (bf16[2048,640]{1,0:T(8,128)(2,1)}, bf16[2048,640]{1,0:T(8,128)(2,1)}, u32[]{:S(2)}, u32[]{:S(2)}) collective-permute-start(bf16[2048,640]{1,0:T(8,128)(2,1)} %collective-permute-done.3.chunk_ref), channel_id=1, source_target_pairs={{2,0},{4,6},{3,1},{5,7},{10,8},{12,14},{11,9},{13,15},{18,16},{20,... | collective-permute-start | bytes 7864328 | tf_op jit(solution)/shard_map/ppermute | solution.py:268
  75.0 213.9 %collective-permute-start.2 = (bf16[2048,640]{1,0:T(8,128)(2,1)}, bf16[2048,640]{1,0:T(8,128)(2,1)}, u32[]{:S(2)}, u32[]{:S(2)}) collective-permute-start(bf16[2048,640]{1,0:T(8,128)(2,1)} %collective-permute-done.1.chunk_ref), channel_id=1, source_target_pairs={{2,0},{4,6},{3,1},{5,7},{10,8},{12,14},{11,9},{13,15},{18,16},{20,... | collective-permute-start | bytes 7864328 | tf_op jit(solution)/shard_map/ppermute | solution.py:268
  76.4 3.6 %collective-permute-start.15 = (bf16[320]{0:T(512)(128)(2,1)S(1)}, bf16[320]{0:T(512)(128)(2,1)S(1)}, u32[]{:S(2)}, u32[]{:S(2)}) collective-permute-start(bf16[320]{0:T(512)(128)(2,1)S(1)} %add_convert_fusion), channel_id=1, source_target_pairs={{0,1},{1,0},{2,3},{3,2},{4,5},{5,4},{6,7},{7,6},{8,9},{9,8},{10,11... | collective-permute-start | bytes 1928 | tf_op jit(solution)/shard_map/ppermute | solution.py:256
  80.1 120.0 %collective-permute-start.16 = (bf16[640]{0:T(1024)(128)(2,1)S(1)}, bf16[640]{0:T(1024)(128)(2,1)S(1)}, u32[]{:S(2)}, u32[]{:S(2)}) collective-permute-start(bf16[640]{0:T(1024)(128)(2,1)S(1)} %pad_maximum_fusion.1), channel_id=1, source_target_pairs={{0,2},{2,0},{4,6},{6,4},{1,3},{3,1},{5,7},{7,5},{8,10},{10,8},{12,... | collective-permute-start | bytes 3848 | tf_op jit(solution)/shard_map/ppermute | solution.py:268
  134.1 66.6 %collective-permute-start.19 = (bf16[640]{0:T(1024)(128)(2,1)S(1)}, bf16[640]{0:T(1024)(128)(2,1)S(1)}, u32[]{:S(2)}, u32[]{:S(2)}) collective-permute-start(bf16[640]{0:T(1024)(128)(2,1)S(1)} %pad_maximum_fusion.1), channel_id=1, source_target_pairs={{2,4},{4,2},{3,5},{5,3},{10,12},{12,10},{11,13},{13,11},{18,20},{2... | collective-permute-start | bytes 3848 | tf_op jit(solution)/shard_map/ppermute | solution.py:268
  200.1 2.0 collective-permute-start.17
  200.8 5.5 %collective-permute-start.20 = (bf16[640]{0:T(1024)(128)(2,1)S(1)}, bf16[640]{0:T(1024)(128)(2,1)S(1)}, u32[]{:S(2)}, u32[]{:S(2)}) collective-permute-start(bf16[640]{0:T(1024)(128)(2,1)S(1)} %collective-permute-done.19), channel_id=1, source_target_pairs={{2,0},{4,6},{3,1},{5,7},{10,8},{12,14},{11,9},{13,15},{18,16},{20,... | collective-permute-start | bytes 3848 | tf_op jit(solution)/shard_map/ppermute | solution.py:268
  202.1 10.4 %collective-permute-start.13 = (bf16[512,640]{1,0:T(8,128)(2,1)}, bf16[512,640]{1,0:T(8,128)(2,1)}, u32[]{:S(2)}, u32[]{:S(2)}) collective-permute-start(bf16[512,640]{1,0:T(8,128)(2,1)} %get-tuple-element.10), channel_id=1, source_target_pairs={{2,4},{4,2},{3,5},{5,3},{10,12},{12,10},{11,13},{13,11},{18,20},{2... | collective-permute-start | bytes 1966088 | tf_op jit(solution)/shard_map/ppermute | solution.py:268
  206.3 5.5 %collective-permute-start.18 = (bf16[640]{0:T(1024)(128)(2,1)S(1)}, bf16[640]{0:T(1024)(128)(2,1)S(1)}, u32[]{:S(2)}, u32[]{:S(2)}) collective-permute-start(bf16[640]{0:T(1024)(128)(2,1)S(1)} %collective-permute-done.17), channel_id=1, source_target_pairs={{2,0},{4,6},{3,1},{5,7},{10,8},{12,14},{11,9},{13,15},{18,16},{20,... | collective-permute-start | bytes 3848 | tf_op jit(solution)/shard_map/ppermute | solution.py:268
  211.8 17.1 %collective-permute-start.5 = (bf16[512,640]{1,0:T(8,128)(2,1)S(1)}, bf16[512,640]{1,0:T(8,128)(2,1)S(1)}, u32[]{:S(2)}, u32[]{:S(2)}) collective-permute-start(bf16[512,640]{1,0:T(8,128)(2,1)S(1)} %merge.4.chunk_ref), channel_id=1, source_target_pairs={{0,2},{2,0},{4,6},{6,4},{1,3},{3,1},{5,7},{7,5},{8,10},{10,8},{12,... | collective-permute-start | bytes 1966088 | tf_op jit(solution)/shard_map/ppermute | solution.py:268
  211.8 32.6 %copy-start.1 = (bf16[512,640]{1,0:T(8,128)(2,1)}, bf16[512,640]{1,0:T(8,128)(2,1)S(1)}, u32[]{:S(2)}) copy-start(bf16[512,640]{1,0:T(8,128)(2,1)S(1)} %collective-permute-done.10.chunk_ref) | copy-start | bytes 1966084
  211.8 18.5 %collective-permute-start.8 = (bf16[512,640]{1,0:T(8,128)(2,1)S(1)}, bf16[512,640]{1,0:T(8,128)(2,1)S(1)}, u32[]{:S(2)}, u32[]{:S(2)}) collective-permute-start(bf16[512,640]{1,0:T(8,128)(2,1)S(1)} %merge.4.chunk_ref), channel_id=1, source_target_pairs={{2,4},{4,2},{3,5},{5,3},{10,12},{12,10},{11,13},{13,11},{18,20},{2... | collective-permute-start | bytes 1966088 | tf_op jit(solution)/shard_map/ppermute | solution.py:268
  212.5 26.2 %collective-permute-start.14 = (bf16[512,640]{1,0:T(8,128)(2,1)}, bf16[512,640]{1,0:T(8,128)(2,1)S(1)}, u32[]{:S(2)}, u32[]{:S(2)}) collective-permute-start(bf16[512,640]{1,0:T(8,128)(2,1)} %collective-permute-done.13.chunk_ref), channel_id=1, source_target_pairs={{2,0},{4,6},{3,1},{5,7},{10,8},{12,14},{11,9},{13,15},{18,16},{20,... | collective-permute-start | bytes 1966088 | tf_op jit(solution)/shard_map/ppermute | solution.py:268
  228.8 17.4 %copy-start.3 = (bf16[512,640]{1,0:T(8,128)(2,1)}, bf16[512,640]{1,0:T(8,128)(2,1)S(1)}, u32[]{:S(2)}) copy-start(bf16[512,640]{1,0:T(8,128)(2,1)S(1)} %collective-permute-done.5.chunk_ref) | copy-start | bytes 1966084
  228.8 11.2 %collective-permute-start.11 = (bf16[512,640]{1,0:T(8,128)(2,1)S(1)}, bf16[512,640]{1,0:T(8,128)(2,1)}, u32[]{:S(2)}, u32[]{:S(2)}) collective-permute-start(bf16[512,640]{1,0:T(8,128)(2,1)S(1)} %collective-permute-done.10.chunk_ref), channel_id=1, source_target_pairs={{2,4},{4,2},{3,5},{5,3},{10,12},{12,10},{11,13},{13,11},{18,20},{2... | collective-permute-start | bytes 1966088 | tf_op jit(solution)/shard_map/ppermute | solution.py:268
  230.3 16.0 %copy-start.2 = (bf16[512,640]{1,0:T(8,128)(2,1)}, bf16[512,640]{1,0:T(8,128)(2,1)S(1)}, u32[]{:S(2)}) copy-start(bf16[512,640]{1,0:T(8,128)(2,1)S(1)} %collective-permute-done.8.chunk_ref) | copy-start | bytes 1966084
  230.3 11.1 %collective-permute-start.6 = (bf16[512,640]{1,0:T(8,128)(2,1)S(1)}, bf16[512,640]{1,0:T(8,128)(2,1)}, u32[]{:S(2)}, u32[]{:S(2)}) collective-permute-start(bf16[512,640]{1,0:T(8,128)(2,1)S(1)} %collective-permute-done.5.chunk_ref), channel_id=1, source_target_pairs={{2,4},{4,2},{3,5},{5,3},{10,12},{12,10},{11,13},{13,11},{18,20},{2... | collective-permute-start | bytes 1966088 | tf_op jit(solution)/shard_map/ppermute | solution.py:268
  238.8 1.3 copy-start.4
  238.8 19.2 %collective-permute-start.9 = (bf16[512,640]{1,0:T(8,128)(2,1)S(1)}, bf16[512,640]{1,0:T(8,128)(2,1)}, u32[]{:S(2)}, u32[]{:S(2)}) collective-permute-start(bf16[512,640]{1,0:T(8,128)(2,1)S(1)} %collective-permute-done.8.chunk_ref), channel_id=1, source_target_pairs={{2,0},{4,6},{3,1},{5,7},{10,8},{12,14},{11,9},{13,15},{18,16},{20,... | collective-permute-start | bytes 1966088 | tf_op jit(solution)/shard_map/ppermute | solution.py:268
  240.1 31.9 %collective-permute-start.12 = (bf16[512,640]{1,0:T(8,128)(2,1)}, bf16[512,640]{1,0:T(8,128)(2,1)S(1)}, u32[]{:S(2)}, u32[]{:S(2)}) collective-permute-start(bf16[512,640]{1,0:T(8,128)(2,1)} %collective-permute-done.11.chunk_ref), channel_id=1, source_target_pairs={{2,0},{4,6},{3,1},{5,7},{10,8},{12,14},{11,9},{13,15},{18,16},{20,... | collective-permute-start | bytes 1966088 | tf_op jit(solution)/shard_map/ppermute | solution.py:268
  241.4 40.1 %collective-permute-start.7 = (bf16[512,640]{1,0:T(8,128)(2,1)}, bf16[512,640]{1,0:T(8,128)(2,1)}, u32[]{:S(2)}, u32[]{:S(2)}) collective-permute-start(bf16[512,640]{1,0:T(8,128)(2,1)} %collective-permute-done.6.chunk_ref), channel_id=1, source_target_pairs={{2,0},{4,6},{3,1},{5,7},{10,8},{12,14},{11,9},{13,15},{18,16},{20,... | collective-permute-start | bytes 1966088 | tf_op jit(solution)/shard_map/ppermute | solution.py:268

commit v3 on v1

--- a/solution.py
+++ b/solution.py
@@ -11,10 +11,16 @@
 
 
 KEY, QUERY, VALUE = range(3)
-FIRST, LAST, NORM = (KEY, 0, 4), (VALUE, 6, 2), None
-KEY_REST, QUERY_ALL, VALUE_REST = (KEY, 4, 4), (QUERY, 0, 8), (VALUE, 0, 6)
+EIGHTHS = 8
+FIRST, KEY_REST = (KEY, 0, 4), (KEY, 4, 4)
+QUERY_ALL = (QUERY, 0, 8)
+NORM = None
+VALUE_REST, LAST = (VALUE, 0, 6), (VALUE, 6, 2)
 CHUNKS = (FIRST, KEY_REST, QUERY_ALL, NORM, VALUE_REST, LAST)
-EIGHTHS = 8
+
+
+def extent(columns, chunk):
+    return columns * chunk[1] // EIGHTHS, columns * chunk[2] // EIGHTHS
 
 
 def merged(weight_ref, low_ref, high_ref):
@@ -29,15 +35,11 @@
     chunk_ref[...] = merged(weight_ref, low_ref, high_ref)
 
 
-def merge_kernel(me_ref, weight_ref, low_ref, high_ref, *rest):
-    chunk_ref, out_ref = rest[-2:]
+def merge_kernel(me_ref, weight_ref, low_ref, high_ref, *refs):
+    chunk_ref, out_ref = refs[-2:]
     fresh = merged(weight_ref, low_ref, high_ref)
     chunk_ref[...] = fresh
     out_ref[...] = fresh
-
-
-def extent(columns, chunk):
-    return columns * chunk[1] // EIGHTHS, columns * chunk[2] // EIGHTHS
 
 
 def cost(rows, depth, rank):
@@ -50,13 +52,14 @@
     depth, columns = weight.shape
     rank = high.shape[0]
     start, rows = extent(columns, chunk)
+    first = start // rows
     return pl.pallas_call(
         first_kernel,
         grid=(1,),
         in_specs=[
-            pl.BlockSpec((depth, rows), lambda j: (0, start // rows)),
+            pl.BlockSpec((depth, rows), lambda j: (0, first)),
             pl.BlockSpec((rank, depth), lambda j: (0, 0)),
-            pl.BlockSpec((rank, rows), lambda j: (0, start // rows)),
+            pl.BlockSpec((rank, rows), lambda j: (0, first)),
         ],
         out_specs=pl.BlockSpec(memory_space=pltpu.VMEM),
         out_shape=pltpu.VMEM((rows, depth), jnp.bfloat16),
@@ -69,17 +72,16 @@
     depth, columns = weight.shape
     rank = high.shape[0]
     start, rows = extent(columns, chunk)
-    block = next(b for b in (512, 256, 128) if start % b == 0 and rows % b == 0)
+    block = next(b for b in (512, 384, 256, 128) if start % b == 0 and rows % b == 0)
     first = start // block
-    in_specs = [
+    specs = [
         pl.BlockSpec((depth, block), lambda j, me: (0, first + j)),
         pl.BlockSpec((rank, depth), lambda j, me: (0, 0)),
         pl.BlockSpec((rank, block), lambda j, me: (0, first + j)),
     ]
-    operands = [weight, low_t, high]
-    aliases = {}
+    operands, aliases = [me, weight, low_t, high], {}
     if isinstance(out, jax.Array):
-        in_specs.append(pl.BlockSpec(memory_space=pl.ANY))
+        specs.append(pl.BlockSpec(memory_space=pl.ANY))
         operands.append(out)
         aliases = {4: 1}
     return pl.pallas_call(
@@ -87,7 +89,7 @@
         grid_spec=pltpu.PrefetchScalarGridSpec(
             num_scalar_prefetch=1,
             grid=(rows // block,),
-            in_specs=in_specs,
+            in_specs=specs,
             out_specs=[
                 pl.BlockSpec((block, depth), lambda j, me: (j, 0)),
                 pl.BlockSpec((block, depth), lambda j, me: (first + j, me[0])),
@@ -100,7 +102,7 @@
         input_output_aliases=aliases,
         cost_estimate=cost(rows, depth, rank),
         name="merge",
-    )(me, *operands)
+    )(*operands)
 
 
 def source_of(me, r, parity):
@@ -108,42 +110,34 @@
     return jnp.where(down, me + r, me - r)
 
 
-def place_kernel(n, r, parity, start, pieces, me_ref, chunk_ref, _, out_ref, out_sem, in_sem=None, tiles=None):
+def place_kernel(n, r, parity, start, me_ref, chunk_ref, _, out_ref, sem, stage=None):
     rows, depth = chunk_ref.shape
-    step = rows // pieces
     source = me_ref[0] if r == 0 else source_of(me_ref[0], r, parity)
 
     @pl.when((source >= 0) & (source < n))
     def _():
+        held = chunk_ref
+        if stage is not None:
+            held = stage
+            copy = pltpu.make_async_copy(chunk_ref, held, sem.at[1])
+            copy.start()
+            copy.wait()
         column = pl.multiple_of(source * depth, 128)
-        held = chunk_ref if tiles is None else tiles
-        ins, outs = [], []
-        for p in range(pieces):
-            part = pl.ds(p * step, step)
-            if tiles is not None:
-                ins.append(pltpu.make_async_copy(chunk_ref.at[part], tiles.at[part], in_sem.at[p]))
-            there = out_ref.at[pl.ds(start + p * step, step), pl.ds(column, depth)]
-            outs.append(pltpu.make_async_copy(held.at[part], there, out_sem.at[p]))
-        for copy in ins:
-            copy.start()
-        for p in range(pieces):
-            if ins:
-                ins[p].wait()
-            outs[p].start()
-        for copy in outs:
-            copy.wait()
+        there = out_ref.at[pl.ds(start, rows), pl.ds(column, depth)]
+        copy = pltpu.make_async_copy(held, there, sem.at[0])
+        copy.start()
+        copy.wait()
 
 
 def place(me, n, r, parity, chunk, out, start, in_vmem):
     rows, depth = chunk.shape
-    pieces = 1 if in_vmem or rows % 64 else 4
-    scratch = [pltpu.SemaphoreType.DMA((pieces,))]
+    scratch = [pltpu.SemaphoreType.DMA((2,))]
     if in_vmem:
         chunk = pltpu.with_memory_space_constraint(chunk, pltpu.VMEM)
     else:
-        scratch += [pltpu.SemaphoreType.DMA((pieces,)), pltpu.VMEM((rows, depth), jnp.bfloat16)]
+        scratch.append(pltpu.VMEM((rows, depth), jnp.bfloat16))
     return pl.pallas_call(
-        functools.partial(place_kernel, n, r, parity, start, pieces),
+        functools.partial(place_kernel, n, r, parity, start),
         grid_spec=pltpu.PrefetchScalarGridSpec(
             num_scalar_prefetch=1,
             grid=(1,),
@@ -183,8 +177,7 @@
         ]
 
     steps = []
-    early = (FIRST, KEY_REST, QUERY_ALL)
-    late = (VALUE_REST, LAST)
+    early, late = (FIRST, KEY_REST, QUERY_ALL), (VALUE_REST, LAST)
     for chunk in early:
         steps.append(("merge", 0, 0, chunk))
         steps += hops(1, [chunk], [0])
@@ -262,7 +255,7 @@
         for what, r, parity, chunk in steps:
             if what == "merge":
                 weight, low_t, high = inputs[chunk[0]]
-                if chunk is FIRST:
+                if chunk == FIRST:
                     piece = merge_first(weight, low_t, high, chunk)
                 else:
                     shape = jax.ShapeDtypeStruct((weight.shape[1], depth * n), jnp.bfloat16)

time: 316 us -> 318 us (level)
  no operation moved by 1% of the time
where the time goes in v3:
time: 318 us; the launch traced here: 316 us
  waiting for transfers between devices  163 us (51%)
  starting transfers between devices  105 us (33%)
  Pallas kernels  42.5 us (13%)
  local copies, waits for them, and re-layouts  3.96 us (1%)
    ppermute x30, waiting for transfers between devices, on_device(): got[r, parity, chunk] = lax.ppermute(held, 'shard', hop_pairs(n, r, parity))  163 us
    ppermute x30, starting transfers between devices, on_device(): got[r, parity, chunk] = lax.ppermute(held, 'shard', hop_pairs(n, r, parity))  103 us
    pallas_call x26, Pallas kernels, place(): pl.pallas_call(functools.partial(place_kernel, n, r, parity, start), grid...  29.5 us
    pallas_call x4, Pallas kernels, merge(): pl.pallas_call(merge_kernel, grid_spec=pltpu.PrefetchScalarGridSpec(num_s...  11.7 us
  transfers between devices with their start and end apart: 31, of which 9 were waited for; matrix products, arithmetic and copies ran while one was open for 0% of the time, Pallas kernels for 11%

profile of v3, /device:TPU:0, one launch (start us, length us, event | category | flops | bytes accessed | tf_op | source)
XLA Modules:
  0.0 316.5 jit_solution(6584347273471559703)
XLA Ops:
  0.7 5.2 %merge.5 = (bf16[2048,640]{1,0:T(8,128)(2,1)}, bf16[2048,2560]{1,0:T(8,128)(2,1)}) custom-call(s32[1]{0:T(128)} %bitcast.me_ref, bf16[640,2048]{1,0:T(8,128)(2,1)} %weight_ref.5, bf16[64,640]{1,0:T(8,128)(2,1)} %bitcast.8, bf16[64,2048]{1,0:T(8,128)(2,1)} %high_ref.5), custom_call_target="tpu_custom_call" | custom-call | flops 167772160 | bytes 7864320 | tf_op jit(solution)/shard_map/merge/pallas_call | solution.py:87
  5.9 3.1 collective-permute-start
  9.0 2.2 collective-permute-start.3
  11.2 54.9 %collective-permute-done.chunk_ref = bf16[2048,640]{1,0:T(8,128)(2,1)S(1)} collective-permute-done((bf16[2048,640]{1,0:T(8,128)(2,1)}, bf16[2048,640]{1,0:T(8,128)(2,1)S(1)}, u32[]{:S(2)}, u32[]{:S(2)}) %collective-permute-start) | collective-permute-done | bytes 2621472 | tf_op jit(solution)/shard_map/ppermute | solution.py:280
  67.6 2.1 collective-permute-start.1
  72.4 1.8 collective-permute-start.25
  74.2 2.4 merge.8
  76.5 2.0 merge.9
  78.5 59.5 %collective-permute-start.15 = (bf16[128,640]{1,0:T(8,128)(2,1)}, bf16[128,640]{1,0:T(8,128)(2,1)S(1)}, u32[]{:S(2)}, u32[]{:S(2)}) collective-permute-start(bf16[128,640]{1,0:T(8,128)(2,1)} %get-tuple-element.17), channel_id=1, source_target_pairs={{0,2},{2,0},{4,6},{6,4},{1,3},{3,1},{5,7},{7,5},{8,10},{10,8},{12,... | collective-permute-start | bytes 491528 | tf_op jit(solution)/shard_map/ppermute | solution.py:280
  140.0 6.7 %collective-permute-start.26 = (bf16[640]{0:T(1024)(128)(2,1)S(1)}, bf16[640]{0:T(1024)(128)(2,1)S(1)}, u32[]{:S(2)}, u32[]{:S(2)}) collective-permute-start(bf16[640]{0:T(1024)(128)(2,1)S(1)} %pad_maximum_fusion.1), channel_id=1, source_target_pairs={{0,2},{2,0},{4,6},{6,4},{1,3},{3,1},{5,7},{7,5},{8,10},{10,8},{12,... | collective-permute-start | bytes 3848 | tf_op jit(solution)/shard_map/ppermute | solution.py:280
  146.7 46.7 %collective-permute-done.26 = bf16[640]{0:T(1024)(128)(2,1)S(1)} collective-permute-done((bf16[640]{0:T(1024)(128)(2,1)S(1)}, bf16[640]{0:T(1024)(128)(2,1)S(1)}, u32[]{:S(2)}, u32[]{:S(2)}) %collective-permute-start.26) | collective-permute-done | bytes 1312 | tf_op jit(solution)/shard_map/ppermute | solution.py:280
  196.1 10.9 %collective-permute-done.30 = bf16[640]{0:T(1024)(128)(2,1)S(1)} collective-permute-done((bf16[640]{0:T(1024)(128)(2,1)S(1)}, bf16[640]{0:T(1024)(128)(2,1)S(1)}, u32[]{:S(2)}, u32[]{:S(2)}) %collective-permute-start.30) | collective-permute-done | bytes 1312 | tf_op jit(solution)/shard_map/ppermute | solution.py:280
  209.6 2.9 collective-permute-done.28
  213.9 2.1 merge.6
  216.7 6.5 %collective-permute-start.5 = (bf16[256,640]{1,0:T(8,128)(2,1)}, bf16[256,640]{1,0:T(8,128)(2,1)S(1)}, u32[]{:S(2)}, u32[]{:S(2)}) collective-permute-start(bf16[256,640]{1,0:T(8,128)(2,1)} %get-tuple-element.14), channel_id=1, source_target_pairs={{0,2},{2,0},{4,6},{6,4},{1,3},{3,1},{5,7},{7,5},{8,10},{10,8},{12,... | collective-permute-start | bytes 983048 | tf_op jit(solution)/shard_map/ppermute | solution.py:280
  224.0 7.9 %collective-permute-done.5.chunk_ref = bf16[256,640]{1,0:T(8,128)(2,1)S(1)} collective-permute-done((bf16[256,640]{1,0:T(8,128)(2,1)}, bf16[256,640]{1,0:T(8,128)(2,1)S(1)}, u32[]{:S(2)}, u32[]{:S(2)}) %collective-permute-start.5) | collective-permute-done | bytes 327712 | tf_op jit(solution)/shard_map/ppermute | solution.py:280
  233.9 7.2 %collective-permute-done.18.chunk_ref = bf16[384,640]{1,0:T(8,128)(2,1)S(1)} collective-permute-done((bf16[384,640]{1,0:T(8,128)(2,1)S(1)}, bf16[384,640]{1,0:T(8,128)(2,1)S(1)}, u32[]{:S(2)}, u32[]{:S(2)}) %collective-permute-start.18) | collective-permute-done | bytes 491552 | tf_op jit(solution)/shard_map/ppermute | solution.py:280
  243.8 7.7 %collective-permute-done.14.chunk_ref = bf16[256,640]{1,0:T(8,128)(2,1)S(1)} collective-permute-done((bf16[256,640]{1,0:T(8,128)(2,1)S(1)}, bf16[256,640]{1,0:T(8,128)(2,1)S(1)}, u32[]{:S(2)}, u32[]{:S(2)}) %collective-permute-start.14) | collective-permute-done | bytes 327712 | tf_op jit(solution)/shard_map/ppermute | solution.py:280
  253.5 13.8 %collective-permute-done.12.chunk_ref = bf16[256,640]{1,0:T(8,128)(2,1)S(1)} collective-permute-done((bf16[256,640]{1,0:T(8,128)(2,1)S(1)}, bf16[256,640]{1,0:T(8,128)(2,1)S(1)}, u32[]{:S(2)}, u32[]{:S(2)}) %collective-permute-start.12) | collective-permute-done | bytes 327712 | tf_op jit(solution)/shard_map/ppermute | solution.py:280
  270.2 1.7 place.32._
  272.0 1.8 place.42._
  273.8 1.7 place.34._
  275.6 1.6 place.44._
  277.3 1.7 place.36._
  279.1 1.8 place.46._
  282.3 1.7 place.38._
  289.9 1.7 place.40._
  291.6 10.9 %collective-permute-done.7.chunk_ref = bf16[256,640]{1,0:T(8,128)(2,1)S(1)} collective-permute-done((bf16[256,640]{1,0:T(8,128)(2,1)S(1)}, bf16[256,640]{1,0:T(8,128)(2,1)S(1)}, u32[]{:S(2)}, u32[]{:S(2)}) %collective-permute-start.7) | collective-permute-done | bytes 327712 | tf_op jit(solution)/shard_map/ppermute | solution.py:280
  303.3 1.7 place.41
  306.6 3.3 %place.26._ = bf16[2048,2560]{1,0:T(8,128)(2,1)} custom-call(s32[1]{0:T(128)} %bitcast.me_ref, bf16[2048,640]{1,0:T(8,128)(2,1)} %copy-done, bf16[2048,2560]{1,0:T(8,128)(2,1)} %get-tuple-element.13._), custom_call_target="tpu_custom_call", output_to_operand_aliasing={{}: (2, {})} | custom-call | flops 1310720 | bytes 5242880 | tf_op jit(solution)/shard_map/place/pallas_call | solution.py:139
  309.9 3.3 %place.28._ = bf16[2048,2560]{1,0:T(8,128)(2,1)} custom-call(s32[1]{0:T(128)} %bitcast.me_ref, bf16[2048,640]{1,0:T(8,128)(2,1)} %collective-permute-done.4.chunk_ref, bf16[2048,2560]{1,0:T(8,128)(2,1)} %place.27._), custom_call_target="tpu_custom_call", output_to_operand_aliasing={{}: (2, {})} | custom-call | flops 1310720 | bytes 5242880 | tf_op jit(solution)/shard_map/place/pallas_call | solution.py:139
  313.2 3.3 %place.30 = bf16[2048,2560]{1,0:T(8,128)(2,1)} custom-call(s32[1]{0:T(128)} %bitcast.me_ref, bf16[2048,640]{1,0:T(8,128)(2,1)} %collective-permute-done.2.chunk_ref, bf16[2048,2560]{1,0:T(8,128)(2,1)} %place.29._), custom_call_target="tpu_custom_call", output_to_operand_aliasing={{}: (2, {})} | custom-call | flops 1310720 | bytes 5242880 | tf_op jit(solution)/shard_map/place/pallas_call | solution.py:139
  (109 shorter events, 33.3 us)
Async XLA Ops:
  5.9 60.1 %collective-permute-start = (bf16[2048,640]{1,0:T(8,128)(2,1)}, bf16[2048,640]{1,0:T(8,128)(2,1)S(1)}, u32[]{:S(2)}, u32[]{:S(2)}) collective-permute-start(bf16[2048,640]{1,0:T(8,128)(2,1)} %get-tuple-element.12), channel_id=1, source_target_pairs={{0,2},{2,0},{4,6},{6,4},{1,3},{3,1},{5,7},{7,5},{8,10},{10,8},{12,... | collective-permute-start | bytes 7864328 | tf_op jit(solution)/shard_map/ppermute | solution.py:280
  9.0 60.8 %collective-permute-start.3 = (bf16[2048,640]{1,0:T(8,128)(2,1)}, bf16[2048,640]{1,0:T(8,128)(2,1)}, u32[]{:S(2)}, u32[]{:S(2)}) collective-permute-start(bf16[2048,640]{1,0:T(8,128)(2,1)} %get-tuple-element.12), channel_id=1, source_target_pairs={{2,4},{4,2},{3,5},{5,3},{10,12},{12,10},{11,13},{13,11},{18,20},{2... | collective-permute-start | bytes 7864328 | tf_op jit(solution)/shard_map/ppermute | solution.py:280
  67.6 3.4 %collective-permute-start.1 = (bf16[2048,640]{1,0:T(8,128)(2,1)S(1)}, bf16[2048,640]{1,0:T(8,128)(2,1)}, u32[]{:S(2)}, u32[]{:S(2)}) collective-permute-start(bf16[2048,640]{1,0:T(8,128)(2,1)S(1)} %collective-permute-done.chunk_ref), channel_id=1, source_target_pairs={{2,4},{4,2},{3,5},{5,3},{10,12},{12,10},{11,13},{13,11},{18,20},{2... | collective-permute-start | bytes 7864328 | tf_op jit(solution)/shard_map/ppermute | solution.py:280
  69.8 240.1 %collective-permute-start.4 = (bf16[2048,640]{1,0:T(8,128)(2,1)}, bf16[2048,640]{1,0:T(8,128)(2,1)}, u32[]{:S(2)}, u32[]{:S(2)}) collective-permute-start(bf16[2048,640]{1,0:T(8,128)(2,1)} %collective-permute-done.3.chunk_ref), channel_id=1, source_target_pairs={{2,0},{4,6},{3,1},{5,7},{10,8},{12,14},{11,9},{13,15},{18,16},{20,... | collective-permute-start | bytes 7864328 | tf_op jit(solution)/shard_map/ppermute | solution.py:280
  71.1 242.1 %collective-permute-start.2 = (bf16[2048,640]{1,0:T(8,128)(2,1)}, bf16[2048,640]{1,0:T(8,128)(2,1)}, u32[]{:S(2)}, u32[]{:S(2)}) collective-permute-start(bf16[2048,640]{1,0:T(8,128)(2,1)} %collective-permute-done.1.chunk_ref), channel_id=1, source_target_pairs={{2,0},{4,6},{3,1},{5,7},{10,8},{12,14},{11,9},{13,15},{18,16},{20,... | collective-permute-start | bytes 7864328 | tf_op jit(solution)/shard_map/ppermute | solution.py:280
  72.4 66.2 %collective-permute-start.25 = (bf16[320]{0:T(512)(128)(2,1)S(1)}, bf16[320]{0:T(512)(128)(2,1)S(1)}, u32[]{:S(2)}, u32[]{:S(2)}) collective-permute-start(bf16[320]{0:T(512)(128)(2,1)S(1)} %add_convert_fusion), channel_id=1, source_target_pairs={{0,1},{1,0},{2,3},{3,2},{4,5},{5,4},{6,7},{7,6},{8,9},{9,8},{10,11... | collective-permute-start | bytes 1928 | tf_op jit(solution)/shard_map/ppermute | solution.py:268
  76.5 146.7 %copy-start.20 = (bf16[384,640]{1,0:T(8,128)(2,1)S(1)}, bf16[384,640]{1,0:T(8,128)(2,1)}, u32[]{:S(2)}) copy-start(bf16[384,640]{1,0:T(8,128)(2,1)} %get-tuple-element.18) | copy-start | bytes 1474564
  78.5 134.0 %collective-permute-start.15 = (bf16[128,640]{1,0:T(8,128)(2,1)}, bf16[128,640]{1,0:T(8,128)(2,1)S(1)}, u32[]{:S(2)}, u32[]{:S(2)}) collective-permute-start(bf16[128,640]{1,0:T(8,128)(2,1)} %get-tuple-element.17), channel_id=1, source_target_pairs={{0,2},{2,0},{4,6},{6,4},{1,3},{3,1},{5,7},{7,5},{8,10},{10,8},{12,... | collective-permute-start | bytes 491528 | tf_op jit(solution)/shard_map/ppermute | solution.py:280
  137.9 0.7 collective-permute-start.21
  138.7 74.5 %collective-permute-start.22 = (bf16[128,640]{1,0:T(8,128)(2,1)S(1)}, bf16[128,640]{1,0:T(8,128)(2,1)S(1)}, u32[]{:S(2)}, u32[]{:S(2)}) collective-permute-start(bf16[128,640]{1,0:T(8,128)(2,1)S(1)} %collective-permute-done.21.chunk_ref), channel_id=1, source_target_pairs={{2,0},{4,6},{3,1},{5,7},{10,8},{12,14},{11,9},{13,15},{18,16},{20,... | collective-permute-start | bytes 491528 | tf_op jit(solution)/shard_map/ppermute | solution.py:280
  140.0 53.4 %collective-permute-start.26 = (bf16[640]{0:T(1024)(128)(2,1)S(1)}, bf16[640]{0:T(1024)(128)(2,1)S(1)}, u32[]{:S(2)}, u32[]{:S(2)}) collective-permute-start(bf16[640]{0:T(1024)(128)(2,1)S(1)} %pad_maximum_fusion.1), channel_id=1, source_target_pairs={{0,2},{2,0},{4,6},{6,4},{1,3},{3,1},{5,7},{7,5},{8,10},{10,8},{12,... | collective-permute-start | bytes 3848 | tf_op jit(solution)/shard_map/ppermute | solution.py:280
  193.4 0.7 collective-permute-start.29
  194.1 0.7 collective-permute-start.27
  194.8 12.2 %collective-permute-start.30 = (bf16[640]{0:T(1024)(128)(2,1)S(1)}, bf16[640]{0:T(1024)(128)(2,1)S(1)}, u32[]{:S(2)}, u32[]{:S(2)}) collective-permute-start(bf16[640]{0:T(1024)(128)(2,1)S(1)} %collective-permute-done.29), channel_id=1, source_target_pairs={{2,0},{4,6},{3,1},{5,7},{10,8},{12,14},{11,9},{13,15},{18,16},{20,... | collective-permute-start | bytes 3848 | tf_op jit(solution)/shard_map/ppermute | solution.py:280
  207.0 5.5 %collective-permute-start.28 = (bf16[640]{0:T(1024)(128)(2,1)S(1)}, bf16[640]{0:T(1024)(128)(2,1)S(1)}, u32[]{:S(2)}, u32[]{:S(2)}) collective-permute-start(bf16[640]{0:T(1024)(128)(2,1)S(1)} %collective-permute-done.27), channel_id=1, source_target_pairs={{2,0},{4,6},{3,1},{5,7},{10,8},{12,14},{11,9},{13,15},{18,16},{20,... | collective-permute-start | bytes 3848 | tf_op jit(solution)/shard_map/ppermute | solution.py:280
  212.5 10.7 %collective-permute-start.8 = (bf16[256,640]{1,0:T(8,128)(2,1)S(1)}, bf16[256,640]{1,0:T(8,128)(2,1)S(1)}, u32[]{:S(2)}, u32[]{:S(2)}) collective-permute-start(bf16[256,640]{1,0:T(8,128)(2,1)S(1)} %merge.7.chunk_ref), channel_id=1, source_target_pairs={{0,2},{2,0},{4,6},{6,4},{1,3},{3,1},{5,7},{7,5},{8,10},{10,8},{12,... | collective-permute-start | bytes 983048 | tf_op jit(solution)/shard_map/ppermute | solution.py:280
  212.5 3.5 %collective-permute-start.16 = (bf16[128,640]{1,0:T(8,128)(2,1)S(1)}, bf16[128,640]{1,0:T(8,128)(2,1)S(1)}, u32[]{:S(2)}, u32[]{:S(2)}) collective-permute-start(bf16[128,640]{1,0:T(8,128)(2,1)S(1)} %collective-permute-done.15.chunk_ref), channel_id=1, source_target_pairs={{2,4},{4,2},{3,5},{5,3},{10,12},{12,10},{11,13},{13,11},{18,20},{2... | collective-permute-start | bytes 491528 | tf_op jit(solution)/shard_map/ppermute | solution.py:280
  213.2 10.1 %collective-permute-start.13 = (bf16[256,640]{1,0:T(8,128)(2,1)S(1)}, bf16[256,640]{1,0:T(8,128)(2,1)S(1)}, u32[]{:S(2)}, u32[]{:S(2)}) collective-permute-start(bf16[256,640]{1,0:T(8,128)(2,1)S(1)} %merge.7.chunk_ref), channel_id=1, source_target_pairs={{2,4},{4,2},{3,5},{5,3},{10,12},{12,10},{11,13},{13,11},{18,20},{2... | collective-permute-start | bytes 983048 | tf_op jit(solution)/shard_map/ppermute | solution.py:280
  216.7 15.2 %collective-permute-start.5 = (bf16[256,640]{1,0:T(8,128)(2,1)}, bf16[256,640]{1,0:T(8,128)(2,1)S(1)}, u32[]{:S(2)}, u32[]{:S(2)}) collective-permute-start(bf16[256,640]{1,0:T(8,128)(2,1)} %get-tuple-element.14), channel_id=1, source_target_pairs={{0,2},{2,0},{4,6},{6,4},{1,3},{3,1},{5,7},{7,5},{8,10},{10,8},{12,... | collective-permute-start | bytes 983048 | tf_op jit(solution)/shard_map/ppermute | solution.py:280
  223.2 17.9 %collective-permute-start.18 = (bf16[384,640]{1,0:T(8,128)(2,1)S(1)}, bf16[384,640]{1,0:T(8,128)(2,1)S(1)}, u32[]{:S(2)}, u32[]{:S(2)}) collective-permute-start(bf16[384,640]{1,0:T(8,128)(2,1)S(1)} %copy-done.20), channel_id=1, source_target_pairs={{0,2},{2,0},{4,6},{6,4},{1,3},{3,1},{5,7},{7,5},{8,10},{10,8},{12,... | collective-permute-start | bytes 1474568 | tf_op jit(solution)/shard_map/ppermute | solution.py:280
  223.3 9.2 %collective-permute-start.11 = (bf16[256,640]{1,0:T(8,128)(2,1)}, bf16[256,640]{1,0:T(8,128)(2,1)S(1)}, u32[]{:S(2)}, u32[]{:S(2)}) collective-permute-start(bf16[256,640]{1,0:T(8,128)(2,1)} %get-tuple-element.14), channel_id=1, source_target_pairs={{2,4},{4,2},{3,5},{5,3},{10,12},{12,10},{11,13},{13,11},{18,20},{2... | collective-permute-start | bytes 983048 | tf_op jit(solution)/shard_map/ppermute | solution.py:280
  231.9 10.6 %collective-permute-start.23 = (bf16[384,640]{1,0:T(8,128)(2,1)S(1)}, bf16[384,640]{1,0:T(8,128)(2,1)S(1)}, u32[]{:S(2)}, u32[]{:S(2)}) collective-permute-start(bf16[384,640]{1,0:T(8,128)(2,1)S(1)} %copy-done.20), channel_id=1, source_target_pairs={{2,4},{4,2},{3,5},{5,3},{10,12},{12,10},{11,13},{13,11},{18,20},{2... | collective-permute-start | bytes 1474568 | tf_op jit(solution)/shard_map/ppermute | solution.py:280
  232.6 18.9 %collective-permute-start.14 = (bf16[256,640]{1,0:T(8,128)(2,1)S(1)}, bf16[256,640]{1,0:T(8,128)(2,1)S(1)}, u32[]{:S(2)}, u32[]{:S(2)}) collective-permute-start(bf16[256,640]{1,0:T(8,128)(2,1)S(1)} %collective-permute-done.13.chunk_ref), channel_id=1, source_target_pairs={{2,0},{4,6},{3,1},{5,7},{10,8},{12,14},{11,9},{13,15},{18,16},{20,... | collective-permute-start | bytes 983048 | tf_op jit(solution)/shard_map/ppermute | solution.py:280
  241.1 11.1 %collective-permute-start.9 = (bf16[256,640]{1,0:T(8,128)(2,1)S(1)}, bf16[256,640]{1,0:T(8,128)(2,1)}, u32[]{:S(2)}, u32[]{:S(2)}) collective-permute-start(bf16[256,640]{1,0:T(8,128)(2,1)S(1)} %collective-permute-done.8.chunk_ref), channel_id=1, source_target_pairs={{2,4},{4,2},{3,5},{5,3},{10,12},{12,10},{11,13},{13,11},{18,20},{2... | collective-permute-start | bytes 983048 | tf_op jit(solution)/shard_map/ppermute | solution.py:280
  242.5 25.5 %collective-permute-start.24 = (bf16[384,640]{1,0:T(8,128)(2,1)S(1)}, bf16[384,640]{1,0:T(8,128)(2,1)S(1)}, u32[]{:S(2)}, u32[]{:S(2)}) collective-permute-start(bf16[384,640]{1,0:T(8,128)(2,1)S(1)} %collective-permute-done.23.chunk_ref), channel_id=1, source_target_pairs={{2,0},{4,6},{3,1},{5,7},{10,8},{12,14},{11,9},{13,15},{18,16},{20,... | collective-permute-start | bytes 1474568 | tf_op jit(solution)/shard_map/ppermute | solution.py:280
  251.5 29.4 %collective-permute-start.19 = (bf16[384,640]{1,0:T(8,128)(2,1)S(1)}, bf16[384,640]{1,0:T(8,128)(2,1)S(1)}, u32[]{:S(2)}, u32[]{:S(2)}) collective-permute-start(bf16[384,640]{1,0:T(8,128)(2,1)S(1)} %collective-permute-done.18.chunk_ref), channel_id=1, source_target_pairs={{2,4},{4,2},{3,5},{5,3},{10,12},{12,10},{11,13},{13,11},{18,20},{2... | collective-permute-start | bytes 1474568 | tf_op jit(solution)/shard_map/ppermute | solution.py:280
  252.2 15.1 %collective-permute-start.12 = (bf16[256,640]{1,0:T(8,128)(2,1)S(1)}, bf16[256,640]{1,0:T(8,128)(2,1)S(1)}, u32[]{:S(2)}, u32[]{:S(2)}) collective-permute-start(bf16[256,640]{1,0:T(8,128)(2,1)S(1)} %collective-permute-done.11.chunk_ref), channel_id=1, source_target_pairs={{2,0},{4,6},{3,1},{5,7},{10,8},{12,14},{11,9},{13,15},{18,16},{20,... | collective-permute-start | bytes 983048 | tf_op jit(solution)/shard_map/ppermute | solution.py:280
  267.3 16.8 %collective-permute-start.6 = (bf16[256,640]{1,0:T(8,128)(2,1)S(1)}, bf16[256,640]{1,0:T(8,128)(2,1)S(1)}, u32[]{:S(2)}, u32[]{:S(2)}) collective-permute-start(bf16[256,640]{1,0:T(8,128)(2,1)S(1)} %collective-permute-done.5.chunk_ref), channel_id=1, source_target_pairs={{2,4},{4,2},{3,5},{5,3},{10,12},{12,10},{11,13},{13,11},{18,20},{2... | collective-permute-start | bytes 983048 | tf_op jit(solution)/shard_map/ppermute | solution.py:280
  268.0 18.3 %collective-permute-start.10 = (bf16[256,640]{1,0:T(8,128)(2,1)}, bf16[256,640]{1,0:T(8,128)(2,1)}, u32[]{:S(2)}, u32[]{:S(2)}) collective-permute-start(bf16[256,640]{1,0:T(8,128)(2,1)} %collective-permute-done.9.chunk_ref), channel_id=1, source_target_pairs={{2,0},{4,6},{3,1},{5,7},{10,8},{12,14},{11,9},{13,15},{18,16},{20,... | collective-permute-start | bytes 983048 | tf_op jit(solution)/shard_map/ppermute | solution.py:280
  280.9 24.1 %collective-permute-start.20 = (bf16[384,640]{1,0:T(8,128)(2,1)S(1)}, bf16[384,640]{1,0:T(8,128)(2,1)S(1)}, u32[]{:S(2)}, u32[]{:S(2)}) collective-permute-start(bf16[384,640]{1,0:T(8,128)(2,1)S(1)} %collective-permute-done.19.chunk_ref), channel_id=1, source_target_pairs={{2,0},{4,6},{3,1},{5,7},{10,8},{12,14},{11,9},{13,15},{18,16},{20,... | collective-permute-start | bytes 1474568 | tf_op jit(solution)/shard_map/ppermute | solution.py:280
  285.0 20.9 %collective-permute-start.17 = (bf16[128,640]{1,0:T(8,128)(2,1)S(1)}, bf16[128,640]{1,0:T(8,128)(2,1)S(1)}, u32[]{:S(2)}, u32[]{:S(2)}) collective-permute-start(bf16[128,640]{1,0:T(8,128)(2,1)S(1)} %copy-done.15), channel_id=1, source_target_pairs={{2,0},{4,6},{3,1},{5,7},{10,8},{12,14},{11,9},{13,15},{18,16},{20,... | collective-permute-start | bytes 491528 | tf_op jit(solution)/shard_map/ppermute | solution.py:280
  286.3 16.3 %collective-permute-start.7 = (bf16[256,640]{1,0:T(8,128)(2,1)S(1)}, bf16[256,640]{1,0:T(8,128)(2,1)S(1)}, u32[]{:S(2)}, u32[]{:S(2)}) collective-permute-start(bf16[256,640]{1,0:T(8,128)(2,1)S(1)} %collective-permute-done.6.chunk_ref), channel_id=1, source_target_pairs={{2,0},{4,6},{3,1},{5,7},{10,8},{12,14},{11,9},{13,15},{18,16},{20,... | collective-permute-start | bytes 983048 | tf_op jit(solution)/shard_map/ppermute | solution.py:280
  (20 other events, 521.2 us)

commit v4 on v2

--- a/solution.py
+++ b/solution.py
@@ -12,7 +12,6 @@
 
 KEY, QUERY, VALUE = range(3)
 FIRST, LAST, NORM = KEY, VALUE, None
-CHUNKS = (KEY, QUERY, NORM, VALUE)
 
 
 def merged(weight_ref, low_ref, high_ref):
@@ -85,53 +84,43 @@
     return jnp.where(down, me + r, me - r)
 
 
-def place_kernel(n, r, parity, pieces, me_ref, chunk_ref, *refs):
-    staged = pieces > 1
-    out_ref, sem, *stage = refs[-4:] if staged else refs[-2:]
-    rows, depth = chunk_ref.shape
-    step = rows // pieces
-    source = me_ref[0] if r == 0 else source_of(me_ref[0], r, parity)
-
-    @pl.when((source >= 0) & (source < n))
-    def _():
-        column = pl.multiple_of(source * depth, 128)
-        parts = [pl.ds(p * step, step) for p in range(pieces)]
-        held = stage[1] if staged else chunk_ref
-        ins = [
-            pltpu.make_async_copy(chunk_ref.at[part], held.at[part], stage[0].at[p])
-            for p, part in enumerate(parts)
-            if staged
-        ]
-        outs = [
-            pltpu.make_async_copy(held.at[part], out_ref.at[part, pl.ds(column, depth)], sem.at[p])
-            for p, part in enumerate(parts)
-        ]
-        for copy in ins:
+def place_kernel(n, hops, staged, me_ref, *refs):
+    chunk_refs, refs = refs[: len(hops)], refs[-3:] if staged else (*refs[-2:], None)
+    out_ref, sem, stage = refs
+
+    for (r, parity), chunk_ref in zip(hops, chunk_refs):
+        source = me_ref[0] if r == 0 else source_of(me_ref[0], r, parity)
+
+        @pl.when((source >= 0) & (source < n))
+        def _():
+            held = chunk_ref
+            if staged:
+                held = stage
+                copy = pltpu.make_async_copy(chunk_ref, held, sem.at[1])
+                copy.start()
+                copy.wait()
+            depth = chunk_ref.shape[1]
+            there = out_ref.at[:, pl.ds(pl.multiple_of(source * depth, 128), depth)]
+            copy = pltpu.make_async_copy(held, there, sem.at[0])
             copy.start()
-        for p in range(pieces):
-            if staged:
-                ins[p].wait()
-            outs[p].start()
-        for copy in outs:
             copy.wait()
 
 
-def place(me, n, r, parity, chunk, out, in_vmem):
-    rows, depth = chunk.shape
-    pieces = 1 if in_vmem else 4
-    sems = pltpu.SemaphoreType.DMA((pieces,))
-    scratch, operands, aliases = [sems], [me, chunk], {}
-    if in_vmem:
-        operands[1] = pltpu.with_memory_space_constraint(chunk, pltpu.VMEM)
+def place(me, n, hops, chunks, out, staged):
+    rows, depth = chunks[0].shape
+    scratch = [pltpu.SemaphoreType.DMA((2,))]
+    specs = [pl.BlockSpec(memory_space=pl.ANY if staged else pltpu.VMEM)] * len(hops)
+    if staged:
+        scratch.append(pltpu.VMEM((rows, depth), jnp.bfloat16))
     else:
-        scratch += [sems, pltpu.VMEM((rows, depth), jnp.bfloat16)]
+        chunks = [pltpu.with_memory_space_constraint(chunk, pltpu.VMEM) for chunk in chunks]
+    operands, aliases = [me, *chunks], {}
     if isinstance(out, jax.Array):
+        aliases = {len(operands): 0}
         operands.append(out)
-        aliases = {2: 0}
-    specs = [pl.BlockSpec(memory_space=pltpu.VMEM if in_vmem else pl.ANY)]
-    specs += [pl.BlockSpec(memory_space=pl.ANY)] * (len(operands) - 2)
+        specs.append(pl.BlockSpec(memory_space=pl.ANY))
     return pl.pallas_call(
-        functools.partial(place_kernel, n, r, parity, pieces),
+        functools.partial(place_kernel, n, hops, staged),
         grid_spec=pltpu.PrefetchScalarGridSpec(
             num_scalar_prefetch=1,
             grid=(1,),
@@ -159,35 +148,41 @@
 
 
 def steps_of(n):
-    def hops(r, chunks, parities=(0, 1)):
-        return [
-            ("hop", r, parity, chunk)
-            for parity in parities
-            for chunk in chunks
-            if hop_pairs(n, r, parity)
-        ]
+    def hops(chunk, *pairs):
+        return [("hop", pair, chunk) for pair in pairs if hop_pairs(n, *pair)]
 
     steps = []
     for chunk in (FIRST, QUERY):
-        steps.append(("merge", 0, 0, chunk))
-        steps += hops(1, [chunk], [0])
-    steps += hops(1, [FIRST, QUERY], [1])
-    steps.append(("place", 0, 0, FIRST))
-    steps.append(("merge", 0, 0, LAST))
-    steps += hops(1, [LAST])
-    steps.append(("exchange", 0, 0, NORM))
-    steps += hops(1, [NORM])
-    for r in range(2, n + 1):
-        for chunk in CHUNKS:
-            steps += hops(r, [chunk])
-            if chunk is NORM:
-                if r == n:
-                    steps.append(("norm", 0, 0, NORM))
-                continue
-            for parity in (0, 1):
-                if hop_pairs(n, r - 1, parity):
-                    steps.append(("place", r - 1, parity, chunk))
+        steps.append(("merge", None, chunk))
+        steps += hops(chunk, (1, 0))
+    steps += hops(FIRST, (1, 1)) + hops(QUERY, (1, 1))
+    steps.append(("place", ((0, 0),), FIRST))
+    steps.append(("merge", None, LAST))
+    steps += hops(LAST, (1, 0), (1, 1))
+    steps.append(("exchange", None, NORM))
+    steps += [("shift", k, NORM) for k in range(1, n)]
+    for r in range(2, n + 2):
+        for chunk in (FIRST, QUERY, LAST):
+            if r == n and chunk == LAST:
+                steps.append(("norm", None, NORM))
+            steps += hops(chunk, (r, 0), (r, 1))
+            came = tuple(pair for pair in ((r - 1, 0), (r - 2, 1)) if r > 2 or pair[1] == 0)
+            came = tuple(pair for pair in came if hop_pairs(n, *pair))
+            if came:
+                steps.append(("place", came, chunk))
+    if n == 1:
+        steps.append(("norm", None, NORM))
     return steps
+
+
+def ordered(shifted, me, n):
+    parts = []
+    for j in range(n):
+        part = shifted[0]
+        for k in range(1, n):
+            part = jnp.where(me == (j + k) % n, shifted[k], part)
+        parts.append(part)
+    return parts
 
 
 def gathered(arrays, norm_train, norm_step):
@@ -242,42 +237,33 @@
         }
         outs = {}
         got = {}
-        for what, r, parity, chunk in steps:
+        for what, hop, chunk in steps:
             if what == "merge":
                 if chunk == FIRST:
                     piece = merge_first(*inputs[chunk])
                     outs[chunk] = jax.ShapeDtypeStruct((piece.shape[0], depth * n), piece.dtype)
                 else:
                     piece, outs[chunk] = merge(me_ref, *inputs[chunk], depth * n)
-                got[0, 0, chunk] = got[0, 1, chunk] = piece
+                got[(0, 0), chunk] = got[(0, 1), chunk] = piece
+            elif what == "hop":
+                r, parity = hop
+                held = got[(r - 1, 1 - parity), chunk]
+                got[hop, chunk] = lax.ppermute(held, "shard", hop_pairs(n, r, parity))
+            elif what == "place":
+                pieces = [got[pair, chunk] for pair in hop]
+                staged = not (hop[0][0] == 0 or (hop[0][0] >= n - 1 and chunk == LAST))
+                outs[chunk] = place(me_ref, n, hop, pieces, outs[chunk], staged)
             elif what == "exchange":
                 share = (norm_train + norm_step).astype(jnp.bfloat16)
                 shares = [share] + [
                     lax.ppermute(share, "tp", [(j, (j + k) % nt) for j in range(nt)])
                     for k in range(1, nt)
                 ]
-                parts = []
-                for j in range(nt):
-                    part = share
-                    for k in range(1, nt):
-                        part = jnp.where(mine == (j + k) % nt, shares[k], part)
-                    parts.append(part)
-                got[0, 0, NORM] = got[0, 1, NORM] = jnp.concatenate(parts)
-            elif what == "hop":
-                held = got[r - 1, 1 - parity, chunk]
-                got[r, parity, chunk] = lax.ppermute(held, "shard", hop_pairs(n, r, parity))
-            elif what == "place":
-                in_vmem = r == 0 or (r == n - 1 and chunk == LAST)
-                outs[chunk] = place(me_ref, n, r, parity, got[r, parity, chunk], outs[chunk], in_vmem)
+                rows = [jnp.concatenate(ordered(shares, mine, nt))]
+            elif what == "shift":
+                rows.append(lax.ppermute(rows[0], "shard", [(j, (j + hop) % n) for j in range(n)]))
             else:
-                rows = []
-                for s in range(n):
-                    row = got[0, 0, NORM]
-                    for (r, parity, chunk), value in got.items():
-                        if chunk is NORM and r > 0:
-                            row = jnp.where(source_of(me, r, parity) == s, value, row)
-                    rows.append(row)
-                serve_norm = jnp.concatenate(rows)
+                serve_norm = jnp.concatenate(ordered(rows, me, n))
         return outs[QUERY], outs[KEY], outs[VALUE], serve_norm
 
     in_specs = (

time: 292 us -> 289 us (0.990)
  starting transfers between devices: 83 us -> 79.7 us
    ppermute x20 -> x18, starting transfers between devices: 81.4 us -> 78.1 us  [the longest x3 55.5 us: on_device(): lax.ppermute(rows[0], 'shard', [(j, (j + hop) % n) for j in range(n)])]
    pallas_call x16 -> x10, Pallas kernels: 19.7 us -> 21.2 us  [place(): pl.pallas_call(functools.partial(place_kernel, n, hops, staged), grid_spe...]
    ppermute x20 -> x18, waiting for transfers between devices: 176 us -> 174 us  [the longest x15 107 us: on_device(): got[hop, chunk] = lax.ppermute(held, 'shard', hop_pairs(n, r, parity))]
  transfers between devices with their start and end apart: 21 -> 19, of which waited for: 10 -> 9; matrix products, arithmetic and copies ran while one was open for 0% -> 0% of each run, Pallas kernels for 7% -> 8%
where the time goes in v4:
time: 289 us; the launch traced here: 288 us
  waiting for transfers between devices  176 us (61%)
  starting transfers between devices  79.7 us (28%)
  Pallas kernels  30.4 us (11%)
    ppermute x15, waiting for transfers between devices, on_device(): got[hop, chunk] = lax.ppermute(held, 'shard', hop_pairs(n, r, parity))  107 us
    ppermute x3, waiting for transfers between devices, on_device(): lax.ppermute(rows[0], 'shard', [(j, (j + hop) % n) for j in range(n)])  67.7 us
    ppermute x3, starting transfers between devices, on_device(): lax.ppermute(rows[0], 'shard', [(j, (j + hop) % n) for j in range(n)])  55.5 us
    ppermute x15, starting transfers between devices, on_device(): got[hop, chunk] = lax.ppermute(held, 'shard', hop_pairs(n, r, parity))  22.6 us
    pallas_call x10, Pallas kernels, place(): pl.pallas_call(functools.partial(place_kernel, n, hops, staged), grid_spe...  21.2 us
    pallas_call x2, Pallas kernels, merge(): pl.pallas_call(merge_kernel, grid_spec=pltpu.PrefetchScalarGridSpec(num_s...  7.69 us
  transfers between devices with their start and end apart: 19, of which 9 were waited for; matrix products, arithmetic and copies ran while one was open for 0% of the time, Pallas kernels for 8%

profile of v4, /device:TPU:0, one launch (start us, length us, event | category | flops | bytes accessed | tf_op | source)
XLA Modules:
  0.0 288.2 jit_solution(4048832566955886132)
XLA Ops:
  0.7 5.2 %merge.3 = (bf16[2048,640]{1,0:T(8,128)(2,1)}, bf16[2048,2560]{1,0:T(8,128)(2,1)}) custom-call(s32[1]{0:T(128)} %bitcast.me_ref, bf16[640,2048]{1,0:T(8,128)(2,1)} %weight_ref.3, bf16[64,640]{1,0:T(8,128)(2,1)} %bitcast.4, bf16[64,2048]{1,0:T(8,128)(2,1)} %high_ref.3), custom_call_target="tpu_custom_call" | custom-call | flops 167772160 | bytes 7864320 | tf_op jit(solution)/shard_map/merge/pallas_call | solution.py:58
  5.9 3.1 %collective-permute-start = (bf16[2048,640]{1,0:T(8,128)(2,1)}, bf16[2048,640]{1,0:T(8,128)(2,1)S(1)}, u32[]{:S(2)}, u32[]{:S(2)}) collective-permute-start(bf16[2048,640]{1,0:T(8,128)(2,1)} %get-tuple-element.8), channel_id=1, source_target_pairs={{0,2},{2,0},{4,6},{6,4},{1,3},{3,1},{5,7},{7,5},{8,10},{10,8},{12,... | collective-permute-start | bytes 7864328 | tf_op jit(solution)/shard_map/ppermute | solution.py:251
  9.0 2.2 collective-permute-start.3
  11.2 54.9 %collective-permute-done.refs_0_ = bf16[2048,640]{1,0:T(8,128)(2,1)S(1)} collective-permute-done((bf16[2048,640]{1,0:T(8,128)(2,1)}, bf16[2048,640]{1,0:T(8,128)(2,1)S(1)}, u32[]{:S(2)}, u32[]{:S(2)}) %collective-permute-start) | collective-permute-done | bytes 2621472 | tf_op jit(solution)/shard_map/ppermute | solution.py:251
  66.0 2.3 collective-permute-start.1
  68.3 2.4 merge.5
  70.8 3.0 %collective-permute-start.10 = (bf16[512,640]{1,0:T(8,128)(2,1)}, bf16[512,640]{1,0:T(8,128)(2,1)S(1)}, u32[]{:S(2)}, u32[]{:S(2)}) collective-permute-start(bf16[512,640]{1,0:T(8,128)(2,1)} %get-tuple-element.10), channel_id=1, source_target_pairs={{0,2},{2,0},{4,6},{6,4},{1,3},{3,1},{5,7},{7,5},{8,10},{10,8},{12,... | collective-permute-start | bytes 1966088 | tf_op jit(solution)/shard_map/ppermute | solution.py:251
  75.0 1.3 collective-permute-start.2
  76.4 1.6 collective-permute-start.15
  78.0 2.1 collective-permute-done.15
  80.1 1.3 collective-permute-start.16
  81.4 54.2 %collective-permute-start.17 = (bf16[640]{0:T(1024)(128)(2,1)S(1)}, bf16[640]{0:T(1024)(128)(2,1)S(1)}, u32[]{:S(2)}, u32[]{:S(2)}) collective-permute-start(bf16[640]{0:T(1024)(128)(2,1)S(1)} %pad_maximum_fusion.1), channel_id=1, source_target_pairs={{0,4},{2,6},{4,0},{6,2},{1,5},{3,7},{5,1},{7,3},{8,12},{10,14},{12... | collective-permute-start | bytes 3848 | tf_op jit(solution)/shard_map/ppermute | solution.py:264
  135.6 64.6 %collective-permute-done.16 = bf16[640]{0:T(1024)(128)(2,1)S(1)} collective-permute-done((bf16[640]{0:T(1024)(128)(2,1)S(1)}, bf16[640]{0:T(1024)(128)(2,1)S(1)}, u32[]{:S(2)}, u32[]{:S(2)}) %collective-permute-start.16) | collective-permute-done | bytes 1312 | tf_op jit(solution)/shard_map/ppermute | solution.py:264
  200.2 1.5 merge.4.refs_0_
  202.4 3.2 %collective-permute-done.18 = bf16[640]{0:T(1024)(128)(2,1)S(1)} collective-permute-done((bf16[640]{0:T(1024)(128)(2,1)S(1)}, bf16[640]{0:T(1024)(128)(2,1)S(1)}, u32[]{:S(2)}, u32[]{:S(2)}) %collective-permute-start.18) | collective-permute-done | bytes 1312 | tf_op jit(solution)/shard_map/ppermute | solution.py:264
  205.6 1.5 collective-permute-start.8
  208.4 12.5 %collective-permute-done.5.refs_0_ = bf16[512,640]{1,0:T(8,128)(2,1)S(1)} collective-permute-done((bf16[512,640]{1,0:T(8,128)(2,1)S(1)}, bf16[512,640]{1,0:T(8,128)(2,1)S(1)}, u32[]{:S(2)}, u32[]{:S(2)}) %collective-permute-start.5) | collective-permute-done | bytes 655392 | tf_op jit(solution)/shard_map/ppermute | solution.py:251
  221.6 1.5 collective-permute-start.6
  223.1 10.2 %collective-permute-done.14.refs_0_ = bf16[512,640]{1,0:T(8,128)(2,1)S(1)} collective-permute-done((bf16[512,640]{1,0:T(8,128)(2,1)S(1)}, bf16[512,640]{1,0:T(8,128)(2,1)S(1)}, u32[]{:S(2)}, u32[]{:S(2)}) %collective-permute-start.14) | collective-permute-done | bytes 655392 | tf_op jit(solution)/shard_map/ppermute | solution.py:251
  234.7 1.3 collective-permute-start.12
  236.0 1.3 collective-permute-start.7
  238.9 1.9 place.17.refs_2_
  240.8 1.9 place.14.refs_2_
  242.8 1.9 place.18.refs_2_
  244.7 6.2 %collective-permute-done.9.refs_0_ = bf16[512,640]{1,0:T(8,128)(2,1)} collective-permute-done((bf16[512,640]{1,0:T(8,128)(2,1)}, bf16[512,640]{1,0:T(8,128)(2,1)}, u32[]{:S(2)}, u32[]{:S(2)}) %collective-permute-start.9) | collective-permute-done | bytes 655392 | tf_op jit(solution)/shard_map/ppermute | solution.py:251
  250.9 1.9 place.15.refs_2_
  252.8 11.7 %collective-permute-done.12.refs_0_ = bf16[512,640]{1,0:T(8,128)(2,1)S(1)} collective-permute-done((bf16[512,640]{1,0:T(8,128)(2,1)S(1)}, bf16[512,640]{1,0:T(8,128)(2,1)S(1)}, u32[]{:S(2)}, u32[]{:S(2)}) %collective-permute-start.12) | collective-permute-done | bytes 655392 | tf_op jit(solution)/shard_map/ppermute | solution.py:251
  265.4 11.1 %collective-permute-done.7.refs_0_ = bf16[512,640]{1,0:T(8,128)(2,1)} collective-permute-done((bf16[512,640]{1,0:T(8,128)(2,1)}, bf16[512,640]{1,0:T(8,128)(2,1)}, u32[]{:S(2)}, u32[]{:S(2)}) %collective-permute-start.7) | collective-permute-done | bytes 655392 | tf_op jit(solution)/shard_map/ppermute | solution.py:251
  276.5 1.9 place.16
  278.4 3.3 %place.10.refs_2_ = bf16[2048,2560]{1,0:T(8,128)(2,1)} custom-call(s32[1]{0:T(128)} %bitcast.me_ref, bf16[2048,640]{1,0:T(8,128)(2,1)} %copy-done, bf16[2048,2560]{1,0:T(8,128)(2,1)} %get-tuple-element.9.refs_1_), custom_call_target="tpu_custom_call", output_to_operand_aliasing={{}: (2, {})} | custom-call | flops 1310720 | bytes 5242880 | tf_op jit(solution)/shard_map/place/pallas_call | solution.py:122
  281.7 3.3 %place.11.refs_2_ = bf16[2048,2560]{1,0:T(8,128)(2,1)} custom-call(s32[1]{0:T(128)} %bitcast.me_ref, bf16[2048,640]{1,0:T(8,128)(2,1)} %collective-permute-done.4.refs_0_, bf16[2048,640]{1,0:T(8,128)(2,1)} %collective-permute-done.3.refs_1_, bf16[2048,2560]{1,0:T(8,128)(2,1)} %place.10.refs_2_), custom_call_target="tpu_custom_call", output_to_operand_aliasing={{}: (3, {})} | custom-call | flops 1310720 | bytes 5242880 | tf_op jit(solution)/shard_map/place/pallas_call | solution.py:122
  285.0 3.3 %place.12 = bf16[2048,2560]{1,0:T(8,128)(2,1)} custom-call(s32[1]{0:T(128)} %bitcast.me_ref, bf16[2048,640]{1,0:T(8,128)(2,1)} %collective-permute-done.2.refs_0_, bf16[2048,640]{1,0:T(8,128)(2,1)} %collective-permute-done.1.refs_1_, bf16[2048,2560]{1,0:T(8,128)(2,1)} %place.11.refs_2_), custom_call_target="tpu_custom_call", output_to_operand_aliasing={{}: (3, {})} | custom-call | flops 1310720 | bytes 5242880 | tf_op jit(solution)/shard_map/place/pallas_call | solution.py:122
  (38 shorter events, 7.8 us)
Async XLA Ops:
  0.6 75.7 %copy-start.5 = (f32[320]{0:T(512)S(1)}, f32[320]{0:T(512)}, u32[]{:S(2)}) copy-start(f32[320]{0:T(512)} %param.20) | copy-start | bytes 3844
  0.6 75.7 %copy-start.6 = (f32[320]{0:T(512)S(1)}, f32[320]{0:T(512)}, u32[]{:S(2)}) copy-start(f32[320]{0:T(512)} %param.21) | copy-start | bytes 3844
  5.9 60.1 %collective-permute-start = (bf16[2048,640]{1,0:T(8,128)(2,1)}, bf16[2048,640]{1,0:T(8,128)(2,1)S(1)}, u32[]{:S(2)}, u32[]{:S(2)}) collective-permute-start(bf16[2048,640]{1,0:T(8,128)(2,1)} %get-tuple-element.8), channel_id=1, source_target_pairs={{0,2},{2,0},{4,6},{6,4},{1,3},{3,1},{5,7},{7,5},{8,10},{10,8},{12,... | collective-permute-start | bytes 7864328 | tf_op jit(solution)/shard_map/ppermute | solution.py:251
  9.0 64.8 %collective-permute-start.3 = (bf16[2048,640]{1,0:T(8,128)(2,1)}, bf16[2048,640]{1,0:T(8,128)(2,1)}, u32[]{:S(2)}, u32[]{:S(2)}) collective-permute-start(bf16[2048,640]{1,0:T(8,128)(2,1)} %get-tuple-element.8), channel_id=1, source_target_pairs={{2,4},{4,2},{3,5},{5,3},{10,12},{12,10},{11,13},{13,11},{18,20},{2... | collective-permute-start | bytes 7864328 | tf_op jit(solution)/shard_map/ppermute | solution.py:251
  66.0 134.1 %copy-start = (bf16[2048,640]{1,0:T(8,128)(2,1)}, bf16[2048,640]{1,0:T(8,128)(2,1)S(1)}, u32[]{:S(2)}) copy-start(bf16[2048,640]{1,0:T(8,128)(2,1)S(1)} %collective-permute-done.refs_0_) | copy-start | bytes 7864324
  66.0 9.0 %collective-permute-start.1 = (bf16[2048,640]{1,0:T(8,128)(2,1)S(1)}, bf16[2048,640]{1,0:T(8,128)(2,1)}, u32[]{:S(2)}, u32[]{:S(2)}) collective-permute-start(bf16[2048,640]{1,0:T(8,128)(2,1)S(1)} %collective-permute-done.refs_0_), channel_id=1, source_target_pairs={{2,4},{4,2},{3,5},{5,3},{10,12},{12,10},{11,13},{13,11},{18,20},{2... | collective-permute-start | bytes 7864328 | tf_op jit(solution)/shard_map/ppermute | solution.py:251
  70.8 134.8 %collective-permute-start.10 = (bf16[512,640]{1,0:T(8,128)(2,1)}, bf16[512,640]{1,0:T(8,128)(2,1)S(1)}, u32[]{:S(2)}, u32[]{:S(2)}) collective-permute-start(bf16[512,640]{1,0:T(8,128)(2,1)} %get-tuple-element.10), channel_id=1, source_target_pairs={{0,2},{2,0},{4,6},{6,4},{1,3},{3,1},{5,7},{7,5},{8,10},{10,8},{12,... | collective-permute-start | bytes 1966088 | tf_op jit(solution)/shard_map/ppermute | solution.py:251
  73.7 208.0 %collective-permute-start.4 = (bf16[2048,640]{1,0:T(8,128)(2,1)}, bf16[2048,640]{1,0:T(8,128)(2,1)}, u32[]{:S(2)}, u32[]{:S(2)}) collective-permute-start(bf16[2048,640]{1,0:T(8,128)(2,1)} %collective-permute-done.3.refs_1_), channel_id=1, source_target_pairs={{2,0},{4,6},{3,1},{5,7},{10,8},{12,14},{11,9},{13,15},{18,16},{20,... | collective-permute-start | bytes 7864328 | tf_op jit(solution)/shard_map/ppermute | solution.py:251
  75.0 209.9 %collective-permute-start.2 = (bf16[2048,640]{1,0:T(8,128)(2,1)}, bf16[2048,640]{1,0:T(8,128)(2,1)}, u32[]{:S(2)}, u32[]{:S(2)}) collective-permute-start(bf16[2048,640]{1,0:T(8,128)(2,1)} %collective-permute-done.1.refs_1_), channel_id=1, source_target_pairs={{2,0},{4,6},{3,1},{5,7},{10,8},{12,14},{11,9},{13,15},{18,16},{20,... | collective-permute-start | bytes 7864328 | tf_op jit(solution)/shard_map/ppermute | solution.py:251
  76.4 3.6 %collective-permute-start.15 = (bf16[320]{0:T(512)(128)(2,1)S(1)}, bf16[320]{0:T(512)(128)(2,1)S(1)}, u32[]{:S(2)}, u32[]{:S(2)}) collective-permute-start(bf16[320]{0:T(512)(128)(2,1)S(1)} %add_convert_fusion), channel_id=1, source_target_pairs={{0,1},{1,0},{2,3},{3,2},{4,5},{5,4},{6,7},{7,6},{8,9},{9,8},{10,11... | collective-permute-start | bytes 1928 | tf_op jit(solution)/shard_map/ppermute | solution.py:259
  80.1 120.1 %collective-permute-start.16 = (bf16[640]{0:T(1024)(128)(2,1)S(1)}, bf16[640]{0:T(1024)(128)(2,1)S(1)}, u32[]{:S(2)}, u32[]{:S(2)}) collective-permute-start(bf16[640]{0:T(1024)(128)(2,1)S(1)} %pad_maximum_fusion.1), channel_id=1, source_target_pairs={{0,6},{2,0},{4,2},{6,4},{1,7},{3,1},{5,3},{7,5},{8,14},{10,8},{12,... | collective-permute-start | bytes 3848 | tf_op jit(solution)/shard_map/ppermute | solution.py:264
  81.4 120.2 %collective-permute-start.17 = (bf16[640]{0:T(1024)(128)(2,1)S(1)}, bf16[640]{0:T(1024)(128)(2,1)S(1)}, u32[]{:S(2)}, u32[]{:S(2)}) collective-permute-start(bf16[640]{0:T(1024)(128)(2,1)S(1)} %pad_maximum_fusion.1), channel_id=1, source_target_pairs={{0,4},{2,6},{4,0},{6,2},{1,5},{3,7},{5,1},{7,3},{8,12},{10,14},{12... | collective-permute-start | bytes 3848 | tf_op jit(solution)/shard_map/ppermute | solution.py:264
  200.2 5.4 %collective-permute-start.18 = (bf16[640]{0:T(1024)(128)(2,1)S(1)}, bf16[640]{0:T(1024)(128)(2,1)S(1)}, u32[]{:S(2)}, u32[]{:S(2)}) collective-permute-start(bf16[640]{0:T(1024)(128)(2,1)S(1)} %pad_maximum_fusion.1), channel_id=1, source_target_pairs={{0,2},{2,4},{4,6},{6,0},{1,3},{3,5},{5,7},{7,1},{8,10},{10,12},{12... | collective-permute-start | bytes 3848 | tf_op jit(solution)/shard_map/ppermute | solution.py:264
  201.7 5.4 %collective-permute-start.13 = (bf16[512,640]{1,0:T(8,128)(2,1)}, bf16[512,640]{1,0:T(8,128)(2,1)S(1)}, u32[]{:S(2)}, u32[]{:S(2)}) collective-permute-start(bf16[512,640]{1,0:T(8,128)(2,1)} %get-tuple-element.10), channel_id=1, source_target_pairs={{2,4},{4,2},{3,5},{5,3},{10,12},{12,10},{11,13},{13,11},{18,20},{2... | collective-permute-start | bytes 1966088 | tf_op jit(solution)/shard_map/ppermute | solution.py:251
  205.6 15.3 %collective-permute-start.5 = (bf16[512,640]{1,0:T(8,128)(2,1)S(1)}, bf16[512,640]{1,0:T(8,128)(2,1)S(1)}, u32[]{:S(2)}, u32[]{:S(2)}) collective-permute-start(bf16[512,640]{1,0:T(8,128)(2,1)S(1)} %merge.4.refs_0_), channel_id=1, source_target_pairs={{0,2},{2,0},{4,6},{6,4},{1,3},{3,1},{5,7},{7,5},{8,10},{10,8},{12,... | collective-permute-start | bytes 1966088 | tf_op jit(solution)/shard_map/ppermute | solution.py:251
  205.6 33.3 %copy-start.1 = (bf16[512,640]{1,0:T(8,128)(2,1)}, bf16[512,640]{1,0:T(8,128)(2,1)S(1)}, u32[]{:S(2)}) copy-start(bf16[512,640]{1,0:T(8,128)(2,1)S(1)} %collective-permute-done.10.refs_0_) | copy-start | bytes 1966084
  205.6 16.0 %collective-permute-start.8 = (bf16[512,640]{1,0:T(8,128)(2,1)S(1)}, bf16[512,640]{1,0:T(8,128)(2,1)}, u32[]{:S(2)}, u32[]{:S(2)}) collective-permute-start(bf16[512,640]{1,0:T(8,128)(2,1)S(1)} %merge.4.refs_0_), channel_id=1, source_target_pairs={{2,4},{4,2},{3,5},{5,3},{10,12},{12,10},{11,13},{13,11},{18,20},{2... | collective-permute-start | bytes 1966088 | tf_op jit(solution)/shard_map/ppermute | solution.py:251
  207.1 27.6 %copy-start.3 = (bf16[512,640]{1,0:T(8,128)(2,1)}, bf16[512,640]{1,0:T(8,128)(2,1)S(1)}, u32[]{:S(2)}) copy-start(bf16[512,640]{1,0:T(8,128)(2,1)S(1)} %collective-permute-done.13.refs_1_) | copy-start | bytes 1966084
  207.1 26.3 %collective-permute-start.14 = (bf16[512,640]{1,0:T(8,128)(2,1)S(1)}, bf16[512,640]{1,0:T(8,128)(2,1)S(1)}, u32[]{:S(2)}, u32[]{:S(2)}) collective-permute-start(bf16[512,640]{1,0:T(8,128)(2,1)S(1)} %collective-permute-done.13.refs_1_), channel_id=1, source_target_pairs={{2,0},{4,6},{3,1},{5,7},{10,8},{12,14},{11,9},{13,15},{18,16},{20,... | collective-permute-start | bytes 1966088 | tf_op jit(solution)/shard_map/ppermute | solution.py:251
  220.9 19.9 %copy-start.2 = (bf16[512,640]{1,0:T(8,128)(2,1)}, bf16[512,640]{1,0:T(8,128)(2,1)S(1)}, u32[]{:S(2)}) copy-start(bf16[512,640]{1,0:T(8,128)(2,1)S(1)} %collective-permute-done.5.refs_0_) | copy-start | bytes 1966084
  220.9 13.7 %collective-permute-start.11 = (bf16[512,640]{1,0:T(8,128)(2,1)S(1)}, bf16[512,640]{1,0:T(8,128)(2,1)S(1)}, u32[]{:S(2)}, u32[]{:S(2)}) collective-permute-start(bf16[512,640]{1,0:T(8,128)(2,1)S(1)} %collective-permute-done.10.refs_0_), channel_id=1, source_target_pairs={{2,4},{4,2},{3,5},{5,3},{10,12},{12,10},{11,13},{13,11},{18,20},{2... | collective-permute-start | bytes 1966088 | tf_op jit(solution)/shard_map/ppermute | solution.py:251
  221.6 14.3 %collective-permute-start.6 = (bf16[512,640]{1,0:T(8,128)(2,1)S(1)}, bf16[512,640]{1,0:T(8,128)(2,1)}, u32[]{:S(2)}, u32[]{:S(2)}) collective-permute-start(bf16[512,640]{1,0:T(8,128)(2,1)S(1)} %collective-permute-done.5.refs_0_), channel_id=1, source_target_pairs={{2,4},{4,2},{3,5},{5,3},{10,12},{12,10},{11,13},{13,11},{18,20},{2... | collective-permute-start | bytes 1966088 | tf_op jit(solution)/shard_map/ppermute | solution.py:251
  233.4 2.6 copy-start.4
  233.4 17.5 %collective-permute-start.9 = (bf16[512,640]{1,0:T(8,128)(2,1)}, bf16[512,640]{1,0:T(8,128)(2,1)}, u32[]{:S(2)}, u32[]{:S(2)}) collective-permute-start(bf16[512,640]{1,0:T(8,128)(2,1)} %collective-permute-done.8.refs_1_), channel_id=1, source_target_pairs={{2,0},{4,6},{3,1},{5,7},{10,8},{12,14},{11,9},{13,15},{18,16},{20,... | collective-permute-start | bytes 1966088 | tf_op jit(solution)/shard_map/ppermute | solution.py:251
  234.7 29.8 %collective-permute-start.12 = (bf16[512,640]{1,0:T(8,128)(2,1)S(1)}, bf16[512,640]{1,0:T(8,128)(2,1)S(1)}, u32[]{:S(2)}, u32[]{:S(2)}) collective-permute-start(bf16[512,640]{1,0:T(8,128)(2,1)S(1)} %collective-permute-done.11.refs_1_), channel_id=1, source_target_pairs={{2,0},{4,6},{3,1},{5,7},{10,8},{12,14},{11,9},{13,15},{18,16},{20,... | collective-permute-start | bytes 1966088 | tf_op jit(solution)/shard_map/ppermute | solution.py:251
  236.0 40.5 %collective-permute-start.7 = (bf16[512,640]{1,0:T(8,128)(2,1)}, bf16[512,640]{1,0:T(8,128)(2,1)}, u32[]{:S(2)}, u32[]{:S(2)}) collective-permute-start(bf16[512,640]{1,0:T(8,128)(2,1)} %collective-permute-done.6.refs_1_), channel_id=1, source_target_pairs={{2,0},{4,6},{3,1},{5,7},{10,8},{12,14},{11,9},{13,15},{18,16},{20,... | collective-permute-start | bytes 1966088 | tf_op jit(solution)/shard_map/ppermute | solution.py:251

commit v5 on v4

--- a/solution.py
+++ b/solution.py
@@ -12,6 +12,7 @@
 
 KEY, QUERY, VALUE = range(3)
 FIRST, LAST, NORM = KEY, VALUE, None
+LEAD, REST = "lead", "rest"
 
 
 def merged(weight_ref, low_ref, high_ref):
@@ -22,8 +23,18 @@
     return fresh.astype(jnp.bfloat16)
 
 
-def first_kernel(weight_ref, low_ref, high_ref, chunk_ref):
-    chunk_ref[...] = merged(weight_ref, low_ref, high_ref)
+def first_kernel(start, weight_ref, low_ref, high_ref, chunk_ref, weight, low, high, sem):
+    columns = pl.ds(start, chunk_ref.shape[0])
+    copies = [
+        pltpu.make_async_copy(weight_ref.at[:, columns], weight, sem.at[0]),
+        pltpu.make_async_copy(low_ref, low, sem.at[1]),
+        pltpu.make_async_copy(high_ref.at[:, columns], high, sem.at[2]),
+    ]
+    for copy in copies:
+        copy.start()
+    for copy in copies:
+        copy.wait()
+    chunk_ref[...] = merged(weight, low, high)
 
 
 def merge_kernel(me_ref, weight_ref, low_ref, high_ref, chunk_ref, out_ref):
@@ -38,13 +49,20 @@
     )
 
 
-def merge_first(weight, low_t, high):
-    depth, columns = weight.shape
-    rank = high.shape[0]
+def merge_first(weight, low_t, high, start, rows):
+    depth, rank = weight.shape[0], high.shape[0]
     return pl.pallas_call(
-        first_kernel,
-        out_shape=pltpu.VMEM((columns, depth), jnp.bfloat16),
-        cost_estimate=cost(columns, depth, rank),
+        functools.partial(first_kernel, start),
+        in_specs=[pl.BlockSpec(memory_space=pl.ANY)] * 3,
+        out_specs=pl.BlockSpec(memory_space=pltpu.VMEM),
+        out_shape=pltpu.VMEM((rows, depth), jnp.bfloat16),
+        scratch_shapes=[
+            pltpu.VMEM((depth, rows), jnp.bfloat16),
+            pltpu.VMEM((rank, depth), jnp.bfloat16),
+            pltpu.VMEM((rank, rows), jnp.bfloat16),
+            pltpu.SemaphoreType.DMA((3,)),
+        ],
+        cost_estimate=cost(rows, depth, rank),
         name="merge",
     )(weight, low_t, high)
 
@@ -52,9 +70,7 @@
 def merge(me, weight, low_t, high, total):
     depth, columns = weight.shape
     rank = high.shape[0]
-    block = next(b for b in (512, 256, 128) if columns % b == 0)
-    if columns == block and block > 128:
-        block //= 2
+    block = next(b for b in (512, 256, 128) if columns % (2 * b) == 0)
     return pl.pallas_call(
         merge_kernel,
         grid_spec=pltpu.PrefetchScalarGridSpec(
@@ -152,9 +168,10 @@
         return [("hop", pair, chunk) for pair in pairs if hop_pairs(n, *pair)]
 
     steps = []
-    for chunk in (FIRST, QUERY):
+    for chunk in (LEAD, REST, QUERY):
         steps.append(("merge", None, chunk))
         steps += hops(chunk, (1, 0))
+    steps.append(("join", None, FIRST))
     steps += hops(FIRST, (1, 1)) + hops(QUERY, (1, 1))
     steps.append(("place", ((0, 0),), FIRST))
     steps.append(("merge", None, LAST))
@@ -220,7 +237,7 @@
         norm_step,
     ):
         depth = weight_query.shape[0]
-        if depth % 128 or any(w.shape[1] % 128 for w in (weight_query, weight_key, weight_value)):
+        if depth % 128 or any(w.shape[1] % 256 for w in (weight_query, weight_key, weight_value)):
             arrays = (
                 (weight_query, low_query, high_query),
                 (weight_key, low_key, high_key),
@@ -239,12 +256,20 @@
         got = {}
         for what, hop, chunk in steps:
             if what == "merge":
-                if chunk == FIRST:
-                    piece = merge_first(*inputs[chunk])
-                    outs[chunk] = jax.ShapeDtypeStruct((piece.shape[0], depth * n), piece.dtype)
+                if chunk in (LEAD, REST):
+                    rows = inputs[FIRST][0].shape[1]
+                    lead = rows // 2
+                    part = (0, lead) if chunk == LEAD else (lead, rows - lead)
+                    piece = merge_first(*inputs[FIRST], *part)
+                    outs[FIRST] = jax.ShapeDtypeStruct((rows, depth * n), piece.dtype)
                 else:
                     piece, outs[chunk] = merge(me_ref, *inputs[chunk], depth * n)
                 got[(0, 0), chunk] = got[(0, 1), chunk] = piece
+            elif what == "join":
+                for pair in ((0, 0), (0, 1), (1, 0)):
+                    if (pair, LEAD) in got:
+                        parts = [got[pair, LEAD], got[pair, REST]]
+                        got[pair, FIRST] = jnp.concatenate(parts)
             elif what == "hop":
                 r, parity = hop
                 held = got[(r - 1, 1 - parity), chunk]

time: 289 us -> 305 us (1.055)
  waiting for transfers between devices: 176 us -> 186 us
  starting transfers between devices: 79.7 us -> 83.3 us
    ppermute x15 -> x16, starting transfers between devices: 22.6 us -> 79.1 us  [on_device(): got[hop, chunk] = lax.ppermute(held, 'shard', hop_pairs(n, r, parity))]
    ppermute x3, starting transfers between devices: 55.5 us -> 2.47 us  [on_device(): lax.ppermute(rows[0], 'shard', [(j, (j + hop) % n) for j in range(n)])]
    ppermute x15 -> x16, waiting for transfers between devices: 107 us -> 117 us  [on_device(): got[hop, chunk] = lax.ppermute(held, 'shard', hop_pairs(n, r, parity))]
  transfers between devices with their start and end apart: 19 -> 20, of which waited for: 9 -> 9; matrix products, arithmetic and copies ran while one was open for 0% -> 0% of each run, Pallas kernels for 8% -> 8%
where the time goes in v5:
time: 305 us; the launch traced here: 304 us
  waiting for transfers between devices  186 us (61%)
  starting transfers between devices  83.3 us (27%)
  Pallas kernels  31.5 us (10%)
    ppermute x16, waiting for transfers between devices, on_device(): got[hop, chunk] = lax.ppermute(held, 'shard', hop_pairs(n, r, parity))  117 us
    ppermute x16, starting transfers between devices, on_device(): got[hop, chunk] = lax.ppermute(held, 'shard', hop_pairs(n, r, parity))  79.1 us
    ppermute x3, waiting for transfers between devices, on_device(): lax.ppermute(rows[0], 'shard', [(j, (j + hop) % n) for j in range(n)])  68.8 us
    pallas_call x10, Pallas kernels, place(): pl.pallas_call(functools.partial(place_kernel, n, hops, staged), grid_spe...  21.2 us
    pallas_call x2, Pallas kernels, merge(): pl.pallas_call(merge_kernel, grid_spec=pltpu.PrefetchScalarGridSpec(num_s...  7.71 us
  transfers between devices with their start and end apart: 20, of which 9 were waited for; matrix products, arithmetic and copies ran while one was open for 0% of the time, Pallas kernels for 8%

profile of v5, /device:TPU:0, one launch (start us, length us, event | category | flops | bytes accessed | tf_op | source)
XLA Modules:
  0.0 304.5 jit_solution(296494036732254337)
XLA Ops:
  0.7 5.2 %merge.4 = (bf16[2048,640]{1,0:T(8,128)(2,1)}, bf16[2048,2560]{1,0:T(8,128)(2,1)}) custom-call(s32[1]{0:T(128)} %bitcast.me_ref, bf16[640,2048]{1,0:T(8,128)(2,1)} %weight_ref.4, bf16[64,640]{1,0:T(8,128)(2,1)} %bitcast.6, bf16[64,2048]{1,0:T(8,128)(2,1)} %high_ref.4), custom_call_target="tpu_custom_call" | custom-call | flops 167772160 | bytes 7864320 | tf_op jit(solution)/shard_map/merge/pallas_call | solution.py:74
  5.9 3.1 %collective-permute-start = (bf16[2048,640]{1,0:T(8,128)(2,1)}, bf16[2048,640]{1,0:T(8,128)(2,1)S(1)}, u32[]{:S(2)}, u32[]{:S(2)}) collective-permute-start(bf16[2048,640]{1,0:T(8,128)(2,1)} %get-tuple-element.8), channel_id=1, source_target_pairs={{0,2},{2,0},{4,6},{6,4},{1,3},{3,1},{5,7},{7,5},{8,10},{10,8},{12,... | collective-permute-start | bytes 7864328 | tf_op jit(solution)/shard_map/ppermute | solution.py:276
  9.0 2.2 collective-permute-start.3
  11.1 54.9 %collective-permute-done.refs_0_ = bf16[2048,640]{1,0:T(8,128)(2,1)S(1)} collective-permute-done((bf16[2048,640]{1,0:T(8,128)(2,1)}, bf16[2048,640]{1,0:T(8,128)(2,1)S(1)}, u32[]{:S(2)}, u32[]{:S(2)}) %collective-permute-start) | collective-permute-done | bytes 2621472 | tf_op jit(solution)/shard_map/ppermute | solution.py:276
  66.0 1.6 copy-done
  67.6 2.2 collective-permute-start.1
  71.1 1.3 collective-permute-start.2
  72.4 1.8 collective-permute-start.16
  74.2 1.3 merge.5
  75.5 59.5 %collective-permute-start.5 = (bf16[256,640]{1,0:T(8,128)(2,1)S(1)}, bf16[256,640]{1,0:T(8,128)(2,1)S(1)}, u32[]{:S(2)}, u32[]{:S(2)}) collective-permute-start(bf16[256,640]{1,0:T(8,128)(2,1)S(1)} %merge.5), channel_id=1, source_target_pairs={{0,2},{2,0},{4,6},{6,4},{1,3},{3,1},{5,7},{7,5},{8,10},{10,8},{12,... | collective-permute-start | bytes 983048 | tf_op jit(solution)/shard_map/ppermute | solution.py:276
  135.0 1.3 merge.6
  136.5 2.5 collective-permute-start.17
  139.0 61.5 %collective-permute-done.17 = bf16[640]{0:T(1024)(128)(2,1)S(1)} collective-permute-done((bf16[640]{0:T(1024)(128)(2,1)S(1)}, bf16[640]{0:T(1024)(128)(2,1)S(1)}, u32[]{:S(2)}, u32[]{:S(2)}) %collective-permute-start.17) | collective-permute-done | bytes 1312 | tf_op jit(solution)/shard_map/ppermute | solution.py:289
  200.5 4.4 %collective-permute-done.18 = bf16[640]{0:T(1024)(128)(2,1)S(1)} collective-permute-done((bf16[640]{0:T(1024)(128)(2,1)S(1)}, bf16[640]{0:T(1024)(128)(2,1)S(1)}, u32[]{:S(2)}, u32[]{:S(2)}) %collective-permute-start.18) | collective-permute-done | bytes 1312 | tf_op jit(solution)/shard_map/ppermute | solution.py:289
  204.9 2.5 merge.7
  207.4 2.9 collective-permute-done.19
  211.0 1.5 collective-permute-start.9
  212.7 10.3 %collective-permute-done.11.refs_0_ = bf16[512,640]{1,0:T(8,128)(2,1)S(1)} collective-permute-done((bf16[512,640]{1,0:T(8,128)(2,1)}, bf16[512,640]{1,0:T(8,128)(2,1)S(1)}, u32[]{:S(2)}, u32[]{:S(2)}) %collective-permute-start.11) | collective-permute-done | bytes 655392 | tf_op jit(solution)/shard_map/ppermute | solution.py:276
  223.0 1.5 collective-permute-start.7
  226.5 1.3 collective-permute-start.10
  227.8 14.1 %collective-permute-done.15.refs_0_ = bf16[512,640]{1,0:T(8,128)(2,1)S(1)} collective-permute-done((bf16[512,640]{1,0:T(8,128)(2,1)S(1)}, bf16[512,640]{1,0:T(8,128)(2,1)S(1)}, u32[]{:S(2)}, u32[]{:S(2)}) %collective-permute-start.15) | collective-permute-done | bytes 655392 | tf_op jit(solution)/shard_map/ppermute | solution.py:276
  246.1 1.9 place.17.refs_2_
  248.0 1.9 place.14.refs_2_
  250.0 1.9 place.18.refs_2_
  251.9 25.5 %collective-permute-done.10.refs_0_ = bf16[512,640]{1,0:T(8,128)(2,1)} collective-permute-done((bf16[512,640]{1,0:T(8,128)(2,1)}, bf16[512,640]{1,0:T(8,128)(2,1)}, u32[]{:S(2)}, u32[]{:S(2)}) %collective-permute-start.10) | collective-permute-done | bytes 655392 | tf_op jit(solution)/shard_map/ppermute | solution.py:276
  277.4 1.9 place.15.refs_2_
  279.4 7.5 %collective-permute-done.8.refs_0_ = bf16[512,640]{1,0:T(8,128)(2,1)} collective-permute-done((bf16[512,640]{1,0:T(8,128)(2,1)}, bf16[512,640]{1,0:T(8,128)(2,1)}, u32[]{:S(2)}, u32[]{:S(2)}) %collective-permute-start.8) | collective-permute-done | bytes 655392 | tf_op jit(solution)/shard_map/ppermute | solution.py:276
  286.9 1.9 place.16
  288.8 5.0 %collective-permute-done.13.refs_0_ = bf16[512,640]{1,0:T(8,128)(2,1)S(1)} collective-permute-done((bf16[512,640]{1,0:T(8,128)(2,1)S(1)}, bf16[512,640]{1,0:T(8,128)(2,1)S(1)}, u32[]{:S(2)}, u32[]{:S(2)}) %collective-permute-start.13) | collective-permute-done | bytes 655392 | tf_op jit(solution)/shard_map/ppermute | solution.py:276
  294.7 3.3 %place.10.refs_2_ = bf16[2048,2560]{1,0:T(8,128)(2,1)} custom-call(s32[1]{0:T(128)} %bitcast.me_ref, bf16[2048,640]{1,0:T(8,128)(2,1)} %copy-done, bf16[2048,2560]{1,0:T(8,128)(2,1)} %get-tuple-element.9.refs_1_), custom_call_target="tpu_custom_call", output_to_operand_aliasing={{}: (2, {})} | custom-call | flops 1310720 | bytes 5242880 | tf_op jit(solution)/shard_map/place/pallas_call | solution.py:138
  298.0 3.3 %place.11.refs_2_ = bf16[2048,2560]{1,0:T(8,128)(2,1)} custom-call(s32[1]{0:T(128)} %bitcast.me_ref, bf16[2048,640]{1,0:T(8,128)(2,1)} %collective-permute-done.4.refs_0_, bf16[2048,640]{1,0:T(8,128)(2,1)} %collective-permute-done.3.refs_1_, bf16[2048,2560]{1,0:T(8,128)(2,1)} %place.10.refs_2_), custom_call_target="tpu_custom_call", output_to_operand_aliasing={{}: (3, {})} | custom-call | flops 1310720 | bytes 5242880 | tf_op jit(solution)/shard_map/place/pallas_call | solution.py:138
  301.2 3.3 %place.12 = bf16[2048,2560]{1,0:T(8,128)(2,1)} custom-call(s32[1]{0:T(128)} %bitcast.me_ref, bf16[2048,640]{1,0:T(8,128)(2,1)} %collective-permute-done.2.refs_0_, bf16[2048,640]{1,0:T(8,128)(2,1)} %collective-permute-done.1.refs_1_, bf16[2048,2560]{1,0:T(8,128)(2,1)} %place.11.refs_2_), custom_call_target="tpu_custom_call", output_to_operand_aliasing={{}: (3, {})} | custom-call | flops 1310720 | bytes 5242880 | tf_op jit(solution)/shard_map/place/pallas_call | solution.py:138
  (44 shorter events, 9.3 us)
Async XLA Ops:
  0.6 71.8 %copy-start.5 = (f32[320]{0:T(512)S(1)}, f32[320]{0:T(512)}, u32[]{:S(2)}) copy-start(f32[320]{0:T(512)} %param.20) | copy-start | bytes 3844
  0.6 71.8 %copy-start.6 = (f32[320]{0:T(512)S(1)}, f32[320]{0:T(512)}, u32[]{:S(2)}) copy-start(f32[320]{0:T(512)} %param.21) | copy-start | bytes 3844
  5.9 60.1 %collective-permute-start = (bf16[2048,640]{1,0:T(8,128)(2,1)}, bf16[2048,640]{1,0:T(8,128)(2,1)S(1)}, u32[]{:S(2)}, u32[]{:S(2)}) collective-permute-start(bf16[2048,640]{1,0:T(8,128)(2,1)} %get-tuple-element.8), channel_id=1, source_target_pairs={{0,2},{2,0},{4,6},{6,4},{1,3},{3,1},{5,7},{7,5},{8,10},{10,8},{12,... | collective-permute-start | bytes 7864328 | tf_op jit(solution)/shard_map/ppermute | solution.py:276
  9.0 60.8 %collective-permute-start.3 = (bf16[2048,640]{1,0:T(8,128)(2,1)}, bf16[2048,640]{1,0:T(8,128)(2,1)}, u32[]{:S(2)}, u32[]{:S(2)}) collective-permute-start(bf16[2048,640]{1,0:T(8,128)(2,1)} %get-tuple-element.8), channel_id=1, source_target_pairs={{2,4},{4,2},{3,5},{5,3},{10,12},{12,10},{11,13},{13,11},{18,20},{2... | collective-permute-start | bytes 7864328 | tf_op jit(solution)/shard_map/ppermute | solution.py:276
  66.0 1.6 copy-start
  67.6 3.5 %collective-permute-start.1 = (bf16[2048,640]{1,0:T(8,128)(2,1)S(1)}, bf16[2048,640]{1,0:T(8,128)(2,1)}, u32[]{:S(2)}, u32[]{:S(2)}) collective-permute-start(bf16[2048,640]{1,0:T(8,128)(2,1)S(1)} %collective-permute-done.refs_0_), channel_id=1, source_target_pairs={{2,4},{4,2},{3,5},{5,3},{10,12},{12,10},{11,13},{13,11},{18,20},{2... | collective-permute-start | bytes 7864328 | tf_op jit(solution)/shard_map/ppermute | solution.py:276
  69.8 228.2 %collective-permute-start.4 = (bf16[2048,640]{1,0:T(8,128)(2,1)}, bf16[2048,640]{1,0:T(8,128)(2,1)}, u32[]{:S(2)}, u32[]{:S(2)}) collective-permute-start(bf16[2048,640]{1,0:T(8,128)(2,1)} %collective-permute-done.3.refs_1_), channel_id=1, source_target_pairs={{2,0},{4,6},{3,1},{5,7},{10,8},{12,14},{11,9},{13,15},{18,16},{20,... | collective-permute-start | bytes 7864328 | tf_op jit(solution)/shard_map/ppermute | solution.py:276
  71.1 230.1 %collective-permute-start.2 = (bf16[2048,640]{1,0:T(8,128)(2,1)}, bf16[2048,640]{1,0:T(8,128)(2,1)}, u32[]{:S(2)}, u32[]{:S(2)}) collective-permute-start(bf16[2048,640]{1,0:T(8,128)(2,1)} %collective-permute-done.1.refs_1_), channel_id=1, source_target_pairs={{2,0},{4,6},{3,1},{5,7},{10,8},{12,14},{11,9},{13,15},{18,16},{20,... | collective-permute-start | bytes 7864328 | tf_op jit(solution)/shard_map/ppermute | solution.py:276
  72.4 64.0 %collective-permute-start.16 = (bf16[320]{0:T(512)(128)(2,1)S(1)}, bf16[320]{0:T(512)(128)(2,1)S(1)}, u32[]{:S(2)}, u32[]{:S(2)}) collective-permute-start(bf16[320]{0:T(512)(128)(2,1)S(1)} %add_convert_fusion), channel_id=1, source_target_pairs={{0,1},{1,0},{2,3},{3,2},{4,5},{5,4},{6,7},{7,6},{8,9},{9,8},{10,11... | collective-permute-start | bytes 1928 | tf_op jit(solution)/shard_map/ppermute | solution.py:284
  75.5 134.9 %collective-permute-start.5 = (bf16[256,640]{1,0:T(8,128)(2,1)S(1)}, bf16[256,640]{1,0:T(8,128)(2,1)S(1)}, u32[]{:S(2)}, u32[]{:S(2)}) collective-permute-start(bf16[256,640]{1,0:T(8,128)(2,1)S(1)} %merge.5), channel_id=1, source_target_pairs={{0,2},{2,0},{4,6},{6,4},{1,3},{3,1},{5,7},{7,5},{8,10},{10,8},{12,... | collective-permute-start | bytes 983048 | tf_op jit(solution)/shard_map/ppermute | solution.py:276
  136.3 74.7 %collective-permute-start.6 = (bf16[256,640]{1,0:T(8,128)(2,1)S(1)}, bf16[256,640]{1,0:T(8,128)(2,1)S(1)}, u32[]{:S(2)}, u32[]{:S(2)}) collective-permute-start(bf16[256,640]{1,0:T(8,128)(2,1)S(1)} %merge.6), channel_id=1, source_target_pairs={{0,2},{2,0},{4,6},{6,4},{1,3},{3,1},{5,7},{7,5},{8,10},{10,8},{12,... | collective-permute-start | bytes 983048 | tf_op jit(solution)/shard_map/ppermute | solution.py:276
  136.5 63.9 %collective-permute-start.17 = (bf16[640]{0:T(1024)(128)(2,1)S(1)}, bf16[640]{0:T(1024)(128)(2,1)S(1)}, u32[]{:S(2)}, u32[]{:S(2)}) collective-permute-start(bf16[640]{0:T(1024)(128)(2,1)S(1)} %pad_maximum_fusion.2), channel_id=1, source_target_pairs={{0,6},{2,0},{4,2},{6,4},{1,7},{3,1},{5,3},{7,5},{8,14},{10,8},{12,... | collective-permute-start | bytes 3848 | tf_op jit(solution)/shard_map/ppermute | solution.py:289
  200.4 4.5 %collective-permute-start.18 = (bf16[640]{0:T(1024)(128)(2,1)S(1)}, bf16[640]{0:T(1024)(128)(2,1)S(1)}, u32[]{:S(2)}, u32[]{:S(2)}) collective-permute-start(bf16[640]{0:T(1024)(128)(2,1)S(1)} %pad_maximum_fusion.2), channel_id=1, source_target_pairs={{0,4},{2,6},{4,0},{6,2},{1,5},{3,7},{5,1},{7,3},{8,12},{10,14},{12... | collective-permute-start | bytes 3848 | tf_op jit(solution)/shard_map/ppermute | solution.py:289
  204.9 5.4 %collective-permute-start.19 = (bf16[640]{0:T(1024)(128)(2,1)S(1)}, bf16[640]{0:T(1024)(128)(2,1)S(1)}, u32[]{:S(2)}, u32[]{:S(2)}) collective-permute-start(bf16[640]{0:T(1024)(128)(2,1)S(1)} %pad_maximum_fusion.2), channel_id=1, source_target_pairs={{0,2},{2,4},{4,6},{6,0},{1,3},{3,5},{5,7},{7,1},{8,10},{10,12},{12... | collective-permute-start | bytes 3848 | tf_op jit(solution)/shard_map/ppermute | solution.py:289
  210.3 12.6 %collective-permute-start.11 = (bf16[512,640]{1,0:T(8,128)(2,1)}, bf16[512,640]{1,0:T(8,128)(2,1)S(1)}, u32[]{:S(2)}, u32[]{:S(2)}) collective-permute-start(bf16[512,640]{1,0:T(8,128)(2,1)} %get-tuple-element.10), channel_id=1, source_target_pairs={{0,2},{2,0},{4,6},{6,4},{1,3},{3,1},{5,7},{7,5},{8,10},{10,8},{12,... | collective-permute-start | bytes 1966088 | tf_op jit(solution)/shard_map/ppermute | solution.py:276
  210.3 14.1 %collective-permute-start.14 = (bf16[512,640]{1,0:T(8,128)(2,1)}, bf16[512,640]{1,0:T(8,128)(2,1)S(1)}, u32[]{:S(2)}, u32[]{:S(2)}) collective-permute-start(bf16[512,640]{1,0:T(8,128)(2,1)} %get-tuple-element.10), channel_id=1, source_target_pairs={{2,4},{4,2},{3,5},{5,3},{10,12},{12,10},{11,13},{13,11},{18,20},{2... | collective-permute-start | bytes 1966088 | tf_op jit(solution)/shard_map/ppermute | solution.py:276
  211.0 14.7 %collective-permute-start.9 = (bf16[512,640]{1,0:T(8,128)(2,1)S(1)}, bf16[512,640]{1,0:T(8,128)(2,1)}, u32[]{:S(2)}, u32[]{:S(2)}) collective-permute-start(bf16[512,640]{1,0:T(8,128)(2,1)S(1)} %pad_maximum_fusion.refs_0_), channel_id=1, source_target_pairs={{2,4},{4,2},{3,5},{5,3},{10,12},{12,10},{11,13},{13,11},{18,20},{2... | collective-permute-start | bytes 1966088 | tf_op jit(solution)/shard_map/ppermute | solution.py:276
  212.6 35.4 %copy-start.1 = (bf16[512,640]{1,0:T(8,128)(2,1)}, bf16[512,640]{1,0:T(8,128)(2,1)S(1)}, u32[]{:S(2)}) copy-start(bf16[512,640]{1,0:T(8,128)(2,1)S(1)} %constant_dynamic-update-slice_fusion.refs_0_) | copy-start | bytes 1966084
  222.9 23.1 %copy-start.2 = (bf16[512,640]{1,0:T(8,128)(2,1)}, bf16[512,640]{1,0:T(8,128)(2,1)S(1)}, u32[]{:S(2)}) copy-start(bf16[512,640]{1,0:T(8,128)(2,1)S(1)} %collective-permute-done.11.refs_0_) | copy-start | bytes 1966084
  223.0 3.5 %collective-permute-start.7 = (bf16[512,640]{1,0:T(8,128)(2,1)S(1)}, bf16[512,640]{1,0:T(8,128)(2,1)}, u32[]{:S(2)}, u32[]{:S(2)}) collective-permute-start(bf16[512,640]{1,0:T(8,128)(2,1)S(1)} %constant_dynamic-update-slice_fusion.refs_0_), channel_id=1, source_target_pairs={{2,4},{4,2},{3,5},{5,3},{10,12},{12,10},{11,13},{13,11},{18,20},{2... | collective-permute-start | bytes 1966088 | tf_op jit(solution)/shard_map/ppermute | solution.py:276
  224.4 18.7 %copy-start.3 = (bf16[512,640]{1,0:T(8,128)(2,1)}, bf16[512,640]{1,0:T(8,128)(2,1)S(1)}, u32[]{:S(2)}) copy-start(bf16[512,640]{1,0:T(8,128)(2,1)S(1)} %collective-permute-done.14.refs_1_) | copy-start | bytes 1966084
  224.4 17.4 %collective-permute-start.15 = (bf16[512,640]{1,0:T(8,128)(2,1)S(1)}, bf16[512,640]{1,0:T(8,128)(2,1)S(1)}, u32[]{:S(2)}, u32[]{:S(2)}) collective-permute-start(bf16[512,640]{1,0:T(8,128)(2,1)S(1)} %collective-permute-done.14.refs_1_), channel_id=1, source_target_pairs={{2,0},{4,6},{3,1},{5,7},{10,8},{12,14},{11,9},{13,15},{18,16},{20,... | collective-permute-start | bytes 1966088 | tf_op jit(solution)/shard_map/ppermute | solution.py:276
  225.7 17.4 %collective-permute-start.12 = (bf16[512,640]{1,0:T(8,128)(2,1)S(1)}, bf16[512,640]{1,0:T(8,128)(2,1)S(1)}, u32[]{:S(2)}, u32[]{:S(2)}) collective-permute-start(bf16[512,640]{1,0:T(8,128)(2,1)S(1)} %collective-permute-done.11.refs_0_), channel_id=1, source_target_pairs={{2,4},{4,2},{3,5},{5,3},{10,12},{12,10},{11,13},{13,11},{18,20},{2... | collective-permute-start | bytes 1966088 | tf_op jit(solution)/shard_map/ppermute | solution.py:276
  226.5 50.9 %collective-permute-start.10 = (bf16[512,640]{1,0:T(8,128)(2,1)}, bf16[512,640]{1,0:T(8,128)(2,1)}, u32[]{:S(2)}, u32[]{:S(2)}) collective-permute-start(bf16[512,640]{1,0:T(8,128)(2,1)} %collective-permute-done.9.refs_1_), channel_id=1, source_target_pairs={{2,0},{4,6},{3,1},{5,7},{10,8},{12,14},{11,9},{13,15},{18,16},{20,... | collective-permute-start | bytes 1966088 | tf_op jit(solution)/shard_map/ppermute | solution.py:276
  241.9 1.3 copy-start.4
  241.9 45.0 %collective-permute-start.8 = (bf16[512,640]{1,0:T(8,128)(2,1)}, bf16[512,640]{1,0:T(8,128)(2,1)}, u32[]{:S(2)}, u32[]{:S(2)}) collective-permute-start(bf16[512,640]{1,0:T(8,128)(2,1)} %collective-permute-done.7.refs_1_), channel_id=1, source_target_pairs={{2,0},{4,6},{3,1},{5,7},{10,8},{12,14},{11,9},{13,15},{18,16},{20,... | collective-permute-start | bytes 1966088 | tf_op jit(solution)/shard_map/ppermute | solution.py:276
  243.2 50.6 %collective-permute-start.13 = (bf16[512,640]{1,0:T(8,128)(2,1)S(1)}, bf16[512,640]{1,0:T(8,128)(2,1)S(1)}, u32[]{:S(2)}, u32[]{:S(2)}) collective-permute-start(bf16[512,640]{1,0:T(8,128)(2,1)S(1)} %collective-permute-done.12.refs_1_), channel_id=1, source_target_pairs={{2,0},{4,6},{3,1},{5,7},{10,8},{12,14},{11,9},{13,15},{18,16},{20,... | collective-permute-start | bytes 1966088 | tf_op jit(solution)/shard_map/ppermute | solution.py:276

commit v6 on v4

--- a/solution.py
+++ b/solution.py
@@ -79,9 +79,9 @@
     )(me, weight, low_t, high)
 
 
-def source_of(me, r, parity):
-    down = lax.rem(me + parity, 2) == 0
-    return jnp.where(down, me + r, me - r)
+def source_of(me, n, r, parity):
+    forth = lax.rem(me + parity, 2) == 0
+    return lax.rem(jnp.where(forth, me + r, me + n - r), n)
 
 
 def place_kernel(n, hops, staged, me_ref, *refs):
@@ -89,21 +89,17 @@
     out_ref, sem, stage = refs
 
     for (r, parity), chunk_ref in zip(hops, chunk_refs):
-        source = me_ref[0] if r == 0 else source_of(me_ref[0], r, parity)
-
-        @pl.when((source >= 0) & (source < n))
-        def _():
-            held = chunk_ref
-            if staged:
-                held = stage
-                copy = pltpu.make_async_copy(chunk_ref, held, sem.at[1])
-                copy.start()
-                copy.wait()
-            depth = chunk_ref.shape[1]
-            there = out_ref.at[:, pl.ds(pl.multiple_of(source * depth, 128), depth)]
-            copy = pltpu.make_async_copy(held, there, sem.at[0])
+        held = chunk_ref
+        if staged:
+            held = stage
+            copy = pltpu.make_async_copy(chunk_ref, held, sem.at[1])
             copy.start()
             copy.wait()
+        depth = chunk_ref.shape[1]
+        column = pl.multiple_of(source_of(me_ref[0], n, r, parity) * depth, 128)
+        copy = pltpu.make_async_copy(held, out_ref.at[:, pl.ds(column, depth)], sem.at[0])
+        copy.start()
+        copy.wait()
 
 
 def place(me, n, hops, chunks, out, staged):
@@ -137,41 +133,37 @@
     )(*operands)
 
 
-def hop_pairs(n, r, parity):
+def hops_of(n):
+    return [(1 + i // 2, i % 2) for i in range(n - 1)]
+
+
+def hop_pairs(n, parity):
     pairs = []
-    for i in range(parity, n - 1, 2):
-        if i - r + 1 >= 0:
-            pairs.append((i, i + 1))
-        if i + r <= n - 1:
-            pairs.append((i + 1, i))
+    for i in range(parity, n, 2):
+        j = (i + 1) % n
+        pairs += [(i, j), (j, i)]
     return pairs
 
 
 def steps_of(n):
-    def hops(chunk, *pairs):
-        return [("hop", pair, chunk) for pair in pairs if hop_pairs(n, *pair)]
-
+    hops = hops_of(n)
     steps = []
-    for chunk in (FIRST, QUERY):
+    for chunk in (FIRST, QUERY, LAST):
         steps.append(("merge", None, chunk))
-        steps += hops(chunk, (1, 0))
-    steps += hops(FIRST, (1, 1)) + hops(QUERY, (1, 1))
-    steps.append(("place", ((0, 0),), FIRST))
-    steps.append(("merge", None, LAST))
-    steps += hops(LAST, (1, 0), (1, 1))
+        steps += [("hop", hop, chunk) for hop in hops[:2]]
+        if chunk == QUERY:
+            steps.append(("place", ((0, 0),), FIRST))
     steps.append(("exchange", None, NORM))
     steps += [("shift", k, NORM) for k in range(1, n)]
-    for r in range(2, n + 2):
+    placed = 0
+    end = max(len(hops), 2)
+    for i in range(2, end + 1):
         for chunk in (FIRST, QUERY, LAST):
-            if r == n and chunk == LAST:
+            if i == end and chunk == LAST:
                 steps.append(("norm", None, NORM))
-            steps += hops(chunk, (r, 0), (r, 1))
-            came = tuple(pair for pair in ((r - 1, 0), (r - 2, 1)) if r > 2 or pair[1] == 0)
-            came = tuple(pair for pair in came if hop_pairs(n, *pair))
-            if came:
-                steps.append(("place", came, chunk))
-    if n == 1:
-        steps.append(("norm", None, NORM))
+            steps += [("hop", hop, chunk) for hop in hops[i : i + 1]]
+            steps.append(("place", tuple(hops[placed:i]), chunk))
+        placed = i
     return steps
 
 
@@ -220,7 +212,8 @@
         norm_step,
     ):
         depth = weight_query.shape[0]
-        if depth % 128 or any(w.shape[1] % 128 for w in (weight_query, weight_key, weight_value)):
+        weights = (weight_query, weight_key, weight_value)
+        if n % 2 or depth % 128 or any(weight.shape[1] % 128 for weight in weights):
             arrays = (
                 (weight_query, low_query, high_query),
                 (weight_key, low_key, high_key),
@@ -248,10 +241,11 @@
             elif what == "hop":
                 r, parity = hop
                 held = got[(r - 1, 1 - parity), chunk]
-                got[hop, chunk] = lax.ppermute(held, "shard", hop_pairs(n, r, parity))
+                got[hop, chunk] = lax.ppermute(held, "shard", hop_pairs(n, parity))
             elif what == "place":
                 pieces = [got[pair, chunk] for pair in hop]
-                staged = not (hop[0][0] == 0 or (hop[0][0] >= n - 1 and chunk == LAST))
+                ends = hop[-1] == hops_of(n)[-1] and chunk == LAST
+                staged = not (hop[0] == (0, 0) or ends)
                 outs[chunk] = place(me_ref, n, hop, pieces, outs[chunk], staged)
             elif what == "exchange":
                 share = (norm_train + norm_step).astype(jnp.bfloat16)

time: 289 us -> 281 us (0.972)
  waiting for transfers between devices: 176 us -> 154 us
  starting transfers between devices: 79.7 us -> 94 us
    ppermute x15 -> x9, starting transfers between devices: 22.6 us -> 89.3 us  [on_device(): got[hop, chunk] = lax.ppermute(held, 'shard', hop_pairs(n, parity))]
    ppermute x3, starting transfers between devices: 55.5 us -> 3.11 us  [on_device(): lax.ppermute(rows[0], 'shard', [(j, (j + hop) % n) for j in range(n)])]
    ppermute x3, waiting for transfers between devices: 67.7 us -> 47.9 us  [on_device(): lax.ppermute(rows[0], 'shard', [(j, (j + hop) % n) for j in range(n)])]
    ppermute x15 -> x9, waiting for transfers between devices: 107 us -> 106 us  [on_device(): got[hop, chunk] = lax.ppermute(held, 'shard', hop_pairs(n, parity))]
    pallas_call x10 -> x7, Pallas kernels: 21.2 us -> 21.1 us  [place(): pl.pallas_call(functools.partial(place_kernel, n, hops, staged), grid_spe...]
  transfers between devices with their start and end apart: 19 -> 13, of which waited for: 9 -> 7; matrix products, arithmetic and copies ran while one was open for 0% -> 0% of each run, Pallas kernels for 8% -> 8%
where the time goes in v6:
time: 281 us
  waiting for transfers between devices  154 us (55%)
  starting transfers between devices  94 us (33%)
  Pallas kernels  30.3 us (11%)
    ppermute x9, waiting for transfers between devices, on_device(): got[hop, chunk] = lax.ppermute(held, 'shard', hop_pairs(n, parity))  106 us
    ppermute x9, starting transfers between devices, on_device(): got[hop, chunk] = lax.ppermute(held, 'shard', hop_pairs(n, parity))  89.3 us
    ppermute x3, waiting for transfers between devices, on_device(): lax.ppermute(rows[0], 'shard', [(j, (j + hop) % n) for j in range(n)])  47.9 us
    pallas_call x7, Pallas kernels, place(): pl.pallas_call(functools.partial(place_kernel, n, hops, staged), grid_spe...  21.1 us
    pallas_call x2, Pallas kernels, merge(): pl.pallas_call(merge_kernel, grid_spec=pltpu.PrefetchScalarGridSpec(num_s...  7.69 us
  transfers between devices with their start and end apart: 13, of which 7 were waited for; matrix products, arithmetic and copies ran while one was open for 0% of the time, Pallas kernels for 8%

profile of v6, /device:TPU:0, one launch (start us, length us, event | category | flops | bytes accessed | tf_op | source)
XLA Modules:
  0.0 280.9 jit_solution(15343260621000289097)
XLA Ops:
  0.7 5.2 %merge.3 = (bf16[2048,640]{1,0:T(8,128)(2,1)}, bf16[2048,2560]{1,0:T(8,128)(2,1)}) custom-call(s32[1]{0:T(128)} %bitcast.me_ref, bf16[640,2048]{1,0:T(8,128)(2,1)} %weight_ref.3, bf16[64,640]{1,0:T(8,128)(2,1)} %bitcast.4, bf16[64,2048]{1,0:T(8,128)(2,1)} %high_ref.3), custom_call_target="tpu_custom_call" | custom-call | flops 167772160 | bytes 7864320 | tf_op jit(solution)/shard_map/merge/pallas_call | solution.py:58
  5.9 5.1 %collective-permute-start = (bf16[2048,640]{1,0:T(8,128)(2,1)}, bf16[2048,640]{1,0:T(8,128)(2,1)}, u32[]{:S(2)}, u32[]{:S(2)}) collective-permute-start(bf16[2048,640]{1,0:T(8,128)(2,1)} %get-tuple-element.8), channel_id=1, source_target_pairs={{2,4},{4,2},{6,0},{0,6},{3,5},{5,3},{7,1},{1,7},{10,12},{12,10},{1... | collective-permute-start | bytes 7864328 | tf_op jit(solution)/shard_map/ppermute | solution.py:244
  11.0 0.0 collective-permute-start.2
  11.0 58.1 %collective-permute-done.refs_1_ = bf16[2048,640]{1,0:T(8,128)(2,1)} collective-permute-done((bf16[2048,640]{1,0:T(8,128)(2,1)}, bf16[2048,640]{1,0:T(8,128)(2,1)}, u32[]{:S(2)}, u32[]{:S(2)}) %collective-permute-start) | collective-permute-done | bytes 2621472 | tf_op jit(solution)/shard_map/ppermute | solution.py:244
  69.1 55.0 %collective-permute-start.1 = (bf16[2048,640]{1,0:T(8,128)(2,1)}, bf16[2048,640]{1,0:T(8,128)(2,1)}, u32[]{:S(2)}, u32[]{:S(2)}) collective-permute-start(bf16[2048,640]{1,0:T(8,128)(2,1)} %collective-permute-done.refs_1_), channel_id=1, source_target_pairs={{0,2},{2,0},{4,6},{6,4},{1,3},{3,1},{5,7},{7,5},{8,10},{10,8},{12,... | collective-permute-start | bytes 7864328 | tf_op jit(solution)/shard_map/ppermute | solution.py:244
  124.1 1.6 collective-permute-start.9
  125.7 2.4 merge.5
  128.1 0.0 collective-permute-done.9
  128.1 0.1 pad_maximum_fusion.1
  128.2 2.5 collective-permute-start.10
  130.7 0.6 collective-permute-start.12
  131.3 1.5 merge.4.refs_0_
  132.8 47.9 %collective-permute-done.10 = bf16[640]{0:T(1024)(128)(2,1)S(1)} collective-permute-done((bf16[640]{0:T(1024)(128)(2,1)S(1)}, bf16[640]{0:T(1024)(128)(2,1)S(1)}, u32[]{:S(2)}, u32[]{:S(2)}) %collective-permute-start.10) | collective-permute-done | bytes 1312 | tf_op jit(solution)/shard_map/ppermute | solution.py:258
  180.7 3.4 %collective-permute-start.6 = (bf16[512,640]{1,0:T(8,128)(2,1)}, bf16[512,640]{1,0:T(8,128)(2,1)S(1)}, u32[]{:S(2)}, u32[]{:S(2)}) collective-permute-start(bf16[512,640]{1,0:T(8,128)(2,1)} %get-tuple-element.10), channel_id=1, source_target_pairs={{2,4},{4,2},{6,0},{0,6},{3,5},{5,3},{7,1},{1,7},{10,12},{12,10},{1... | collective-permute-start | bytes 1966088 | tf_op jit(solution)/shard_map/ppermute | solution.py:244
  184.1 0.6 collective-permute-start.3
  184.7 15.7 %collective-permute-done.6.refs_1_ = bf16[512,640]{1,0:T(8,128)(2,1)S(1)} collective-permute-done((bf16[512,640]{1,0:T(8,128)(2,1)}, bf16[512,640]{1,0:T(8,128)(2,1)S(1)}, u32[]{:S(2)}, u32[]{:S(2)}) %collective-permute-start.6) | collective-permute-done | bytes 655392 | tf_op jit(solution)/shard_map/ppermute | solution.py:244
  200.4 14.6 %collective-permute-start.5 = (bf16[512,640]{1,0:T(8,128)(2,1)S(1)}, bf16[512,640]{1,0:T(8,128)(2,1)}, u32[]{:S(2)}, u32[]{:S(2)}) collective-permute-start(bf16[512,640]{1,0:T(8,128)(2,1)S(1)} %merge.4.refs_0_), channel_id=1, source_target_pairs={{0,2},{2,0},{4,6},{6,4},{1,3},{3,1},{5,7},{7,5},{8,10},{10,8},{12,... | collective-permute-start | bytes 1966088 | tf_op jit(solution)/shard_map/ppermute | solution.py:244
  215.0 9.2 %collective-permute-done.8.refs_0_ = bf16[512,640]{1,0:T(8,128)(2,1)} collective-permute-done((bf16[512,640]{1,0:T(8,128)(2,1)}, bf16[512,640]{1,0:T(8,128)(2,1)}, u32[]{:S(2)}, u32[]{:S(2)}) %collective-permute-start.8) | collective-permute-done | bytes 655392 | tf_op jit(solution)/shard_map/ppermute | solution.py:244
  224.2 4.3 %collective-permute-done.3.refs_1_ = bf16[512,640]{1,0:T(8,128)(2,1)S(1)} collective-permute-done((bf16[512,640]{1,0:T(8,128)(2,1)S(1)}, bf16[512,640]{1,0:T(8,128)(2,1)S(1)}, u32[]{:S(2)}, u32[]{:S(2)}) %collective-permute-start.3) | collective-permute-done | bytes 655392 | tf_op jit(solution)/shard_map/ppermute | solution.py:244
  228.5 10.7 %collective-permute-start.4 = (bf16[512,640]{1,0:T(8,128)(2,1)S(1)}, bf16[512,640]{1,0:T(8,128)(2,1)S(1)}, u32[]{:S(2)}, u32[]{:S(2)}) collective-permute-start(bf16[512,640]{1,0:T(8,128)(2,1)S(1)} %collective-permute-done.3.refs_1_), channel_id=1, source_target_pairs={{0,2},{2,0},{4,6},{6,4},{1,3},{3,1},{5,7},{7,5},{8,10},{10,8},{12,... | collective-permute-start | bytes 1966088 | tf_op jit(solution)/shard_map/ppermute | solution.py:244
  239.2 0.9 place.9.refs_2_
  240.0 0.1 select_select_fusion.3
  240.1 0.6 pad_maximum_fusion
  240.7 3.9 %place.12.refs_1_ = bf16[512,2560]{1,0:T(8,128)(2,1)} custom-call(s32[1]{0:T(128)} %bitcast.me_ref, bf16[512,640]{1,0:T(8,128)(2,1)} %collective-permute-done.8.refs_0_, bf16[512,640]{1,0:T(8,128)(2,1)} %copy-done.1, bf16[512,2560]{1,0:T(8,128)(2,1)} %get-tuple-element.11.refs_2_), custom_call_target="tpu_custom_call", output_to_operand_aliasing={{}: (3, {})} | custom-call | flops 327680 | bytes 1310720 | tf_op jit(solution)/shard_map/place/pallas_call | solution.py:118
  244.6 3.9 %place.10.refs_1_ = bf16[512,2560]{1,0:T(8,128)(2,1)} custom-call(s32[1]{0:T(128)} %bitcast.me_ref, bf16[512,640]{1,0:T(8,128)(2,1)} %collective-permute-done.5.refs_0_, bf16[512,640]{1,0:T(8,128)(2,1)} %copy-done.2, bf16[512,2560]{1,0:T(8,128)(2,1)} %place.9.refs_2_), custom_call_target="tpu_custom_call", output_to_operand_aliasing={{}: (3, {})} | custom-call | flops 327680 | bytes 1310720 | tf_op jit(solution)/shard_map/place/pallas_call | solution.py:118
  248.5 7.2 %collective-permute-done.7.refs_0_ = bf16[512,640]{1,0:T(8,128)(2,1)S(1)} collective-permute-done((bf16[512,640]{1,0:T(8,128)(2,1)S(1)}, bf16[512,640]{1,0:T(8,128)(2,1)S(1)}, u32[]{:S(2)}, u32[]{:S(2)}) %collective-permute-start.7) | collective-permute-done | bytes 655392 | tf_op jit(solution)/shard_map/ppermute | solution.py:244
  255.6 0.9 place.13
  256.5 11.8 %collective-permute-done.4.refs_0_ = bf16[512,640]{1,0:T(8,128)(2,1)S(1)} collective-permute-done((bf16[512,640]{1,0:T(8,128)(2,1)S(1)}, bf16[512,640]{1,0:T(8,128)(2,1)S(1)}, u32[]{:S(2)}, u32[]{:S(2)}) %collective-permute-start.4) | collective-permute-done | bytes 655392 | tf_op jit(solution)/shard_map/ppermute | solution.py:244
  268.3 0.9 copy-done
  269.2 1.9 place.11
  271.1 6.5 %place.7.refs_1_ = bf16[2048,2560]{1,0:T(8,128)(2,1)} custom-call(s32[1]{0:T(128)} %bitcast.me_ref, bf16[2048,640]{1,0:T(8,128)(2,1)} %collective-permute-done.2.refs_0_, bf16[2048,640]{1,0:T(8,128)(2,1)} %collective-permute-done.refs_1_, bf16[2048,2560]{1,0:T(8,128)(2,1)} %get-tuple-element.9.refs_2_), custom_call_target="tpu_custom_call", output_to_operand_aliasing={{}: (3, {})} | custom-call | flops 1310720 | bytes 5242880 | tf_op jit(solution)/shard_map/place/pallas_call | solution.py:118
  277.6 3.3 %place.8 = bf16[2048,2560]{1,0:T(8,128)(2,1)} custom-call(s32[1]{0:T(128)} %bitcast.me_ref, bf16[2048,640]{1,0:T(8,128)(2,1)} %collective-permute-done.1.refs_0_, bf16[2048,2560]{1,0:T(8,128)(2,1)} %place.7.refs_1_), custom_call_target="tpu_custom_call", output_to_operand_aliasing={{}: (2, {})} | custom-call | flops 1310720 | bytes 5242880 | tf_op jit(solution)/shard_map/place/pallas_call | solution.py:118
  (19 shorter events, 0.0 us)
Async XLA Ops:
  0.6 123.4 %copy-start.3 = (f32[320]{0:T(512)S(1)}, f32[320]{0:T(512)}, u32[]{:S(2)}) copy-start(f32[320]{0:T(512)} %param.20) | copy-start | bytes 3844
  0.6 123.4 %copy-start.4 = (f32[320]{0:T(512)S(1)}, f32[320]{0:T(512)}, u32[]{:S(2)}) copy-start(f32[320]{0:T(512)} %param.21) | copy-start | bytes 3844
  5.9 63.2 %collective-permute-start = (bf16[2048,640]{1,0:T(8,128)(2,1)}, bf16[2048,640]{1,0:T(8,128)(2,1)}, u32[]{:S(2)}, u32[]{:S(2)}) collective-permute-start(bf16[2048,640]{1,0:T(8,128)(2,1)} %get-tuple-element.8), channel_id=1, source_target_pairs={{2,4},{4,2},{6,0},{0,6},{3,5},{5,3},{7,1},{1,7},{10,12},{12,10},{1... | collective-permute-start | bytes 7864328 | tf_op jit(solution)/shard_map/ppermute | solution.py:244
  11.0 260.1 %collective-permute-start.2 = (bf16[2048,640]{1,0:T(8,128)(2,1)}, bf16[2048,640]{1,0:T(8,128)(2,1)}, u32[]{:S(2)}, u32[]{:S(2)}) collective-permute-start(bf16[2048,640]{1,0:T(8,128)(2,1)} %get-tuple-element.8), channel_id=1, source_target_pairs={{0,2},{2,0},{4,6},{6,4},{1,3},{3,1},{5,7},{7,5},{8,10},{10,8},{12,... | collective-permute-start | bytes 7864328 | tf_op jit(solution)/shard_map/ppermute | solution.py:244
  69.1 208.5 %collective-permute-start.1 = (bf16[2048,640]{1,0:T(8,128)(2,1)}, bf16[2048,640]{1,0:T(8,128)(2,1)}, u32[]{:S(2)}, u32[]{:S(2)}) collective-permute-start(bf16[2048,640]{1,0:T(8,128)(2,1)} %collective-permute-done.refs_1_), channel_id=1, source_target_pairs={{0,2},{2,0},{4,6},{6,4},{1,3},{3,1},{5,7},{7,5},{8,10},{10,8},{12,... | collective-permute-start | bytes 7864328 | tf_op jit(solution)/shard_map/ppermute | solution.py:244
  124.1 4.0 %collective-permute-start.9 = (bf16[320]{0:T(512)(128)(2,1)S(1)}, bf16[320]{0:T(512)(128)(2,1)S(1)}, u32[]{:S(2)}, u32[]{:S(2)}) collective-permute-start(bf16[320]{0:T(512)(128)(2,1)S(1)} %add_convert_fusion), channel_id=1, source_target_pairs={{0,1},{1,0},{2,3},{3,2},{4,5},{5,4},{6,7},{7,6},{8,9},{9,8},{10,11... | collective-permute-start | bytes 1928 | tf_op jit(solution)/shard_map/ppermute | solution.py:253
  128.2 52.5 %collective-permute-start.10 = (bf16[640]{0:T(1024)(128)(2,1)S(1)}, bf16[640]{0:T(1024)(128)(2,1)S(1)}, u32[]{:S(2)}, u32[]{:S(2)}) collective-permute-start(bf16[640]{0:T(1024)(128)(2,1)S(1)} %pad_maximum_fusion.1), channel_id=1, source_target_pairs={{0,6},{2,0},{4,2},{6,4},{1,7},{3,1},{5,3},{7,5},{8,14},{10,8},{12,... | collective-permute-start | bytes 3848 | tf_op jit(solution)/shard_map/ppermute | solution.py:258
  130.7 53.4 %collective-permute-start.11 = (bf16[640]{0:T(1024)(128)(2,1)S(1)}, bf16[640]{0:T(1024)(128)(2,1)S(1)}, u32[]{:S(2)}, u32[]{:S(2)}) collective-permute-start(bf16[640]{0:T(1024)(128)(2,1)S(1)} %pad_maximum_fusion.1), channel_id=1, source_target_pairs={{0,4},{2,6},{4,0},{6,2},{1,5},{3,7},{5,1},{7,3},{8,12},{10,14},{12... | collective-permute-start | bytes 3848 | tf_op jit(solution)/shard_map/ppermute | solution.py:258
  130.7 53.4 %collective-permute-start.12 = (bf16[640]{0:T(1024)(128)(2,1)S(1)}, bf16[640]{0:T(1024)(128)(2,1)S(1)}, u32[]{:S(2)}, u32[]{:S(2)}) collective-permute-start(bf16[640]{0:T(1024)(128)(2,1)S(1)} %pad_maximum_fusion.1), channel_id=1, source_target_pairs={{0,2},{2,4},{4,6},{6,0},{1,3},{3,5},{5,7},{7,1},{8,10},{10,12},{12... | collective-permute-start | bytes 3848 | tf_op jit(solution)/shard_map/ppermute | solution.py:258
  180.7 19.7 %collective-permute-start.6 = (bf16[512,640]{1,0:T(8,128)(2,1)}, bf16[512,640]{1,0:T(8,128)(2,1)S(1)}, u32[]{:S(2)}, u32[]{:S(2)}) collective-permute-start(bf16[512,640]{1,0:T(8,128)(2,1)} %get-tuple-element.10), channel_id=1, source_target_pairs={{2,4},{4,2},{6,0},{0,6},{3,5},{5,3},{7,1},{1,7},{10,12},{12,10},{1... | collective-permute-start | bytes 1966088 | tf_op jit(solution)/shard_map/ppermute | solution.py:244
  184.1 40.1 %collective-permute-start.8 = (bf16[512,640]{1,0:T(8,128)(2,1)}, bf16[512,640]{1,0:T(8,128)(2,1)}, u32[]{:S(2)}, u32[]{:S(2)}) collective-permute-start(bf16[512,640]{1,0:T(8,128)(2,1)} %get-tuple-element.10), channel_id=1, source_target_pairs={{0,2},{2,0},{4,6},{6,4},{1,3},{3,1},{5,7},{7,5},{8,10},{10,8},{12,... | collective-permute-start | bytes 1966088 | tf_op jit(solution)/shard_map/ppermute | solution.py:244
  184.1 44.4 %collective-permute-start.3 = (bf16[512,640]{1,0:T(8,128)(2,1)S(1)}, bf16[512,640]{1,0:T(8,128)(2,1)S(1)}, u32[]{:S(2)}, u32[]{:S(2)}) collective-permute-start(bf16[512,640]{1,0:T(8,128)(2,1)S(1)} %merge.4.refs_0_), channel_id=1, source_target_pairs={{2,4},{4,2},{6,0},{0,6},{3,5},{5,3},{7,1},{1,7},{10,12},{12,10},{1... | collective-permute-start | bytes 1966088 | tf_op jit(solution)/shard_map/ppermute | solution.py:244
  200.4 40.4 %copy-start.1 = (bf16[512,640]{1,0:T(8,128)(2,1)}, bf16[512,640]{1,0:T(8,128)(2,1)S(1)}, u32[]{:S(2)}) copy-start(bf16[512,640]{1,0:T(8,128)(2,1)S(1)} %collective-permute-done.6.refs_1_) | copy-start | bytes 1966084
  200.4 44.2 %collective-permute-start.5 = (bf16[512,640]{1,0:T(8,128)(2,1)S(1)}, bf16[512,640]{1,0:T(8,128)(2,1)}, u32[]{:S(2)}, u32[]{:S(2)}) collective-permute-start(bf16[512,640]{1,0:T(8,128)(2,1)S(1)} %merge.4.refs_0_), channel_id=1, source_target_pairs={{0,2},{2,0},{4,6},{6,4},{1,3},{3,1},{5,7},{7,5},{8,10},{10,8},{12,... | collective-permute-start | bytes 1966088 | tf_op jit(solution)/shard_map/ppermute | solution.py:244
  224.2 31.5 %collective-permute-start.7 = (bf16[512,640]{1,0:T(8,128)(2,1)S(1)}, bf16[512,640]{1,0:T(8,128)(2,1)S(1)}, u32[]{:S(2)}, u32[]{:S(2)}) collective-permute-start(bf16[512,640]{1,0:T(8,128)(2,1)S(1)} %collective-permute-done.6.refs_1_), channel_id=1, source_target_pairs={{0,2},{2,0},{4,6},{6,4},{1,3},{3,1},{5,7},{7,5},{8,10},{10,8},{12,... | collective-permute-start | bytes 1966088 | tf_op jit(solution)/shard_map/ppermute | solution.py:244
  228.5 16.1 %copy-start.2 = (bf16[512,640]{1,0:T(8,128)(2,1)}, bf16[512,640]{1,0:T(8,128)(2,1)S(1)}, u32[]{:S(2)}) copy-start(bf16[512,640]{1,0:T(8,128)(2,1)S(1)} %collective-permute-done.3.refs_1_) | copy-start | bytes 1966084
  228.5 39.8 %collective-permute-start.4 = (bf16[512,640]{1,0:T(8,128)(2,1)S(1)}, bf16[512,640]{1,0:T(8,128)(2,1)S(1)}, u32[]{:S(2)}, u32[]{:S(2)}) collective-permute-start(bf16[512,640]{1,0:T(8,128)(2,1)S(1)} %collective-permute-done.3.refs_1_), channel_id=1, source_target_pairs={{0,2},{2,0},{4,6},{6,4},{1,3},{3,1},{5,7},{7,5},{8,10},{10,8},{12,... | collective-permute-start | bytes 1966088 | tf_op jit(solution)/shard_map/ppermute | solution.py:244
  268.3 0.9 copy-start

commit v7 on v6

--- a/solution.py
+++ b/solution.py
@@ -11,7 +11,16 @@
 
 
 KEY, QUERY, VALUE = range(3)
-FIRST, LAST, NORM = KEY, VALUE, None
+EIGHTHS = 8
+LEAD, KEY_REST = (KEY, 0, 4), (KEY, 4, 4)
+QUERY_ALL = (QUERY, 0, 8)
+NORM = None
+VALUE_REST, LAST = (VALUE, 0, 6), (VALUE, 6, 2)
+CHUNKS = (LEAD, KEY_REST, QUERY_ALL, VALUE_REST, LAST)
+
+
+def extent(columns, chunk):
+    return columns * chunk[1] // EIGHTHS, columns * chunk[2] // EIGHTHS
 
 
 def merged(weight_ref, low_ref, high_ref):
@@ -22,11 +31,22 @@
     return fresh.astype(jnp.bfloat16)
 
 
-def first_kernel(weight_ref, low_ref, high_ref, chunk_ref):
-    chunk_ref[...] = merged(weight_ref, low_ref, high_ref)
-
-
-def merge_kernel(me_ref, weight_ref, low_ref, high_ref, chunk_ref, out_ref):
+def first_kernel(start, weight_ref, low_ref, high_ref, chunk_ref, weight, low, high, sem):
+    columns = pl.ds(start, chunk_ref.shape[0])
+    copies = [
+        pltpu.make_async_copy(weight_ref.at[:, columns], weight, sem.at[0]),
+        pltpu.make_async_copy(low_ref, low, sem.at[1]),
+        pltpu.make_async_copy(high_ref.at[:, columns], high, sem.at[2]),
+    ]
+    for copy in copies:
+        copy.start()
+    for copy in copies:
+        copy.wait()
+    chunk_ref[...] = merged(weight, low, high)
+
+
+def merge_kernel(me_ref, weight_ref, low_ref, high_ref, *refs):
+    chunk_ref, out_ref = refs[-2:]
     fresh = merged(weight_ref, low_ref, high_ref)
     chunk_ref[...] = fresh
     out_ref[...] = fresh
@@ -38,45 +58,59 @@
     )
 
 
-def merge_first(weight, low_t, high):
+def merge_first(weight, low_t, high, start, rows):
+    depth, rank = weight.shape[0], high.shape[0]
+    return pl.pallas_call(
+        functools.partial(first_kernel, start),
+        in_specs=[pl.BlockSpec(memory_space=pl.ANY)] * 3,
+        out_specs=pl.BlockSpec(memory_space=pltpu.VMEM),
+        out_shape=pltpu.VMEM((rows, depth), jnp.bfloat16),
+        scratch_shapes=[
+            pltpu.VMEM((depth, rows), jnp.bfloat16),
+            pltpu.VMEM((rank, depth), jnp.bfloat16),
+            pltpu.VMEM((rank, rows), jnp.bfloat16),
+            pltpu.SemaphoreType.DMA((3,)),
+        ],
+        cost_estimate=cost(rows, depth, rank),
+        name="merge",
+    )(weight, low_t, high)
+
+
+def merge(me, weight, low_t, high, chunk, out):
     depth, columns = weight.shape
     rank = high.shape[0]
-    return pl.pallas_call(
-        first_kernel,
-        out_shape=pltpu.VMEM((columns, depth), jnp.bfloat16),
-        cost_estimate=cost(columns, depth, rank),
-        name="merge",
-    )(weight, low_t, high)
-
-
-def merge(me, weight, low_t, high, total):
-    depth, columns = weight.shape
-    rank = high.shape[0]
-    block = next(b for b in (512, 256, 128) if columns % b == 0)
-    if columns == block and block > 128:
-        block //= 2
+    start, rows = extent(columns, chunk)
+    block = next(b for b in (512, 384, 256, 128) if start % b == 0 and rows % b == 0)
+    first = start // block
+    specs = [
+        pl.BlockSpec((depth, block), lambda j, me: (0, first + j)),
+        pl.BlockSpec((rank, depth), lambda j, me: (0, 0)),
+        pl.BlockSpec((rank, block), lambda j, me: (0, first + j)),
+    ]
+    operands, aliases = [me, weight, low_t, high], {}
+    if isinstance(out, jax.Array):
+        specs.append(pl.BlockSpec(memory_space=pl.ANY))
+        operands.append(out)
+        aliases = {4: 1}
     return pl.pallas_call(
         merge_kernel,
         grid_spec=pltpu.PrefetchScalarGridSpec(
             num_scalar_prefetch=1,
-            grid=(columns // block,),
-            in_specs=[
-                pl.BlockSpec((depth, block), lambda j, me: (0, j)),
-                pl.BlockSpec((rank, depth), lambda j, me: (0, 0)),
-                pl.BlockSpec((rank, block), lambda j, me: (0, j)),
-            ],
+            grid=(rows // block,),
+            in_specs=specs,
             out_specs=[
                 pl.BlockSpec((block, depth), lambda j, me: (j, 0)),
-                pl.BlockSpec((block, depth), lambda j, me: (j, me[0])),
+                pl.BlockSpec((block, depth), lambda j, me: (first + j, me[0])),
             ],
         ),
         out_shape=[
-            jax.ShapeDtypeStruct((columns, depth), jnp.bfloat16),
-            jax.ShapeDtypeStruct((columns, total), jnp.bfloat16),
+            jax.ShapeDtypeStruct((rows, depth), jnp.bfloat16),
+            jax.ShapeDtypeStruct(out.shape, jnp.bfloat16),
         ],
-        cost_estimate=cost(columns, depth, rank),
+        input_output_aliases=aliases,
+        cost_estimate=cost(rows, depth, rank),
         name="merge",
-    )(me, weight, low_t, high)
+    )(*operands)
 
 
 def source_of(me, n, r, parity):
@@ -84,7 +118,7 @@
     return lax.rem(jnp.where(forth, me + r, me + n - r), n)
 
 
-def place_kernel(n, hops, staged, me_ref, *refs):
+def place_kernel(n, hops, start, staged, me_ref, *refs):
     chunk_refs, refs = refs[: len(hops)], refs[-3:] if staged else (*refs[-2:], None)
     out_ref, sem, stage = refs
 
@@ -95,14 +129,15 @@
             copy = pltpu.make_async_copy(chunk_ref, held, sem.at[1])
             copy.start()
             copy.wait()
-        depth = chunk_ref.shape[1]
+        rows, depth = chunk_ref.shape
         column = pl.multiple_of(source_of(me_ref[0], n, r, parity) * depth, 128)
-        copy = pltpu.make_async_copy(held, out_ref.at[:, pl.ds(column, depth)], sem.at[0])
+        there = out_ref.at[pl.ds(start, rows), pl.ds(column, depth)]
+        copy = pltpu.make_async_copy(held, there, sem.at[0])
         copy.start()
         copy.wait()
 
 
-def place(me, n, hops, chunks, out, staged):
+def place(me, n, hops, chunks, out, start, staged):
     rows, depth = chunks[0].shape
     scratch = [pltpu.SemaphoreType.DMA((2,))]
     specs = [pl.BlockSpec(memory_space=pl.ANY if staged else pltpu.VMEM)] * len(hops)
@@ -116,7 +151,7 @@
         operands.append(out)
         specs.append(pl.BlockSpec(memory_space=pl.ANY))
     return pl.pallas_call(
-        functools.partial(place_kernel, n, hops, staged),
+        functools.partial(place_kernel, n, hops, start, staged),
         grid_spec=pltpu.PrefetchScalarGridSpec(
             num_scalar_prefetch=1,
             grid=(1,),
@@ -148,17 +183,19 @@
 def steps_of(n):
     hops = hops_of(n)
     steps = []
-    for chunk in (FIRST, QUERY, LAST):
-        steps.append(("merge", None, chunk))
-        steps += [("hop", hop, chunk) for hop in hops[:2]]
-        if chunk == QUERY:
-            steps.append(("place", ((0, 0),), FIRST))
+    for chunk in (LEAD, KEY_REST):
+        steps += [("merge", None, chunk)] + [("hop", hop, chunk) for hop in hops[:1]]
+    steps += [("hop", hop, chunk) for hop in hops[1:2] for chunk in (LEAD, KEY_REST)]
+    for chunk in (QUERY_ALL, VALUE_REST, LAST):
+        steps += [("merge", None, chunk)] + [("hop", hop, chunk) for hop in hops[:2]]
+        if chunk == QUERY_ALL:
+            steps += [("place", ((0, 0),), part) for part in (LEAD, KEY_REST)]
     steps.append(("exchange", None, NORM))
     steps += [("shift", k, NORM) for k in range(1, n)]
     placed = 0
     end = max(len(hops), 2)
     for i in range(2, end + 1):
-        for chunk in (FIRST, QUERY, LAST):
+        for chunk in CHUNKS:
             if i == end and chunk == LAST:
                 steps.append(("norm", None, NORM))
             steps += [("hop", hop, chunk) for hop in hops[i : i + 1]]
@@ -213,7 +250,7 @@
     ):
         depth = weight_query.shape[0]
         weights = (weight_query, weight_key, weight_value)
-        if n % 2 or depth % 128 or any(weight.shape[1] % 128 for weight in weights):
+        if n % 2 or depth % 128 or any(weight.shape[1] % 512 for weight in weights):
             arrays = (
                 (weight_query, low_query, high_query),
                 (weight_key, low_key, high_key),
@@ -232,11 +269,14 @@
         got = {}
         for what, hop, chunk in steps:
             if what == "merge":
-                if chunk == FIRST:
-                    piece = merge_first(*inputs[chunk])
-                    outs[chunk] = jax.ShapeDtypeStruct((piece.shape[0], depth * n), piece.dtype)
+                which = chunk[0]
+                columns = inputs[which][0].shape[1]
+                whole = jax.ShapeDtypeStruct((columns, depth * n), jnp.bfloat16)
+                out = outs.setdefault(which, whole)
+                if which == KEY:
+                    piece = merge_first(*inputs[which], *extent(columns, chunk))
                 else:
-                    piece, outs[chunk] = merge(me_ref, *inputs[chunk], depth * n)
+                    piece, outs[which] = merge(me_ref, *inputs[which], chunk, out)
                 got[(0, 0), chunk] = got[(0, 1), chunk] = piece
             elif what == "hop":
                 r, parity = hop
@@ -244,9 +284,11 @@
                 got[hop, chunk] = lax.ppermute(held, "shard", hop_pairs(n, parity))
             elif what == "place":
                 pieces = [got[pair, chunk] for pair in hop]
-                ends = hop[-1] == hops_of(n)[-1] and chunk == LAST
+                ends = hop[-1] == hops_of(n)[-1] and chunk[0] == VALUE
                 staged = not (hop[0] == (0, 0) or ends)
-                outs[chunk] = place(me_ref, n, hop, pieces, outs[chunk], staged)
+                out = outs[chunk[0]]
+                start, _ = extent(out.shape[0], chunk)
+                outs[chunk[0]] = place(me_ref, n, hop, pieces, out, start, staged)
             elif what == "exchange":
                 share = (norm_train + norm_step).astype(jnp.bfloat16)
                 shares = [share] + [

time: 281 us -> 284 us (1.011)
  waiting for transfers between devices: 154 us -> 142 us
  Pallas kernels: 30.3 us -> 41.9 us
    ppermute x9 -> x15, waiting for transfers between devices: 106 us -> 91.6 us  [on_device(): got[hop, chunk] = lax.ppermute(held, 'shard', hop_pairs(n, parity))]
    pallas_call x8 -> x14, Pallas kernels: 22.6 us -> 32.4 us  [the longest x12 29.8 us: place(): pl.pallas_call(functools.partial(place_kernel, n, hops, start, staged), g...]
    ppermute x9 -> x15, starting transfers between devices: 89.3 us -> 93.8 us  [on_device(): got[hop, chunk] = lax.ppermute(held, 'shard', hop_pairs(n, parity))]
    pallas_call x2 -> x3, Pallas kernels: 7.69 us -> 9.51 us  [merge(): pl.pallas_call(merge_kernel, grid_spec=pltpu.PrefetchScalarGridSpec(num_s...]
  transfers between devices with their start and end apart: 13 -> 19, of which waited for: 7 -> 11; matrix products, arithmetic and copies ran while one was open for 0% -> 0% of each run, Pallas kernels for 8% -> 12%
where the time goes in v7:
time: 284 us; the launch traced here: 283 us
  waiting for transfers between devices  142 us (50%)
  starting transfers between devices  96.7 us (34%)
  Pallas kernels  41.9 us (15%)
    ppermute x15, starting transfers between devices, on_device(): got[hop, chunk] = lax.ppermute(held, 'shard', hop_pairs(n, parity))  93.8 us
    ppermute x15, waiting for transfers between devices, on_device(): got[hop, chunk] = lax.ppermute(held, 'shard', hop_pairs(n, parity))  91.6 us
    ppermute x3, waiting for transfers between devices, on_device(): lax.ppermute(rows[0], 'shard', [(j, (j + hop) % n) for j in range(n)])  50.4 us
    pallas_call x12, Pallas kernels, place(): pl.pallas_call(functools.partial(place_kernel, n, hops, start, staged), g...  29.8 us
    pallas_call x3, Pallas kernels, merge(): pl.pallas_call(merge_kernel, grid_spec=pltpu.PrefetchScalarGridSpec(num_s...  9.51 us
  transfers between devices with their start and end apart: 19, of which 11 were waited for; matrix products, arithmetic and copies ran while one was open for 0% of the time, Pallas kernels for 12%

profile of v7, /device:TPU:0, one launch (start us, length us, event | category | flops | bytes accessed | tf_op | source)
XLA Modules:
  0.0 283.1 jit_solution(11135709605262634927)
XLA Ops:
  0.7 5.2 %merge.5 = (bf16[2048,640]{1,0:T(8,128)(2,1)}, bf16[2048,2560]{1,0:T(8,128)(2,1)}) custom-call(s32[1]{0:T(128)} %bitcast.me_ref, bf16[640,2048]{1,0:T(8,128)(2,1)} %weight_ref.5, bf16[64,640]{1,0:T(8,128)(2,1)} %bitcast.8, bf16[64,2048]{1,0:T(8,128)(2,1)} %high_ref.5), custom_call_target="tpu_custom_call" | custom-call | flops 167772160 | bytes 7864320 | tf_op jit(solution)/shard_map/merge/pallas_call | solution.py:95
  5.9 5.1 %collective-permute-start = (bf16[2048,640]{1,0:T(8,128)(2,1)}, bf16[2048,640]{1,0:T(8,128)(2,1)}, u32[]{:S(2)}, u32[]{:S(2)}) collective-permute-start(bf16[2048,640]{1,0:T(8,128)(2,1)} %get-tuple-element.10), channel_id=1, source_target_pairs={{2,4},{4,2},{6,0},{0,6},{3,5},{5,3},{7,1},{1,7},{10,12},{12,10},{1... | collective-permute-start | bytes 7864328 | tf_op jit(solution)/shard_map/ppermute | solution.py:284
  11.0 58.1 %collective-permute-done.refs_1_ = bf16[2048,640]{1,0:T(8,128)(2,1)} collective-permute-done((bf16[2048,640]{1,0:T(8,128)(2,1)}, bf16[2048,640]{1,0:T(8,128)(2,1)}, u32[]{:S(2)}, u32[]{:S(2)}) %collective-permute-start) | collective-permute-done | bytes 2621472 | tf_op jit(solution)/shard_map/ppermute | solution.py:284
  69.1 55.0 %collective-permute-start.1 = (bf16[2048,640]{1,0:T(8,128)(2,1)}, bf16[2048,640]{1,0:T(8,128)(2,1)}, u32[]{:S(2)}, u32[]{:S(2)}) collective-permute-start(bf16[2048,640]{1,0:T(8,128)(2,1)} %collective-permute-done.refs_1_), channel_id=1, source_target_pairs={{0,2},{2,0},{4,6},{6,4},{1,3},{3,1},{5,7},{7,5},{8,10},{10,8},{12,... | collective-permute-start | bytes 7864328 | tf_op jit(solution)/shard_map/ppermute | solution.py:284
  124.1 1.6 collective-permute-start.15
  125.7 2.4 merge.8
  128.0 1.9 merge.9
  129.9 2.5 collective-permute-start.9
  133.8 49.6 %collective-permute-done.16 = bf16[640]{0:T(1024)(128)(2,1)S(1)} collective-permute-done((bf16[640]{0:T(1024)(128)(2,1)S(1)}, bf16[640]{0:T(1024)(128)(2,1)S(1)}, u32[]{:S(2)}, u32[]{:S(2)}) %collective-permute-start.16) | collective-permute-done | bytes 1312 | tf_op jit(solution)/shard_map/ppermute | solution.py:300
  184.7 3.8 %collective-permute-start.13 = (bf16[128,640]{1,0:T(8,128)(2,1)}, bf16[128,640]{1,0:T(8,128)(2,1)S(1)}, u32[]{:S(2)}, u32[]{:S(2)}) collective-permute-start(bf16[128,640]{1,0:T(8,128)(2,1)} %get-tuple-element.13), channel_id=1, source_target_pairs={{0,2},{2,0},{4,6},{6,4},{1,3},{3,1},{5,7},{7,5},{8,10},{10,8},{12,... | collective-permute-start | bytes 491528 | tf_op jit(solution)/shard_map/ppermute | solution.py:284
  189.3 1.9 collective-permute-start.5
  192.6 4.7 %collective-permute-done.13.refs_0_ = bf16[128,640]{1,0:T(8,128)(2,1)S(1)} collective-permute-done((bf16[128,640]{1,0:T(8,128)(2,1)}, bf16[128,640]{1,0:T(8,128)(2,1)S(1)}, u32[]{:S(2)}, u32[]{:S(2)}) %collective-permute-start.13) | collective-permute-done | bytes 163872 | tf_op jit(solution)/shard_map/ppermute | solution.py:284
  197.3 4.8 %collective-permute-start.3 = (bf16[256,640]{1,0:T(8,128)(2,1)S(1)}, bf16[256,640]{1,0:T(8,128)(2,1)S(1)}, u32[]{:S(2)}, u32[]{:S(2)}) collective-permute-start(bf16[256,640]{1,0:T(8,128)(2,1)S(1)} %merge.6.refs_0_), channel_id=1, source_target_pairs={{2,4},{4,2},{6,0},{0,6},{3,5},{5,3},{7,1},{1,7},{10,12},{12,10},{1... | collective-permute-start | bytes 983048 | tf_op jit(solution)/shard_map/ppermute | solution.py:284
  203.4 4.2 %collective-permute-start.7 = (bf16[256,640]{1,0:T(8,128)(2,1)S(1)}, bf16[256,640]{1,0:T(8,128)(2,1)S(1)}, u32[]{:S(2)}, u32[]{:S(2)}) collective-permute-start(bf16[256,640]{1,0:T(8,128)(2,1)S(1)} %merge.6.refs_0_), channel_id=1, source_target_pairs={{0,2},{2,0},{4,6},{6,4},{1,3},{3,1},{5,7},{7,5},{8,10},{10,8},{12,... | collective-permute-start | bytes 983048 | tf_op jit(solution)/shard_map/ppermute | solution.py:284
  207.5 3.8 %collective-permute-done.8.refs_0_ = bf16[256,640]{1,0:T(8,128)(2,1)S(1)} collective-permute-done((bf16[256,640]{1,0:T(8,128)(2,1)S(1)}, bf16[256,640]{1,0:T(8,128)(2,1)S(1)}, u32[]{:S(2)}, u32[]{:S(2)}) %collective-permute-start.8) | collective-permute-done | bytes 327712 | tf_op jit(solution)/shard_map/ppermute | solution.py:284
  211.3 4.7 %collective-permute-start.11 = (bf16[384,640]{1,0:T(8,128)(2,1)}, bf16[384,640]{1,0:T(8,128)(2,1)S(1)}, u32[]{:S(2)}, u32[]{:S(2)}) collective-permute-start(bf16[384,640]{1,0:T(8,128)(2,1)} %get-tuple-element.14), channel_id=1, source_target_pairs={{2,4},{4,2},{6,0},{0,6},{3,5},{5,3},{7,1},{1,7},{10,12},{12,10},{1... | collective-permute-start | bytes 1474568 | tf_op jit(solution)/shard_map/ppermute | solution.py:284
  217.4 4.2 %collective-permute-start.14 = (bf16[384,640]{1,0:T(8,128)(2,1)}, bf16[384,640]{1,0:T(8,128)(2,1)S(1)}, u32[]{:S(2)}, u32[]{:S(2)}) collective-permute-start(bf16[384,640]{1,0:T(8,128)(2,1)} %get-tuple-element.14), channel_id=1, source_target_pairs={{0,2},{2,0},{4,6},{6,4},{1,3},{3,1},{5,7},{7,5},{8,10},{10,8},{12,... | collective-permute-start | bytes 1474568 | tf_op jit(solution)/shard_map/ppermute | solution.py:284
  221.6 7.3 %collective-permute-done.7.refs_0_ = bf16[256,640]{1,0:T(8,128)(2,1)S(1)} collective-permute-done((bf16[256,640]{1,0:T(8,128)(2,1)S(1)}, bf16[256,640]{1,0:T(8,128)(2,1)S(1)}, u32[]{:S(2)}, u32[]{:S(2)}) %collective-permute-start.7) | collective-permute-done | bytes 327712 | tf_op jit(solution)/shard_map/ppermute | solution.py:284
  228.9 6.2 %collective-permute-done.11.refs_1_ = bf16[384,640]{1,0:T(8,128)(2,1)S(1)} collective-permute-done((bf16[384,640]{1,0:T(8,128)(2,1)}, bf16[384,640]{1,0:T(8,128)(2,1)S(1)}, u32[]{:S(2)}, u32[]{:S(2)}) %collective-permute-start.11) | collective-permute-done | bytes 491552 | tf_op jit(solution)/shard_map/ppermute | solution.py:284
  235.0 3.3 %collective-permute-start.12 = (bf16[384,640]{1,0:T(8,128)(2,1)S(1)}, bf16[384,640]{1,0:T(8,128)(2,1)S(1)}, u32[]{:S(2)}, u32[]{:S(2)}) collective-permute-start(bf16[384,640]{1,0:T(8,128)(2,1)S(1)} %collective-permute-done.11.refs_1_), channel_id=1, source_target_pairs={{0,2},{2,0},{4,6},{6,4},{1,3},{3,1},{5,7},{7,5},{8,10},{10,8},{12,... | collective-permute-start | bytes 1474568 | tf_op jit(solution)/shard_map/ppermute | solution.py:284
  239.9 3.4 %place.16.refs_2_ = bf16[512,2560]{1,0:T(8,128)(2,1)} custom-call(s32[1]{0:T(128)} %bitcast.me_ref, bf16[256,640]{1,0:T(8,128)(2,1)} %copy-done.5, bf16[256,640]{1,0:T(8,128)(2,1)} %copy-done.3, bf16[512,2560]{1,0:T(8,128)(2,1)} %place.15.refs_2_), custom_call_target="tpu_custom_call", output_to_operand_aliasing={{}: (3, {})} | custom-call | flops 163840 | bytes 655360 | tf_op jit(solution)/shard_map/place/pallas_call | solution.py:153
  243.3 1.7 collective-permute-start.10
  245.1 4.5 %collective-permute-done.6.refs_0_ = bf16[256,640]{1,0:T(8,128)(2,1)} collective-permute-done((bf16[256,640]{1,0:T(8,128)(2,1)S(1)}, bf16[256,640]{1,0:T(8,128)(2,1)}, u32[]{:S(2)}, u32[]{:S(2)}) %collective-permute-start.6) | collective-permute-done | bytes 327712 | tf_op jit(solution)/shard_map/ppermute | solution.py:284
  249.6 2.6 collective-permute-start.4
  252.3 3.4 %place.17.refs_1_ = bf16[512,2560]{1,0:T(8,128)(2,1)} custom-call(s32[1]{0:T(128)} %bitcast.me_ref, bf16[256,640]{1,0:T(8,128)(2,1)} %copy-done.4, bf16[256,640]{1,0:T(8,128)(2,1)} %copy-done.2, bf16[512,2560]{1,0:T(8,128)(2,1)} %place.16.refs_2_), custom_call_target="tpu_custom_call", output_to_operand_aliasing={{}: (3, {})} | custom-call | flops 163840 | bytes 655360 | tf_op jit(solution)/shard_map/place/pallas_call | solution.py:153
  255.7 3.6 %place.20.refs_2_ = bf16[512,2560]{1,0:T(8,128)(2,1)} custom-call(s32[1]{0:T(128)} %bitcast.me_ref, bf16[384,640]{1,0:T(8,128)(2,1)} %copy-done.1, bf16[384,640]{1,0:T(8,128)(2,1)} %copy-done, bf16[512,2560]{1,0:T(8,128)(2,1)} %get-tuple-element.15.refs_2_), custom_call_target="tpu_custom_call", output_to_operand_aliasing={{}: (3, {})} | custom-call | flops 245760 | bytes 983040 | tf_op jit(solution)/shard_map/place/pallas_call | solution.py:153
  260.0 3.2 %place.21.refs_1_ = bf16[512,2560]{1,0:T(8,128)(2,1)} custom-call(s32[1]{0:T(128)} %bitcast.me_ref, bf16[128,640]{1,0:T(8,128)(2,1)} %copy-done.7, bf16[128,640]{1,0:T(8,128)(2,1)} %collective-permute-done.9.refs_1_, bf16[512,2560]{1,0:T(8,128)(2,1)} %place.20.refs_2_), custom_call_target="tpu_custom_call", output_to_operand_aliasing={{}: (3, {})} | custom-call | flops 81920 | bytes 327680 | tf_op jit(solution)/shard_map/place/pallas_call | solution.py:153
  263.1 1.7 place.18.refs_1_
  264.9 4.4 %collective-permute-done.4.refs_0_ = bf16[256,640]{1,0:T(8,128)(2,1)S(1)} collective-permute-done((bf16[256,640]{1,0:T(8,128)(2,1)S(1)}, bf16[256,640]{1,0:T(8,128)(2,1)S(1)}, u32[]{:S(2)}, u32[]{:S(2)}) %collective-permute-start.4) | collective-permute-done | bytes 327712 | tf_op jit(solution)/shard_map/ppermute | solution.py:284
  270.0 1.7 place.19
  273.3 6.5 %place.12.refs_1_ = bf16[2048,2560]{1,0:T(8,128)(2,1)} custom-call(s32[1]{0:T(128)} %bitcast.me_ref, bf16[2048,640]{1,0:T(8,128)(2,1)} %collective-permute-done.2.refs_0_, bf16[2048,640]{1,0:T(8,128)(2,1)} %collective-permute-done.refs_1_, bf16[2048,2560]{1,0:T(8,128)(2,1)} %get-tuple-element.11.refs_2_), custom_call_target="tpu_custom_call", output_to_operand_aliasing={{}: (3, {})} | custom-call | flops 1310720 | bytes 5242880 | tf_op jit(solution)/shard_map/place/pallas_call | solution.py:153
  279.8 3.3 %place.13 = bf16[2048,2560]{1,0:T(8,128)(2,1)} custom-call(s32[1]{0:T(128)} %bitcast.me_ref, bf16[2048,640]{1,0:T(8,128)(2,1)} %collective-permute-done.1.refs_0_, bf16[2048,2560]{1,0:T(8,128)(2,1)} %place.12.refs_1_), custom_call_target="tpu_custom_call", output_to_operand_aliasing={{}: (2, {})} | custom-call | flops 1310720 | bytes 5242880 | tf_op jit(solution)/shard_map/place/pallas_call | solution.py:153
  (48 shorter events, 11.9 us)
Async XLA Ops:
  0.6 123.4 %copy-start.8 = (f32[320]{0:T(512)S(1)}, f32[320]{0:T(512)}, u32[]{:S(2)}) copy-start(f32[320]{0:T(512)} %param.20) | copy-start | bytes 3844
  0.6 123.4 %copy-start.9 = (f32[320]{0:T(512)S(1)}, f32[320]{0:T(512)}, u32[]{:S(2)}) copy-start(f32[320]{0:T(512)} %param.21) | copy-start | bytes 3844
  5.9 63.2 %collective-permute-start = (bf16[2048,640]{1,0:T(8,128)(2,1)}, bf16[2048,640]{1,0:T(8,128)(2,1)}, u32[]{:S(2)}, u32[]{:S(2)}) collective-permute-start(bf16[2048,640]{1,0:T(8,128)(2,1)} %get-tuple-element.10), channel_id=1, source_target_pairs={{2,4},{4,2},{6,0},{0,6},{3,5},{5,3},{7,1},{1,7},{10,12},{12,10},{1... | collective-permute-start | bytes 7864328 | tf_op jit(solution)/shard_map/ppermute | solution.py:284
  11.0 262.3 %collective-permute-start.2 = (bf16[2048,640]{1,0:T(8,128)(2,1)}, bf16[2048,640]{1,0:T(8,128)(2,1)}, u32[]{:S(2)}, u32[]{:S(2)}) collective-permute-start(bf16[2048,640]{1,0:T(8,128)(2,1)} %get-tuple-element.10), channel_id=1, source_target_pairs={{0,2},{2,0},{4,6},{6,4},{1,3},{3,1},{5,7},{7,5},{8,10},{10,8},{12,... | collective-permute-start | bytes 7864328 | tf_op jit(solution)/shard_map/ppermute | solution.py:284
  69.1 210.7 %collective-permute-start.1 = (bf16[2048,640]{1,0:T(8,128)(2,1)}, bf16[2048,640]{1,0:T(8,128)(2,1)}, u32[]{:S(2)}, u32[]{:S(2)}) collective-permute-start(bf16[2048,640]{1,0:T(8,128)(2,1)} %collective-permute-done.refs_1_), channel_id=1, source_target_pairs={{0,2},{2,0},{4,6},{6,4},{1,3},{3,1},{5,7},{7,5},{8,10},{10,8},{12,... | collective-permute-start | bytes 7864328 | tf_op jit(solution)/shard_map/ppermute | solution.py:284
  124.1 8.3 %collective-permute-start.15 = (bf16[320]{0:T(512)(128)(2,1)S(1)}, bf16[320]{0:T(512)(128)(2,1)S(1)}, u32[]{:S(2)}, u32[]{:S(2)}) collective-permute-start(bf16[320]{0:T(512)(128)(2,1)S(1)} %add_convert_fusion), channel_id=1, source_target_pairs={{0,1},{1,0},{2,3},{3,2},{4,5},{5,4},{6,7},{7,6},{8,9},{9,8},{10,11... | collective-permute-start | bytes 1928 | tf_op jit(solution)/shard_map/ppermute | solution.py:295
  129.9 61.4 %collective-permute-start.9 = (bf16[128,640]{1,0:T(8,128)(2,1)}, bf16[128,640]{1,0:T(8,128)(2,1)}, u32[]{:S(2)}, u32[]{:S(2)}) collective-permute-start(bf16[128,640]{1,0:T(8,128)(2,1)} %get-tuple-element.13), channel_id=1, source_target_pairs={{2,4},{4,2},{6,0},{0,6},{3,5},{5,3},{7,1},{1,7},{10,12},{12,10},{1... | collective-permute-start | bytes 491528 | tf_op jit(solution)/shard_map/ppermute | solution.py:284
  132.5 50.9 %collective-permute-start.16 = (bf16[640]{0:T(1024)(128)(2,1)S(1)}, bf16[640]{0:T(1024)(128)(2,1)S(1)}, u32[]{:S(2)}, u32[]{:S(2)}) collective-permute-start(bf16[640]{0:T(1024)(128)(2,1)S(1)} %pad_maximum_fusion.1), channel_id=1, source_target_pairs={{0,6},{2,0},{4,2},{6,4},{1,7},{3,1},{5,3},{7,5},{8,14},{10,8},{12,... | collective-permute-start | bytes 3848 | tf_op jit(solution)/shard_map/ppermute | solution.py:300
  133.8 50.9 %collective-permute-start.17 = (bf16[640]{0:T(1024)(128)(2,1)S(1)}, bf16[640]{0:T(1024)(128)(2,1)S(1)}, u32[]{:S(2)}, u32[]{:S(2)}) collective-permute-start(bf16[640]{0:T(1024)(128)(2,1)S(1)} %pad_maximum_fusion.1), channel_id=1, source_target_pairs={{0,4},{2,6},{4,0},{6,2},{1,5},{3,7},{5,1},{7,3},{8,12},{10,14},{12... | collective-permute-start | bytes 3848 | tf_op jit(solution)/shard_map/ppermute | solution.py:300
  183.4 5.9 %collective-permute-start.18 = (bf16[640]{0:T(1024)(128)(2,1)S(1)}, bf16[640]{0:T(1024)(128)(2,1)S(1)}, u32[]{:S(2)}, u32[]{:S(2)}) collective-permute-start(bf16[640]{0:T(1024)(128)(2,1)S(1)} %pad_maximum_fusion.1), channel_id=1, source_target_pairs={{0,2},{2,4},{4,6},{6,0},{1,3},{3,5},{5,7},{7,1},{8,10},{10,12},{12... | collective-permute-start | bytes 3848 | tf_op jit(solution)/shard_map/ppermute | solution.py:300
  184.7 12.6 %collective-permute-start.13 = (bf16[128,640]{1,0:T(8,128)(2,1)}, bf16[128,640]{1,0:T(8,128)(2,1)S(1)}, u32[]{:S(2)}, u32[]{:S(2)}) collective-permute-start(bf16[128,640]{1,0:T(8,128)(2,1)} %get-tuple-element.13), channel_id=1, source_target_pairs={{0,2},{2,0},{4,6},{6,4},{1,3},{3,1},{5,7},{7,5},{8,10},{10,8},{12,... | collective-permute-start | bytes 491528 | tf_op jit(solution)/shard_map/ppermute | solution.py:284
  189.3 14.0 %collective-permute-start.5 = (bf16[256,640]{1,0:T(8,128)(2,1)S(1)}, bf16[256,640]{1,0:T(8,128)(2,1)S(1)}, u32[]{:S(2)}, u32[]{:S(2)}) collective-permute-start(bf16[256,640]{1,0:T(8,128)(2,1)S(1)} %merge.7.refs_0_), channel_id=1, source_target_pairs={{2,4},{4,2},{6,0},{0,6},{3,5},{5,3},{7,1},{1,7},{10,12},{12,10},{1... | collective-permute-start | bytes 983048 | tf_op jit(solution)/shard_map/ppermute | solution.py:284
  191.3 20.1 %collective-permute-start.8 = (bf16[256,640]{1,0:T(8,128)(2,1)S(1)}, bf16[256,640]{1,0:T(8,128)(2,1)S(1)}, u32[]{:S(2)}, u32[]{:S(2)}) collective-permute-start(bf16[256,640]{1,0:T(8,128)(2,1)S(1)} %merge.7.refs_0_), channel_id=1, source_target_pairs={{0,2},{2,0},{4,6},{6,4},{1,3},{3,1},{5,7},{7,5},{8,10},{10,8},{12,... | collective-permute-start | bytes 983048 | tf_op jit(solution)/shard_map/ppermute | solution.py:284
  197.3 31.6 %copy-start.7 = (bf16[128,640]{1,0:T(8,128)(2,1)}, bf16[128,640]{1,0:T(8,128)(2,1)S(1)}, u32[]{:S(2)}) copy-start(bf16[128,640]{1,0:T(8,128)(2,1)S(1)} %collective-permute-done.13.refs_0_) | copy-start | bytes 491524
  197.3 20.1 %collective-permute-start.3 = (bf16[256,640]{1,0:T(8,128)(2,1)S(1)}, bf16[256,640]{1,0:T(8,128)(2,1)S(1)}, u32[]{:S(2)}, u32[]{:S(2)}) collective-permute-start(bf16[256,640]{1,0:T(8,128)(2,1)S(1)} %merge.6.refs_0_), channel_id=1, source_target_pairs={{2,4},{4,2},{6,0},{0,6},{3,5},{5,3},{7,1},{1,7},{10,12},{12,10},{1... | collective-permute-start | bytes 983048 | tf_op jit(solution)/shard_map/ppermute | solution.py:284
  203.4 36.5 %copy-start.3 = (bf16[256,640]{1,0:T(8,128)(2,1)}, bf16[256,640]{1,0:T(8,128)(2,1)S(1)}, u32[]{:S(2)}) copy-start(bf16[256,640]{1,0:T(8,128)(2,1)S(1)} %collective-permute-done.5.refs_1_) | copy-start | bytes 983044
  203.4 25.5 %collective-permute-start.7 = (bf16[256,640]{1,0:T(8,128)(2,1)S(1)}, bf16[256,640]{1,0:T(8,128)(2,1)S(1)}, u32[]{:S(2)}, u32[]{:S(2)}) collective-permute-start(bf16[256,640]{1,0:T(8,128)(2,1)S(1)} %merge.6.refs_0_), channel_id=1, source_target_pairs={{0,2},{2,0},{4,6},{6,4},{1,3},{3,1},{5,7},{7,5},{8,10},{10,8},{12,... | collective-permute-start | bytes 983048 | tf_op jit(solution)/shard_map/ppermute | solution.py:284
  211.3 28.5 %copy-start.5 = (bf16[256,640]{1,0:T(8,128)(2,1)}, bf16[256,640]{1,0:T(8,128)(2,1)S(1)}, u32[]{:S(2)}) copy-start(bf16[256,640]{1,0:T(8,128)(2,1)S(1)} %collective-permute-done.8.refs_0_) | copy-start | bytes 983044
  211.3 23.7 %collective-permute-start.11 = (bf16[384,640]{1,0:T(8,128)(2,1)}, bf16[384,640]{1,0:T(8,128)(2,1)S(1)}, u32[]{:S(2)}, u32[]{:S(2)}) collective-permute-start(bf16[384,640]{1,0:T(8,128)(2,1)} %get-tuple-element.14), channel_id=1, source_target_pairs={{2,4},{4,2},{6,0},{0,6},{3,5},{5,3},{7,1},{1,7},{10,12},{12,10},{1... | collective-permute-start | bytes 1474568 | tf_op jit(solution)/shard_map/ppermute | solution.py:284
  217.4 32.2 %copy-start.2 = (bf16[256,640]{1,0:T(8,128)(2,1)}, bf16[256,640]{1,0:T(8,128)(2,1)S(1)}, u32[]{:S(2)}) copy-start(bf16[256,640]{1,0:T(8,128)(2,1)S(1)} %collective-permute-done.3.refs_1_) | copy-start | bytes 983044
  217.4 25.9 %collective-permute-start.14 = (bf16[384,640]{1,0:T(8,128)(2,1)}, bf16[384,640]{1,0:T(8,128)(2,1)S(1)}, u32[]{:S(2)}, u32[]{:S(2)}) collective-permute-start(bf16[384,640]{1,0:T(8,128)(2,1)} %get-tuple-element.14), channel_id=1, source_target_pairs={{0,2},{2,0},{4,6},{6,4},{1,3},{3,1},{5,7},{7,5},{8,10},{10,8},{12,... | collective-permute-start | bytes 1474568 | tf_op jit(solution)/shard_map/ppermute | solution.py:284
  228.9 11.0 %copy-start.4 = (bf16[256,640]{1,0:T(8,128)(2,1)}, bf16[256,640]{1,0:T(8,128)(2,1)S(1)}, u32[]{:S(2)}) copy-start(bf16[256,640]{1,0:T(8,128)(2,1)S(1)} %collective-permute-done.7.refs_0_) | copy-start | bytes 983044
  228.9 20.8 %collective-permute-start.6 = (bf16[256,640]{1,0:T(8,128)(2,1)S(1)}, bf16[256,640]{1,0:T(8,128)(2,1)}, u32[]{:S(2)}, u32[]{:S(2)}) collective-permute-start(bf16[256,640]{1,0:T(8,128)(2,1)S(1)} %collective-permute-done.5.refs_1_), channel_id=1, source_target_pairs={{0,2},{2,0},{4,6},{6,4},{1,3},{3,1},{5,7},{7,5},{8,10},{10,8},{12,... | collective-permute-start | bytes 983048 | tf_op jit(solution)/shard_map/ppermute | solution.py:284
  235.0 4.9 %copy-start = (bf16[384,640]{1,0:T(8,128)(2,1)}, bf16[384,640]{1,0:T(8,128)(2,1)S(1)}, u32[]{:S(2)}) copy-start(bf16[384,640]{1,0:T(8,128)(2,1)S(1)} %collective-permute-done.11.refs_1_) | copy-start | bytes 1474564
  235.0 36.7 %collective-permute-start.12 = (bf16[384,640]{1,0:T(8,128)(2,1)S(1)}, bf16[384,640]{1,0:T(8,128)(2,1)S(1)}, u32[]{:S(2)}, u32[]{:S(2)}) collective-permute-start(bf16[384,640]{1,0:T(8,128)(2,1)S(1)} %collective-permute-done.11.refs_1_), channel_id=1, source_target_pairs={{0,2},{2,0},{4,6},{6,4},{1,3},{3,1},{5,7},{7,5},{8,10},{10,8},{12,... | collective-permute-start | bytes 1474568 | tf_op jit(solution)/shard_map/ppermute | solution.py:284
  243.3 12.4 %copy-start.1 = (bf16[384,640]{1,0:T(8,128)(2,1)}, bf16[384,640]{1,0:T(8,128)(2,1)S(1)}, u32[]{:S(2)}) copy-start(bf16[384,640]{1,0:T(8,128)(2,1)S(1)} %collective-permute-done.14.refs_0_) | copy-start | bytes 1474564
  243.3 29.2 %collective-permute-start.10 = (bf16[128,640]{1,0:T(8,128)(2,1)}, bf16[128,640]{1,0:T(8,128)(2,1)S(1)}, u32[]{:S(2)}, u32[]{:S(2)}) collective-permute-start(bf16[128,640]{1,0:T(8,128)(2,1)} %collective-permute-done.9.refs_1_), channel_id=1, source_target_pairs={{0,2},{2,0},{4,6},{6,4},{1,3},{3,1},{5,7},{7,5},{8,10},{10,8},{12,... | collective-permute-start | bytes 491528 | tf_op jit(solution)/shard_map/ppermute | solution.py:284
  249.6 19.7 %collective-permute-start.4 = (bf16[256,640]{1,0:T(8,128)(2,1)S(1)}, bf16[256,640]{1,0:T(8,128)(2,1)S(1)}, u32[]{:S(2)}, u32[]{:S(2)}) collective-permute-start(bf16[256,640]{1,0:T(8,128)(2,1)S(1)} %collective-permute-done.3.refs_1_), channel_id=1, source_target_pairs={{0,2},{2,0},{4,6},{6,4},{1,3},{3,1},{5,7},{7,5},{8,10},{10,8},{12,... | collective-permute-start | bytes 983048 | tf_op jit(solution)/shard_map/ppermute | solution.py:284
  269.3 0.7 copy-start.6

commit v8 on v7

--- a/solution.py
+++ b/solution.py
@@ -118,9 +118,10 @@
     return lax.rem(jnp.where(forth, me + r, me + n - r), n)
 
 
-def place_kernel(n, hops, start, staged, me_ref, *refs):
+def place_kernel(n, hops, start, staged, *refs):
     chunk_refs, refs = refs[: len(hops)], refs[-3:] if staged else (*refs[-2:], None)
     out_ref, sem, stage = refs
+    me = lax.axis_index("shard")
 
     for (r, parity), chunk_ref in zip(hops, chunk_refs):
         held = chunk_ref
@@ -130,14 +131,14 @@
             copy.start()
             copy.wait()
         rows, depth = chunk_ref.shape
-        column = pl.multiple_of(source_of(me_ref[0], n, r, parity) * depth, 128)
+        column = pl.multiple_of(source_of(me, n, r, parity) * depth, 128)
         there = out_ref.at[pl.ds(start, rows), pl.ds(column, depth)]
         copy = pltpu.make_async_copy(held, there, sem.at[0])
         copy.start()
         copy.wait()
 
 
-def place(me, n, hops, chunks, out, start, staged):
+def place(n, hops, chunks, out, start, staged):
     rows, depth = chunks[0].shape
     scratch = [pltpu.SemaphoreType.DMA((2,))]
     specs = [pl.BlockSpec(memory_space=pl.ANY if staged else pltpu.VMEM)] * len(hops)
@@ -145,20 +146,16 @@
         scratch.append(pltpu.VMEM((rows, depth), jnp.bfloat16))
     else:
         chunks = [pltpu.with_memory_space_constraint(chunk, pltpu.VMEM) for chunk in chunks]
-    operands, aliases = [me, *chunks], {}
+    operands, aliases = [*chunks], {}
     if isinstance(out, jax.Array):
         aliases = {len(operands): 0}
         operands.append(out)
         specs.append(pl.BlockSpec(memory_space=pl.ANY))
     return pl.pallas_call(
         functools.partial(place_kernel, n, hops, start, staged),
-        grid_spec=pltpu.PrefetchScalarGridSpec(
-            num_scalar_prefetch=1,
-            grid=(1,),
-            in_specs=specs,
-            out_specs=pl.BlockSpec(memory_space=pl.ANY),
-            scratch_shapes=scratch,
-        ),
+        in_specs=specs,
+        out_specs=pl.BlockSpec(memory_space=pl.ANY),
+        scratch_shapes=scratch,
         out_shape=jax.ShapeDtypeStruct(out.shape, out.dtype),
         input_output_aliases=aliases,
         cost_estimate=pl.CostEstimate(
@@ -288,7 +285,7 @@
                 staged = not (hop[0] == (0, 0) or ends)
                 out = outs[chunk[0]]
                 start, _ = extent(out.shape[0], chunk)
-                outs[chunk[0]] = place(me_ref, n, hop, pieces, out, start, staged)
+                outs[chunk[0]] = place(n, hop, pieces, out, start, staged)
             elif what == "exchange":
                 share = (norm_train + norm_step).astype(jnp.bfloat16)
                 shares = [share] + [

time: 284 us -> 284 us (level)
  transfers between devices with their start and end apart: 19 -> 19, of which waited for: 11 -> 9; matrix products, arithmetic and copies ran while one was open for 0% -> 0% of each run, Pallas kernels for 12% -> 12%
where the time goes in v8:
time: 284 us; the launch traced here: 283 us
  waiting for transfers between devices  142 us (50%)
  starting transfers between devices  96.7 us (34%)
  Pallas kernels  41.9 us (15%)
    ppermute x15, starting transfers between devices, on_device(): got[hop, chunk] = lax.ppermute(held, 'shard', hop_pairs(n, parity))  93.7 us
    ppermute x15, waiting for transfers between devices, on_device(): got[hop, chunk] = lax.ppermute(held, 'shard', hop_pairs(n, parity))  91.7 us
    ppermute x3, waiting for transfers between devices, on_device(): lax.ppermute(rows[0], 'shard', [(j, (j + hop) % n) for j in range(n)])  50.3 us
    pallas_call x12, Pallas kernels, place(): pl.pallas_call(functools.partial(place_kernel, n, hops, start, staged), i...  29.8 us
    pallas_call x3, Pallas kernels, merge(): pl.pallas_call(merge_kernel, grid_spec=pltpu.PrefetchScalarGridSpec(num_s...  9.51 us
  transfers between devices with their start and end apart: 19, of which 9 were waited for; matrix products, arithmetic and copies ran while one was open for 0% of the time, Pallas kernels for 12%

profile of v8, /device:TPU:0, one launch (start us, length us, event | category | flops | bytes accessed | tf_op | source)
XLA Modules:
  0.0 283.1 jit_solution(14137288587032875238)
XLA Ops:
  0.7 5.2 %merge.5 = (bf16[2048,640]{1,0:T(8,128)(2,1)}, bf16[2048,2560]{1,0:T(8,128)(2,1)}) custom-call(s32[1]{0:T(128)} %bitcast.me_ref, bf16[640,2048]{1,0:T(8,128)(2,1)} %weight_ref.5, bf16[64,640]{1,0:T(8,128)(2,1)} %bitcast.8, bf16[64,2048]{1,0:T(8,128)(2,1)} %high_ref.5), custom_call_target="tpu_custom_call" | custom-call | flops 167772160 | bytes 7864320 | tf_op jit(solution)/shard_map/merge/pallas_call | solution.py:95
  5.9 5.1 %collective-permute-start = (bf16[2048,640]{1,0:T(8,128)(2,1)}, bf16[2048,640]{1,0:T(8,128)(2,1)}, u32[]{:S(2)}, u32[]{:S(2)}) collective-permute-start(bf16[2048,640]{1,0:T(8,128)(2,1)} %get-tuple-element.10), channel_id=1, source_target_pairs={{2,4},{4,2},{6,0},{0,6},{3,5},{5,3},{7,1},{1,7},{10,12},{12,10},{1... | collective-permute-start | bytes 7864328 | tf_op jit(solution)/shard_map/ppermute | solution.py:281
  11.0 58.1 %collective-permute-done.refs_1_ = bf16[2048,640]{1,0:T(8,128)(2,1)} collective-permute-done((bf16[2048,640]{1,0:T(8,128)(2,1)}, bf16[2048,640]{1,0:T(8,128)(2,1)}, u32[]{:S(2)}, u32[]{:S(2)}) %collective-permute-start) | collective-permute-done | bytes 2621472 | tf_op jit(solution)/shard_map/ppermute | solution.py:281
  69.1 55.0 %collective-permute-start.1 = (bf16[2048,640]{1,0:T(8,128)(2,1)}, bf16[2048,640]{1,0:T(8,128)(2,1)}, u32[]{:S(2)}, u32[]{:S(2)}) collective-permute-start(bf16[2048,640]{1,0:T(8,128)(2,1)} %collective-permute-done.refs_1_), channel_id=1, source_target_pairs={{0,2},{2,0},{4,6},{6,4},{1,3},{3,1},{5,7},{7,5},{8,10},{10,8},{12,... | collective-permute-start | bytes 7864328 | tf_op jit(solution)/shard_map/ppermute | solution.py:281
  124.1 1.6 collective-permute-start.15
  125.7 2.4 merge.8
  128.0 1.9 merge.9
  129.9 2.5 collective-permute-start.9
  132.5 1.3 collective-permute-start.16
  133.8 49.6 %collective-permute-done.16 = bf16[640]{0:T(1024)(128)(2,1)S(1)} collective-permute-done((bf16[640]{0:T(1024)(128)(2,1)S(1)}, bf16[640]{0:T(1024)(128)(2,1)S(1)}, u32[]{:S(2)}, u32[]{:S(2)}) %collective-permute-start.16) | collective-permute-done | bytes 1312 | tf_op jit(solution)/shard_map/ppermute | solution.py:297
  184.7 3.8 %collective-permute-start.13 = (bf16[128,640]{1,0:T(8,128)(2,1)}, bf16[128,640]{1,0:T(8,128)(2,1)S(1)}, u32[]{:S(2)}, u32[]{:S(2)}) collective-permute-start(bf16[128,640]{1,0:T(8,128)(2,1)} %get-tuple-element.13), channel_id=1, source_target_pairs={{0,2},{2,0},{4,6},{6,4},{1,3},{3,1},{5,7},{7,5},{8,10},{10,8},{12,... | collective-permute-start | bytes 491528 | tf_op jit(solution)/shard_map/ppermute | solution.py:281
  189.3 1.9 collective-permute-start.3
  192.5 2.0 collective-permute-start.5
  195.8 7.4 %collective-permute-done.3.refs_1_ = bf16[256,640]{1,0:T(8,128)(2,1)S(1)} collective-permute-done((bf16[256,640]{1,0:T(8,128)(2,1)S(1)}, bf16[256,640]{1,0:T(8,128)(2,1)S(1)}, u32[]{:S(2)}, u32[]{:S(2)}) %collective-permute-start.3) | collective-permute-done | bytes 327712 | tf_op jit(solution)/shard_map/ppermute | solution.py:281
  203.3 9.7 %collective-permute-start.8 = (bf16[256,640]{1,0:T(8,128)(2,1)S(1)}, bf16[256,640]{1,0:T(8,128)(2,1)S(1)}, u32[]{:S(2)}, u32[]{:S(2)}) collective-permute-start(bf16[256,640]{1,0:T(8,128)(2,1)S(1)} %merge.7.refs_0_), channel_id=1, source_target_pairs={{0,2},{2,0},{4,6},{6,4},{1,3},{3,1},{5,7},{7,5},{8,10},{10,8},{12,... | collective-permute-start | bytes 983048 | tf_op jit(solution)/shard_map/ppermute | solution.py:281
  213.0 1.8 collective-permute-start.11
  214.8 3.8 %collective-permute-start.14 = (bf16[384,640]{1,0:T(8,128)(2,1)}, bf16[384,640]{1,0:T(8,128)(2,1)S(1)}, u32[]{:S(2)}, u32[]{:S(2)}) collective-permute-start(bf16[384,640]{1,0:T(8,128)(2,1)} %get-tuple-element.14), channel_id=1, source_target_pairs={{0,2},{2,0},{4,6},{6,4},{1,3},{3,1},{5,7},{7,5},{8,10},{10,8},{12,... | collective-permute-start | bytes 1474568 | tf_op jit(solution)/shard_map/ppermute | solution.py:281
  218.6 10.6 %collective-permute-done.8.refs_0_ = bf16[256,640]{1,0:T(8,128)(2,1)S(1)} collective-permute-done((bf16[256,640]{1,0:T(8,128)(2,1)S(1)}, bf16[256,640]{1,0:T(8,128)(2,1)S(1)}, u32[]{:S(2)}, u32[]{:S(2)}) %collective-permute-start.8) | collective-permute-done | bytes 327712 | tf_op jit(solution)/shard_map/ppermute | solution.py:281
  229.2 5.8 %collective-permute-done.11.refs_1_ = bf16[384,640]{1,0:T(8,128)(2,1)S(1)} collective-permute-done((bf16[384,640]{1,0:T(8,128)(2,1)}, bf16[384,640]{1,0:T(8,128)(2,1)S(1)}, u32[]{:S(2)}, u32[]{:S(2)}) %collective-permute-start.11) | collective-permute-done | bytes 491552 | tf_op jit(solution)/shard_map/ppermute | solution.py:281
  234.9 3.6 %collective-permute-start.12 = (bf16[384,640]{1,0:T(8,128)(2,1)S(1)}, bf16[384,640]{1,0:T(8,128)(2,1)S(1)}, u32[]{:S(2)}, u32[]{:S(2)}) collective-permute-start(bf16[384,640]{1,0:T(8,128)(2,1)S(1)} %collective-permute-done.11.refs_1_), channel_id=1, source_target_pairs={{0,2},{2,0},{4,6},{6,4},{1,3},{3,1},{5,7},{7,5},{8,10},{10,8},{12,... | collective-permute-start | bytes 1474568 | tf_op jit(solution)/shard_map/ppermute | solution.py:281
  240.1 3.4 %place.16.refs_2_ = bf16[512,2560]{1,0:T(8,128)(2,1)} custom-call(bf16[256,640]{1,0:T(8,128)(2,1)} %copy-done.5, bf16[256,640]{1,0:T(8,128)(2,1)} %copy-done.4, bf16[512,2560]{1,0:T(8,128)(2,1)} %place.15.refs_2_), custom_call_target="tpu_custom_call", output_to_operand_aliasing={{}: (2, {})} | custom-call | flops 163840 | bytes 655360 | tf_op jit(solution)/shard_map/place/pallas_call | solution.py:154
  243.6 1.4 collective-permute-start.10
  245.0 4.7 %collective-permute-done.6.refs_0_ = bf16[256,640]{1,0:T(8,128)(2,1)} collective-permute-done((bf16[256,640]{1,0:T(8,128)(2,1)S(1)}, bf16[256,640]{1,0:T(8,128)(2,1)}, u32[]{:S(2)}, u32[]{:S(2)}) %collective-permute-start.6) | collective-permute-done | bytes 327712 | tf_op jit(solution)/shard_map/ppermute | solution.py:281
  249.7 2.4 collective-permute-start.4
  252.2 3.4 %place.17.refs_1_ = bf16[512,2560]{1,0:T(8,128)(2,1)} custom-call(bf16[256,640]{1,0:T(8,128)(2,1)} %copy-done.3, bf16[256,640]{1,0:T(8,128)(2,1)} %copy-done.2, bf16[512,2560]{1,0:T(8,128)(2,1)} %place.16.refs_2_), custom_call_target="tpu_custom_call", output_to_operand_aliasing={{}: (2, {})} | custom-call | flops 163840 | bytes 655360 | tf_op jit(solution)/shard_map/place/pallas_call | solution.py:154
  255.7 3.6 %place.20.refs_2_ = bf16[512,2560]{1,0:T(8,128)(2,1)} custom-call(bf16[384,640]{1,0:T(8,128)(2,1)} %copy-done.1, bf16[384,640]{1,0:T(8,128)(2,1)} %copy-done, bf16[512,2560]{1,0:T(8,128)(2,1)} %get-tuple-element.15.refs_2_), custom_call_target="tpu_custom_call", output_to_operand_aliasing={{}: (2, {})} | custom-call | flops 245760 | bytes 983040 | tf_op jit(solution)/shard_map/place/pallas_call | solution.py:154
  259.9 3.2 %place.21.refs_1_ = bf16[512,2560]{1,0:T(8,128)(2,1)} custom-call(bf16[128,640]{1,0:T(8,128)(2,1)} %copy-done.9, bf16[128,640]{1,0:T(8,128)(2,1)} %copy-done.7, bf16[512,2560]{1,0:T(8,128)(2,1)} %place.20.refs_2_), custom_call_target="tpu_custom_call", output_to_operand_aliasing={{}: (2, {})} | custom-call | flops 81920 | bytes 327680 | tf_op jit(solution)/shard_map/place/pallas_call | solution.py:154
  263.1 1.7 place.18.refs_1_
  264.8 4.5 %collective-permute-done.4.refs_0_ = bf16[256,640]{1,0:T(8,128)(2,1)S(1)} collective-permute-done((bf16[256,640]{1,0:T(8,128)(2,1)S(1)}, bf16[256,640]{1,0:T(8,128)(2,1)S(1)}, u32[]{:S(2)}, u32[]{:S(2)}) %collective-permute-start.4) | collective-permute-done | bytes 327712 | tf_op jit(solution)/shard_map/ppermute | solution.py:281
  270.0 1.7 place.19
  273.3 6.5 %place.12.refs_1_ = bf16[2048,2560]{1,0:T(8,128)(2,1)} custom-call(bf16[2048,640]{1,0:T(8,128)(2,1)} %collective-permute-done.2.refs_0_, bf16[2048,640]{1,0:T(8,128)(2,1)} %collective-permute-done.refs_1_, bf16[2048,2560]{1,0:T(8,128)(2,1)} %get-tuple-element.11.refs_2_), custom_call_target="tpu_custom_call", output_to_operand_aliasing={{}: (2, {})} | custom-call | flops 1310720 | bytes 5242880 | tf_op jit(solution)/shard_map/place/pallas_call | solution.py:154
  279.8 3.3 %place.13 = bf16[2048,2560]{1,0:T(8,128)(2,1)} custom-call(bf16[2048,640]{1,0:T(8,128)(2,1)} %collective-permute-done.1.refs_0_, bf16[2048,2560]{1,0:T(8,128)(2,1)} %place.12.refs_1_), custom_call_target="tpu_custom_call", output_to_operand_aliasing={{}: (1, {})} | custom-call | flops 1310720 | bytes 5242880 | tf_op jit(solution)/shard_map/place/pallas_call | solution.py:154
  (52 shorter events, 9.3 us)
Async XLA Ops:
  0.6 123.4 %copy-start.10 = (f32[320]{0:T(512)S(1)}, f32[320]{0:T(512)}, u32[]{:S(2)}) copy-start(f32[320]{0:T(512)} %param.20) | copy-start | bytes 3844
  0.6 123.4 %copy-start.11 = (f32[320]{0:T(512)S(1)}, f32[320]{0:T(512)}, u32[]{:S(2)}) copy-start(f32[320]{0:T(512)} %param.21) | copy-start | bytes 3844
  5.9 63.2 %collective-permute-start = (bf16[2048,640]{1,0:T(8,128)(2,1)}, bf16[2048,640]{1,0:T(8,128)(2,1)}, u32[]{:S(2)}, u32[]{:S(2)}) collective-permute-start(bf16[2048,640]{1,0:T(8,128)(2,1)} %get-tuple-element.10), channel_id=1, source_target_pairs={{2,4},{4,2},{6,0},{0,6},{3,5},{5,3},{7,1},{1,7},{10,12},{12,10},{1... | collective-permute-start | bytes 7864328 | tf_op jit(solution)/shard_map/ppermute | solution.py:281
  11.0 262.3 %collective-permute-start.2 = (bf16[2048,640]{1,0:T(8,128)(2,1)}, bf16[2048,640]{1,0:T(8,128)(2,1)}, u32[]{:S(2)}, u32[]{:S(2)}) collective-permute-start(bf16[2048,640]{1,0:T(8,128)(2,1)} %get-tuple-element.10), channel_id=1, source_target_pairs={{0,2},{2,0},{4,6},{6,4},{1,3},{3,1},{5,7},{7,5},{8,10},{10,8},{12,... | collective-permute-start | bytes 7864328 | tf_op jit(solution)/shard_map/ppermute | solution.py:281
  69.1 210.7 %collective-permute-start.1 = (bf16[2048,640]{1,0:T(8,128)(2,1)}, bf16[2048,640]{1,0:T(8,128)(2,1)}, u32[]{:S(2)}, u32[]{:S(2)}) collective-permute-start(bf16[2048,640]{1,0:T(8,128)(2,1)} %collective-permute-done.refs_1_), channel_id=1, source_target_pairs={{0,2},{2,0},{4,6},{6,4},{1,3},{3,1},{5,7},{7,5},{8,10},{10,8},{12,... | collective-permute-start | bytes 7864328 | tf_op jit(solution)/shard_map/ppermute | solution.py:281
  124.1 8.3 %collective-permute-start.15 = (bf16[320]{0:T(512)(128)(2,1)S(1)}, bf16[320]{0:T(512)(128)(2,1)S(1)}, u32[]{:S(2)}, u32[]{:S(2)}) collective-permute-start(bf16[320]{0:T(512)(128)(2,1)S(1)} %add_convert_fusion), channel_id=1, source_target_pairs={{0,1},{1,0},{2,3},{3,2},{4,5},{5,4},{6,7},{7,6},{8,9},{9,8},{10,11... | collective-permute-start | bytes 1928 | tf_op jit(solution)/shard_map/ppermute | solution.py:292
  129.9 62.6 %collective-permute-start.9 = (bf16[128,640]{1,0:T(8,128)(2,1)}, bf16[128,640]{1,0:T(8,128)(2,1)S(1)}, u32[]{:S(2)}, u32[]{:S(2)}) collective-permute-start(bf16[128,640]{1,0:T(8,128)(2,1)} %get-tuple-element.13), channel_id=1, source_target_pairs={{2,4},{4,2},{6,0},{0,6},{3,5},{5,3},{7,1},{1,7},{10,12},{12,10},{1... | collective-permute-start | bytes 491528 | tf_op jit(solution)/shard_map/ppermute | solution.py:281
  132.5 50.9 %collective-permute-start.16 = (bf16[640]{0:T(1024)(128)(2,1)S(1)}, bf16[640]{0:T(1024)(128)(2,1)S(1)}, u32[]{:S(2)}, u32[]{:S(2)}) collective-permute-start(bf16[640]{0:T(1024)(128)(2,1)S(1)} %pad_maximum_fusion.1), channel_id=1, source_target_pairs={{0,6},{2,0},{4,2},{6,4},{1,7},{3,1},{5,3},{7,5},{8,14},{10,8},{12,... | collective-permute-start | bytes 3848 | tf_op jit(solution)/shard_map/ppermute | solution.py:297
  133.8 50.9 %collective-permute-start.17 = (bf16[640]{0:T(1024)(128)(2,1)S(1)}, bf16[640]{0:T(1024)(128)(2,1)S(1)}, u32[]{:S(2)}, u32[]{:S(2)}) collective-permute-start(bf16[640]{0:T(1024)(128)(2,1)S(1)} %pad_maximum_fusion.1), channel_id=1, source_target_pairs={{0,4},{2,6},{4,0},{6,2},{1,5},{3,7},{5,1},{7,3},{8,12},{10,14},{12... | collective-permute-start | bytes 3848 | tf_op jit(solution)/shard_map/ppermute | solution.py:297
  183.4 5.9 %collective-permute-start.18 = (bf16[640]{0:T(1024)(128)(2,1)S(1)}, bf16[640]{0:T(1024)(128)(2,1)S(1)}, u32[]{:S(2)}, u32[]{:S(2)}) collective-permute-start(bf16[640]{0:T(1024)(128)(2,1)S(1)} %pad_maximum_fusion.1), channel_id=1, source_target_pairs={{0,2},{2,4},{4,6},{6,0},{1,3},{3,5},{5,7},{7,1},{8,10},{10,12},{12... | collective-permute-start | bytes 3848 | tf_op jit(solution)/shard_map/ppermute | solution.py:297
  184.7 10.4 %collective-permute-start.13 = (bf16[128,640]{1,0:T(8,128)(2,1)}, bf16[128,640]{1,0:T(8,128)(2,1)S(1)}, u32[]{:S(2)}, u32[]{:S(2)}) collective-permute-start(bf16[128,640]{1,0:T(8,128)(2,1)} %get-tuple-element.13), channel_id=1, source_target_pairs={{0,2},{2,0},{4,6},{6,4},{1,3},{3,1},{5,7},{7,5},{8,10},{10,8},{12,... | collective-permute-start | bytes 491528 | tf_op jit(solution)/shard_map/ppermute | solution.py:281
  189.3 14.0 %collective-permute-start.3 = (bf16[256,640]{1,0:T(8,128)(2,1)S(1)}, bf16[256,640]{1,0:T(8,128)(2,1)S(1)}, u32[]{:S(2)}, u32[]{:S(2)}) collective-permute-start(bf16[256,640]{1,0:T(8,128)(2,1)S(1)} %merge.6.refs_0_), channel_id=1, source_target_pairs={{2,4},{4,2},{6,0},{0,6},{3,5},{5,3},{7,1},{1,7},{10,12},{12,10},{1... | collective-permute-start | bytes 983048 | tf_op jit(solution)/shard_map/ppermute | solution.py:281
  192.5 3.3 %copy-start.7 = (bf16[128,640]{1,0:T(8,128)(2,1)}, bf16[128,640]{1,0:T(8,128)(2,1)S(1)}, u32[]{:S(2)}) copy-start(bf16[128,640]{1,0:T(8,128)(2,1)S(1)} %collective-permute-done.9.refs_1_) | copy-start | bytes 491524
  192.5 20.4 %collective-permute-start.5 = (bf16[256,640]{1,0:T(8,128)(2,1)S(1)}, bf16[256,640]{1,0:T(8,128)(2,1)S(1)}, u32[]{:S(2)}, u32[]{:S(2)}) collective-permute-start(bf16[256,640]{1,0:T(8,128)(2,1)S(1)} %merge.7.refs_0_), channel_id=1, source_target_pairs={{2,4},{4,2},{6,0},{0,6},{3,5},{5,3},{7,1},{1,7},{10,12},{12,10},{1... | collective-permute-start | bytes 983048 | tf_op jit(solution)/shard_map/ppermute | solution.py:281
  195.1 0.7 copy-start.9
  195.1 19.7 %collective-permute-start.7 = (bf16[256,640]{1,0:T(8,128)(2,1)S(1)}, bf16[256,640]{1,0:T(8,128)(2,1)S(1)}, u32[]{:S(2)}, u32[]{:S(2)}) collective-permute-start(bf16[256,640]{1,0:T(8,128)(2,1)S(1)} %merge.6.refs_0_), channel_id=1, source_target_pairs={{0,2},{2,0},{4,6},{6,4},{1,3},{3,1},{5,7},{7,5},{8,10},{10,8},{12,... | collective-permute-start | bytes 983048 | tf_op jit(solution)/shard_map/ppermute | solution.py:281
  203.3 46.4 %copy-start.2 = (bf16[256,640]{1,0:T(8,128)(2,1)}, bf16[256,640]{1,0:T(8,128)(2,1)S(1)}, u32[]{:S(2)}) copy-start(bf16[256,640]{1,0:T(8,128)(2,1)S(1)} %collective-permute-done.3.refs_1_) | copy-start | bytes 983044
  203.3 25.9 %collective-permute-start.8 = (bf16[256,640]{1,0:T(8,128)(2,1)S(1)}, bf16[256,640]{1,0:T(8,128)(2,1)S(1)}, u32[]{:S(2)}, u32[]{:S(2)}) collective-permute-start(bf16[256,640]{1,0:T(8,128)(2,1)S(1)} %merge.7.refs_0_), channel_id=1, source_target_pairs={{0,2},{2,0},{4,6},{6,4},{1,3},{3,1},{5,7},{7,5},{8,10},{10,8},{12,... | collective-permute-start | bytes 983048 | tf_op jit(solution)/shard_map/ppermute | solution.py:281
  213.0 27.1 %copy-start.4 = (bf16[256,640]{1,0:T(8,128)(2,1)}, bf16[256,640]{1,0:T(8,128)(2,1)S(1)}, u32[]{:S(2)}) copy-start(bf16[256,640]{1,0:T(8,128)(2,1)S(1)} %collective-permute-done.5.refs_1_) | copy-start | bytes 983044
  213.0 22.0 %collective-permute-start.11 = (bf16[384,640]{1,0:T(8,128)(2,1)}, bf16[384,640]{1,0:T(8,128)(2,1)S(1)}, u32[]{:S(2)}, u32[]{:S(2)}) collective-permute-start(bf16[384,640]{1,0:T(8,128)(2,1)} %get-tuple-element.14), channel_id=1, source_target_pairs={{2,4},{4,2},{6,0},{0,6},{3,5},{5,3},{7,1},{1,7},{10,12},{12,10},{1... | collective-permute-start | bytes 1474568 | tf_op jit(solution)/shard_map/ppermute | solution.py:281
  214.8 25.3 %copy-start.3 = (bf16[256,640]{1,0:T(8,128)(2,1)}, bf16[256,640]{1,0:T(8,128)(2,1)S(1)}, u32[]{:S(2)}) copy-start(bf16[256,640]{1,0:T(8,128)(2,1)S(1)} %collective-permute-done.7.refs_0_) | copy-start | bytes 983044
  214.8 28.8 %collective-permute-start.14 = (bf16[384,640]{1,0:T(8,128)(2,1)}, bf16[384,640]{1,0:T(8,128)(2,1)S(1)}, u32[]{:S(2)}, u32[]{:S(2)}) collective-permute-start(bf16[384,640]{1,0:T(8,128)(2,1)} %get-tuple-element.14), channel_id=1, source_target_pairs={{0,2},{2,0},{4,6},{6,4},{1,3},{3,1},{5,7},{7,5},{8,10},{10,8},{12,... | collective-permute-start | bytes 1474568 | tf_op jit(solution)/shard_map/ppermute | solution.py:281
  229.2 10.9 %copy-start.5 = (bf16[256,640]{1,0:T(8,128)(2,1)}, bf16[256,640]{1,0:T(8,128)(2,1)S(1)}, u32[]{:S(2)}) copy-start(bf16[256,640]{1,0:T(8,128)(2,1)S(1)} %collective-permute-done.8.refs_0_) | copy-start | bytes 983044
  229.2 20.5 %collective-permute-start.6 = (bf16[256,640]{1,0:T(8,128)(2,1)S(1)}, bf16[256,640]{1,0:T(8,128)(2,1)}, u32[]{:S(2)}, u32[]{:S(2)}) collective-permute-start(bf16[256,640]{1,0:T(8,128)(2,1)S(1)} %collective-permute-done.5.refs_1_), channel_id=1, source_target_pairs={{0,2},{2,0},{4,6},{6,4},{1,3},{3,1},{5,7},{7,5},{8,10},{10,8},{12,... | collective-permute-start | bytes 983048 | tf_op jit(solution)/shard_map/ppermute | solution.py:281
  234.9 5.2 %copy-start = (bf16[384,640]{1,0:T(8,128)(2,1)}, bf16[384,640]{1,0:T(8,128)(2,1)S(1)}, u32[]{:S(2)}) copy-start(bf16[384,640]{1,0:T(8,128)(2,1)S(1)} %collective-permute-done.11.refs_1_) | copy-start | bytes 1474564
  234.9 36.8 %collective-permute-start.12 = (bf16[384,640]{1,0:T(8,128)(2,1)S(1)}, bf16[384,640]{1,0:T(8,128)(2,1)S(1)}, u32[]{:S(2)}, u32[]{:S(2)}) collective-permute-start(bf16[384,640]{1,0:T(8,128)(2,1)S(1)} %collective-permute-done.11.refs_1_), channel_id=1, source_target_pairs={{0,2},{2,0},{4,6},{6,4},{1,3},{3,1},{5,7},{7,5},{8,10},{10,8},{12,... | collective-permute-start | bytes 1474568 | tf_op jit(solution)/shard_map/ppermute | solution.py:281
  240.1 3.5 %copy-start.8 = (bf16[128,640]{1,0:T(8,128)(2,1)S(1)}, bf16[128,640]{1,0:T(8,128)(2,1)}, u32[]{:S(2)}) copy-start(bf16[128,640]{1,0:T(8,128)(2,1)} %copy-done.7) | copy-start | bytes 491524
  243.6 12.1 %copy-start.1 = (bf16[384,640]{1,0:T(8,128)(2,1)}, bf16[384,640]{1,0:T(8,128)(2,1)S(1)}, u32[]{:S(2)}) copy-start(bf16[384,640]{1,0:T(8,128)(2,1)S(1)} %collective-permute-done.14.refs_0_) | copy-start | bytes 1474564
  243.6 29.0 %collective-permute-start.10 = (bf16[128,640]{1,0:T(8,128)(2,1)S(1)}, bf16[128,640]{1,0:T(8,128)(2,1)S(1)}, u32[]{:S(2)}, u32[]{:S(2)}) collective-permute-start(bf16[128,640]{1,0:T(8,128)(2,1)S(1)} %copy-done.8), channel_id=1, source_target_pairs={{0,2},{2,0},{4,6},{6,4},{1,3},{3,1},{5,7},{7,5},{8,10},{10,8},{12,... | collective-permute-start | bytes 491528 | tf_op jit(solution)/shard_map/ppermute | solution.py:281
  249.7 19.6 %collective-permute-start.4 = (bf16[256,640]{1,0:T(8,128)(2,1)S(1)}, bf16[256,640]{1,0:T(8,128)(2,1)S(1)}, u32[]{:S(2)}, u32[]{:S(2)}) collective-permute-start(bf16[256,640]{1,0:T(8,128)(2,1)S(1)} %collective-permute-done.3.refs_1_), channel_id=1, source_target_pairs={{0,2},{2,0},{4,6},{6,4},{1,3},{3,1},{5,7},{7,5},{8,10},{10,8},{12,... | collective-permute-start | bytes 983048 | tf_op jit(solution)/shard_map/ppermute | solution.py:281
  269.3 0.7 copy-start.6

commit v9 on v7

--- a/solution.py
+++ b/solution.py
@@ -12,11 +12,10 @@
 
 KEY, QUERY, VALUE = range(3)
 EIGHTHS = 8
-LEAD, KEY_REST = (KEY, 0, 4), (KEY, 4, 4)
+LEAD, KEY_REST, KEY_ALL = (KEY, 0, 4), (KEY, 4, 4), (KEY, 0, 8)
 QUERY_ALL = (QUERY, 0, 8)
 NORM = None
-VALUE_REST, LAST = (VALUE, 0, 6), (VALUE, 6, 2)
-CHUNKS = (LEAD, KEY_REST, QUERY_ALL, VALUE_REST, LAST)
+VALUE_ALL, VALUE_REST, LAST = (VALUE, 0, 8), (VALUE, 0, 6), (VALUE, 6, 2)
 
 
 def extent(columns, chunk):
@@ -80,7 +79,7 @@
     depth, columns = weight.shape
     rank = high.shape[0]
     start, rows = extent(columns, chunk)
-    block = next(b for b in (512, 384, 256, 128) if start % b == 0 and rows % b == 0)
+    block = next(b for b in (256, 128) if start % b == 0 and rows % (4 * b) == 0)
     first = start // block
     specs = [
         pl.BlockSpec((depth, block), lambda j, me: (0, first + j)),
@@ -185,21 +184,27 @@
     steps = []
     for chunk in (LEAD, KEY_REST):
         steps += [("merge", None, chunk)] + [("hop", hop, chunk) for hop in hops[:1]]
-    steps += [("hop", hop, chunk) for hop in hops[1:2] for chunk in (LEAD, KEY_REST)]
-    for chunk in (QUERY_ALL, VALUE_REST, LAST):
+    steps.append(("join", hops[:1], KEY_ALL))
+    steps += [("hop", hop, KEY_ALL) for hop in hops[1:2]]
+    for chunk in (QUERY_ALL, VALUE_ALL):
         steps += [("merge", None, chunk)] + [("hop", hop, chunk) for hop in hops[:2]]
         if chunk == QUERY_ALL:
-            steps += [("place", ((0, 0),), part) for part in (LEAD, KEY_REST)]
+            steps.append(("place", ((0, 0),), KEY_ALL))
     steps.append(("exchange", None, NORM))
     steps += [("shift", k, NORM) for k in range(1, n)]
     placed = 0
     end = max(len(hops), 2)
     for i in range(2, end + 1):
-        for chunk in CHUNKS:
-            if i == end and chunk == LAST:
+        for chunk in (KEY_ALL, QUERY_ALL, VALUE_ALL):
+            if i == end and chunk == VALUE_ALL:
                 steps.append(("norm", None, NORM))
-            steps += [("hop", hop, chunk) for hop in hops[i : i + 1]]
-            steps.append(("place", tuple(hops[placed:i]), chunk))
+            parts = (chunk,)
+            if chunk == VALUE_ALL and i == len(hops) - 1:
+                steps.append(("split", hops[i], chunk))
+                parts = (VALUE_REST, LAST)
+            steps += [("hop", hop, part) for hop in hops[i : i + 1] for part in parts]
+            parts = (VALUE_REST, LAST) if chunk == VALUE_ALL and i == end > 2 else (chunk,)
+            steps += [("place", tuple(hops[placed:i]), part) for part in parts]
         placed = i
     return steps
 
@@ -278,6 +283,16 @@
                 else:
                     piece, outs[which] = merge(me_ref, *inputs[which], chunk, out)
                 got[(0, 0), chunk] = got[(0, 1), chunk] = piece
+            elif what == "join":
+                for pair in ((0, 0), (0, 1), *hop):
+                    parts = [got[pair, LEAD], got[pair, KEY_REST]]
+                    got[pair, chunk] = jnp.concatenate(parts)
+            elif what == "split":
+                r, parity = hop
+                held = got[(r - 1, 1 - parity), chunk]
+                for part in (VALUE_REST, LAST):
+                    start, size = extent(held.shape[0], part)
+                    got[(r - 1, 1 - parity), part] = held[start : start + size]
             elif what == "hop":
                 r, parity = hop
                 held = got[(r - 1, 1 - parity), chunk]

time: 284 us -> 291 us (1.025)
  waiting for transfers between devices: 142 us -> 172 us
  starting transfers between devices: 96.7 us -> 77 us
  Pallas kernels: 41.9 us -> 35.5 us
    ppermute x15 -> x11, starting transfers between devices: 93.8 us -> 68.2 us  [on_device(): got[hop, chunk] = lax.ppermute(held, 'shard', hop_pairs(n, parity))]
    ppermute x3, waiting for transfers between devices: 50.4 us -> 74.8 us  [on_device(): lax.ppermute(rows[0], 'shard', [(j, (j + hop) % n) for j in range(n)])]
    pallas_call x12 -> x8, Pallas kernels: 29.8 us -> 21.7 us  [place(): pl.pallas_call(functools.partial(place_kernel, n, hops, start, staged), g...]
    ppermute x3, starting transfers between devices: 1.35 us -> 7.23 us  [on_device(): lax.ppermute(rows[0], 'shard', [(j, (j + hop) % n) for j in range(n)])]
    ppermute x15 -> x11, waiting for transfers between devices: 91.6 us -> 97.1 us  [on_device(): got[hop, chunk] = lax.ppermute(held, 'shard', hop_pairs(n, parity))]
    pallas_call x3 -> x2, Pallas kernels: 9.51 us -> 11.2 us  [merge(): pl.pallas_call(merge_kernel, grid_spec=pltpu.PrefetchScalarGridSpec(num_s...]
  transfers between devices with their start and end apart: 19 -> 15, of which waited for: 11 -> 8; matrix products, arithmetic and copies ran while one was open for 0% -> 1% of each run, Pallas kernels for 12% -> 9%
where the time goes in v9:
time: 291 us; the launch traced here: 290 us
  waiting for transfers between devices  172 us (59%)
  starting transfers between devices  77 us (26%)
  Pallas kernels  35.5 us (12%)
    ppermute x11, waiting for transfers between devices, on_device(): got[hop, chunk] = lax.ppermute(held, 'shard', hop_pairs(n, parity))  97.1 us
    ppermute x3, waiting for transfers between devices, on_device(): lax.ppermute(rows[0], 'shard', [(j, (j + hop) % n) for j in range(n)])  74.8 us
    ppermute x11, starting transfers between devices, on_device(): got[hop, chunk] = lax.ppermute(held, 'shard', hop_pairs(n, parity))  68.2 us
    pallas_call x8, Pallas kernels, place(): pl.pallas_call(functools.partial(place_kernel, n, hops, start, staged), g...  21.7 us
    pallas_call x2, Pallas kernels, merge(): pl.pallas_call(merge_kernel, grid_spec=pltpu.PrefetchScalarGridSpec(num_s...  11.2 us
    ppermute x3, starting transfers between devices, on_device(): lax.ppermute(rows[0], 'shard', [(j, (j + hop) % n) for j in range(n)])  7.23 us
  transfers between devices with their start and end apart: 15, of which 8 were waited for; matrix products, arithmetic and copies ran while one was open for 1% of the time, Pallas kernels for 9%

profile of v9, /device:TPU:0, one launch (start us, length us, event | category | flops | bytes accessed | tf_op | source)
XLA Modules:
  0.0 289.8 jit_solution(12089376291803259623)
XLA Ops:
  0.7 7.4 %merge.4 = (bf16[2048,640]{1,0:T(8,128)(2,1)}, bf16[2048,2560]{1,0:T(8,128)(2,1)}) custom-call(s32[1]{0:T(128)} %bitcast.me_ref, bf16[640,2048]{1,0:T(8,128)(2,1)} %weight_ref.4, bf16[64,640]{1,0:T(8,128)(2,1)} %bitcast.6, bf16[64,2048]{1,0:T(8,128)(2,1)} %high_ref.4), custom_call_target="tpu_custom_call" | custom-call | flops 167772160 | bytes 7864320 | tf_op jit(solution)/shard_map/merge/pallas_call | solution.py:94
  8.0 5.1 %collective-permute-start = (bf16[2048,640]{1,0:T(8,128)(2,1)}, bf16[2048,640]{1,0:T(8,128)(2,1)}, u32[]{:S(2)}, u32[]{:S(2)}) collective-permute-start(bf16[2048,640]{1,0:T(8,128)(2,1)} %get-tuple-element.8), channel_id=1, source_target_pairs={{2,4},{4,2},{6,0},{0,6},{3,5},{5,3},{7,1},{1,7},{10,12},{12,10},{1... | collective-permute-start | bytes 7864328 | tf_op jit(solution)/shard_map/ppermute | solution.py:299
  13.1 58.1 %collective-permute-done.refs_1_ = bf16[2048,640]{1,0:T(8,128)(2,1)} collective-permute-done((bf16[2048,640]{1,0:T(8,128)(2,1)}, bf16[2048,640]{1,0:T(8,128)(2,1)}, u32[]{:S(2)}, u32[]{:S(2)}) %collective-permute-start) | collective-permute-done | bytes 2621472 | tf_op jit(solution)/shard_map/ppermute | solution.py:299
  71.2 55.0 %collective-permute-start.1 = (bf16[2048,640]{1,0:T(8,128)(2,1)}, bf16[2048,640]{1,0:T(8,128)(2,1)}, u32[]{:S(2)}, u32[]{:S(2)}) collective-permute-start(bf16[2048,640]{1,0:T(8,128)(2,1)} %collective-permute-done.refs_1_), channel_id=1, source_target_pairs={{0,2},{2,0},{4,6},{6,4},{1,3},{3,1},{5,7},{7,5},{8,10},{10,8},{12,... | collective-permute-start | bytes 7864328 | tf_op jit(solution)/shard_map/ppermute | solution.py:299
  126.2 1.3 merge.6
  127.5 1.3 merge.5
  128.9 2.5 collective-permute-start.3
  131.4 1.6 collective-permute-start.11
  133.0 3.8 %merge.7 = (bf16[512,640]{1,0:T(8,128)(2,1)}, bf16[512,2560]{1,0:T(8,128)(2,1)}) custom-call(s32[1]{0:T(128)} %bitcast.me_ref, bf16[640,512]{1,0:T(8,128)(2,1)} %weight_ref.7, bf16[64,640]{1,0:T(8,128)(2,1)} %bitcast.7, bf16[64,512]{1,0:T(8,128)(2,1)} %high_ref.7), custom_call_target="tpu_custom_call" | custom-call | flops 41943040 | bytes 1966080 | tf_op jit(solution)/shard_map/merge/pallas_call | solution.py:94
  136.8 1.4 collective-permute-start.7
  138.3 2.5 collective-permute-start.12
  140.7 69.3 %collective-permute-done.12 = bf16[640]{0:T(1024)(128)(2,1)S(1)} collective-permute-done((bf16[640]{0:T(1024)(128)(2,1)S(1)}, bf16[640]{0:T(1024)(128)(2,1)S(1)}, u32[]{:S(2)}, u32[]{:S(2)}) %collective-permute-start.12) | collective-permute-done | bytes 1312 | tf_op jit(solution)/shard_map/ppermute | solution.py:315
  210.1 3.2 %collective-permute-start.13 = (bf16[640]{0:T(1024)(128)(2,1)S(1)}, bf16[640]{0:T(1024)(128)(2,1)S(1)}, u32[]{:S(2)}, u32[]{:S(2)}) collective-permute-start(bf16[640]{0:T(1024)(128)(2,1)S(1)} %pad_maximum_fusion.3), channel_id=1, source_target_pairs={{0,4},{2,6},{4,0},{6,2},{1,5},{3,7},{5,1},{7,3},{8,12},{10,14},{12... | collective-permute-start | bytes 3848 | tf_op jit(solution)/shard_map/ppermute | solution.py:315
  213.3 1.6 collective-permute-done.13
  214.8 1.5 collective-permute-start.14
  216.4 3.9 %collective-permute-done.14 = bf16[640]{0:T(1024)(128)(2,1)S(1)} collective-permute-done((bf16[640]{0:T(1024)(128)(2,1)S(1)}, bf16[640]{0:T(1024)(128)(2,1)S(1)}, u32[]{:S(2)}, u32[]{:S(2)}) %collective-permute-start.14) | collective-permute-done | bytes 1312 | tf_op jit(solution)/shard_map/ppermute | solution.py:315
  220.3 9.1 %collective-permute-done.6 = bf16[256,640]{1,0:T(8,128)(2,1)S(1)} collective-permute-done((bf16[256,640]{1,0:T(8,128)(2,1)S(1)}, bf16[256,640]{1,0:T(8,128)(2,1)S(1)}, u32[]{:S(2)}, u32[]{:S(2)}) %collective-permute-start.6) | collective-permute-done | bytes 327712 | tf_op jit(solution)/shard_map/ppermute | solution.py:299
  229.5 2.0 collective-permute-start.5
  231.6 0.9 slice.9
  232.5 21.9 %collective-permute-done.5 = bf16[256,640]{1,0:T(8,128)(2,1)} collective-permute-done((bf16[256,640]{1,0:T(8,128)(2,1)S(1)}, bf16[256,640]{1,0:T(8,128)(2,1)}, u32[]{:S(2)}, u32[]{:S(2)}) %collective-permute-start.5) | collective-permute-done | bytes 327712 | tf_op jit(solution)/shard_map/ppermute | solution.py:299
  254.4 0.9 place.10.refs_2_
  255.4 2.1 collective-permute-start.8
  257.5 1.9 pad_maximum_fusion.1.refs_0_
  260.0 3.9 %place.11.refs_1_ = bf16[512,2560]{1,0:T(8,128)(2,1)} custom-call(s32[1]{0:T(128)} %bitcast.me_ref, bf16[512,640]{1,0:T(8,128)(2,1)} %pad_maximum_fusion.1.refs_0_, bf16[512,640]{1,0:T(8,128)(2,1)} %copy-done.2, bf16[512,2560]{1,0:T(8,128)(2,1)} %place.10.refs_2_), custom_call_target="tpu_custom_call", output_to_operand_aliasing={{}: (3, {})} | custom-call | flops 327680 | bytes 1310720 | tf_op jit(solution)/shard_map/place/pallas_call | solution.py:152
  263.9 3.9 %place.13.refs_1_ = bf16[512,2560]{1,0:T(8,128)(2,1)} custom-call(s32[1]{0:T(128)} %bitcast.me_ref, bf16[512,640]{1,0:T(8,128)(2,1)} %collective-permute-done.10.refs_0_, bf16[512,640]{1,0:T(8,128)(2,1)} %copy-done, bf16[512,2560]{1,0:T(8,128)(2,1)} %get-tuple-element.11.refs_2_), custom_call_target="tpu_custom_call", output_to_operand_aliasing={{}: (3, {})} | custom-call | flops 327680 | bytes 1310720 | tf_op jit(solution)/shard_map/place/pallas_call | solution.py:152
  267.8 7.0 %collective-permute-done.9.refs_0_ = bf16[384,640]{1,0:T(8,128)(2,1)S(1)} collective-permute-done((bf16[384,640]{1,0:T(8,128)(2,1)}, bf16[384,640]{1,0:T(8,128)(2,1)S(1)}, u32[]{:S(2)}, u32[]{:S(2)}) %collective-permute-start.9) | collective-permute-done | bytes 491552 | tf_op jit(solution)/shard_map/ppermute | solution.py:299
  274.8 0.8 place.14.refs_1_
  275.6 1.0 collective-permute-done.8.refs_0_
  277.3 0.8 copy-done.1
  278.1 1.9 place.12
  280.1 6.5 %place.8.refs_1_ = bf16[2048,2560]{1,0:T(8,128)(2,1)} custom-call(s32[1]{0:T(128)} %bitcast.me_ref, bf16[2048,640]{1,0:T(8,128)(2,1)} %collective-permute-done.2.refs_0_, bf16[2048,640]{1,0:T(8,128)(2,1)} %collective-permute-done.refs_1_, bf16[2048,2560]{1,0:T(8,128)(2,1)} %get-tuple-element.9.refs_2_), custom_call_target="tpu_custom_call", output_to_operand_aliasing={{}: (3, {})} | custom-call | flops 1310720 | bytes 5242880 | tf_op jit(solution)/shard_map/place/pallas_call | solution.py:152
  286.6 3.3 %place.9 = bf16[2048,2560]{1,0:T(8,128)(2,1)} custom-call(s32[1]{0:T(128)} %bitcast.me_ref, bf16[2048,640]{1,0:T(8,128)(2,1)} %collective-permute-done.1.refs_0_, bf16[2048,2560]{1,0:T(8,128)(2,1)} %place.8.refs_1_), custom_call_target="tpu_custom_call", output_to_operand_aliasing={{}: (2, {})} | custom-call | flops 1310720 | bytes 5242880 | tf_op jit(solution)/shard_map/place/pallas_call | solution.py:152
  (33 shorter events, 1.7 us)
Async XLA Ops:
  0.6 130.8 %copy-start.5 = (f32[320]{0:T(512)S(1)}, f32[320]{0:T(512)}, u32[]{:S(2)}) copy-start(f32[320]{0:T(512)} %param.20) | copy-start | bytes 3844
  0.6 130.8 %copy-start.6 = (f32[320]{0:T(512)S(1)}, f32[320]{0:T(512)}, u32[]{:S(2)}) copy-start(f32[320]{0:T(512)} %param.21) | copy-start | bytes 3844
  8.0 63.2 %collective-permute-start = (bf16[2048,640]{1,0:T(8,128)(2,1)}, bf16[2048,640]{1,0:T(8,128)(2,1)}, u32[]{:S(2)}, u32[]{:S(2)}) collective-permute-start(bf16[2048,640]{1,0:T(8,128)(2,1)} %get-tuple-element.8), channel_id=1, source_target_pairs={{2,4},{4,2},{6,0},{0,6},{3,5},{5,3},{7,1},{1,7},{10,12},{12,10},{1... | collective-permute-start | bytes 7864328 | tf_op jit(solution)/shard_map/ppermute | solution.py:299
  13.1 266.9 %collective-permute-start.2 = (bf16[2048,640]{1,0:T(8,128)(2,1)}, bf16[2048,640]{1,0:T(8,128)(2,1)}, u32[]{:S(2)}, u32[]{:S(2)}) collective-permute-start(bf16[2048,640]{1,0:T(8,128)(2,1)} %get-tuple-element.8), channel_id=1, source_target_pairs={{0,2},{2,0},{4,6},{6,4},{1,3},{3,1},{5,7},{7,5},{8,10},{10,8},{12,... | collective-permute-start | bytes 7864328 | tf_op jit(solution)/shard_map/ppermute | solution.py:299
  71.2 215.3 %collective-permute-start.1 = (bf16[2048,640]{1,0:T(8,128)(2,1)}, bf16[2048,640]{1,0:T(8,128)(2,1)}, u32[]{:S(2)}, u32[]{:S(2)}) collective-permute-start(bf16[2048,640]{1,0:T(8,128)(2,1)} %collective-permute-done.refs_1_), channel_id=1, source_target_pairs={{0,2},{2,0},{4,6},{6,4},{1,3},{3,1},{5,7},{7,5},{8,10},{10,8},{12,... | collective-permute-start | bytes 7864328 | tf_op jit(solution)/shard_map/ppermute | solution.py:299
  128.9 100.6 %collective-permute-start.3 = (bf16[512,640]{1,0:T(8,128)(2,1)S(1)}, bf16[512,640]{1,0:T(8,128)(2,1)S(1)}, u32[]{:S(2)}, u32[]{:S(2)}) collective-permute-start(bf16[512,640]{1,0:T(8,128)(2,1)S(1)} %pad_maximum_fusion.refs_0_), channel_id=1, source_target_pairs={{2,4},{4,2},{6,0},{0,6},{3,5},{5,3},{7,1},{1,7},{10,12},{12,10},{1... | collective-permute-start | bytes 1966088 | tf_op jit(solution)/shard_map/ppermute | solution.py:299
  131.4 6.8 %collective-permute-start.11 = (bf16[320]{0:T(512)(128)(2,1)S(1)}, bf16[320]{0:T(512)(128)(2,1)S(1)}, u32[]{:S(2)}, u32[]{:S(2)}) collective-permute-start(bf16[320]{0:T(512)(128)(2,1)S(1)} %add_convert_fusion), channel_id=1, source_target_pairs={{0,1},{1,0},{2,3},{3,2},{4,5},{5,4},{6,7},{7,6},{8,9},{9,8},{10,11... | collective-permute-start | bytes 1928 | tf_op jit(solution)/shard_map/ppermute | solution.py:310
  136.8 94.7 %collective-permute-start.7 = (bf16[512,640]{1,0:T(8,128)(2,1)}, bf16[512,640]{1,0:T(8,128)(2,1)S(1)}, u32[]{:S(2)}, u32[]{:S(2)}) collective-permute-start(bf16[512,640]{1,0:T(8,128)(2,1)} %get-tuple-element.10), channel_id=1, source_target_pairs={{2,4},{4,2},{6,0},{0,6},{3,5},{5,3},{7,1},{1,7},{10,12},{12,10},{1... | collective-permute-start | bytes 1966088 | tf_op jit(solution)/shard_map/ppermute | solution.py:299
  138.3 71.8 %collective-permute-start.12 = (bf16[640]{0:T(1024)(128)(2,1)S(1)}, bf16[640]{0:T(1024)(128)(2,1)S(1)}, u32[]{:S(2)}, u32[]{:S(2)}) collective-permute-start(bf16[640]{0:T(1024)(128)(2,1)S(1)} %pad_maximum_fusion.3), channel_id=1, source_target_pairs={{0,6},{2,0},{4,2},{6,4},{1,7},{3,1},{5,3},{7,5},{8,14},{10,8},{12,... | collective-permute-start | bytes 3848 | tf_op jit(solution)/shard_map/ppermute | solution.py:315
  210.1 4.8 %collective-permute-start.13 = (bf16[640]{0:T(1024)(128)(2,1)S(1)}, bf16[640]{0:T(1024)(128)(2,1)S(1)}, u32[]{:S(2)}, u32[]{:S(2)}) collective-permute-start(bf16[640]{0:T(1024)(128)(2,1)S(1)} %pad_maximum_fusion.3), channel_id=1, source_target_pairs={{0,4},{2,6},{4,0},{6,2},{1,5},{3,7},{5,1},{7,3},{8,12},{10,14},{12... | collective-permute-start | bytes 3848 | tf_op jit(solution)/shard_map/ppermute | solution.py:315
  214.8 5.5 %collective-permute-start.14 = (bf16[640]{0:T(1024)(128)(2,1)S(1)}, bf16[640]{0:T(1024)(128)(2,1)S(1)}, u32[]{:S(2)}, u32[]{:S(2)}) collective-permute-start(bf16[640]{0:T(1024)(128)(2,1)S(1)} %pad_maximum_fusion.3), channel_id=1, source_target_pairs={{0,2},{2,4},{4,6},{6,0},{1,3},{3,5},{5,7},{7,1},{8,10},{10,12},{12... | collective-permute-start | bytes 3848 | tf_op jit(solution)/shard_map/ppermute | solution.py:315
  220.3 9.1 %collective-permute-start.6 = (bf16[256,640]{1,0:T(8,128)(2,1)S(1)}, bf16[256,640]{1,0:T(8,128)(2,1)S(1)}, u32[]{:S(2)}, u32[]{:S(2)}) collective-permute-start(bf16[256,640]{1,0:T(8,128)(2,1)S(1)} %merge.6), channel_id=1, source_target_pairs={{0,2},{2,0},{4,6},{6,4},{1,3},{3,1},{5,7},{7,5},{8,10},{10,8},{12,... | collective-permute-start | bytes 983048 | tf_op jit(solution)/shard_map/ppermute | solution.py:299
  229.4 2.0 copy-start.3
  229.4 25.9 %collective-permute-start.10 = (bf16[512,640]{1,0:T(8,128)(2,1)}, bf16[512,640]{1,0:T(8,128)(2,1)}, u32[]{:S(2)}, u32[]{:S(2)}) collective-permute-start(bf16[512,640]{1,0:T(8,128)(2,1)} %get-tuple-element.10), channel_id=1, source_target_pairs={{0,2},{2,0},{4,6},{6,4},{1,3},{3,1},{5,7},{7,5},{8,10},{10,8},{12,... | collective-permute-start | bytes 1966088 | tf_op jit(solution)/shard_map/ppermute | solution.py:299
  229.5 30.6 %copy-start.2 = (bf16[512,640]{1,0:T(8,128)(2,1)}, bf16[512,640]{1,0:T(8,128)(2,1)S(1)}, u32[]{:S(2)}) copy-start(bf16[512,640]{1,0:T(8,128)(2,1)S(1)} %collective-permute-done.3.refs_1_) | copy-start | bytes 1966084
  229.5 24.9 %collective-permute-start.5 = (bf16[256,640]{1,0:T(8,128)(2,1)S(1)}, bf16[256,640]{1,0:T(8,128)(2,1)}, u32[]{:S(2)}, u32[]{:S(2)}) collective-permute-start(bf16[256,640]{1,0:T(8,128)(2,1)S(1)} %merge.5), channel_id=1, source_target_pairs={{0,2},{2,0},{4,6},{6,4},{1,3},{3,1},{5,7},{7,5},{8,10},{10,8},{12,... | collective-permute-start | bytes 983048 | tf_op jit(solution)/shard_map/ppermute | solution.py:299
  231.5 27.9 %copy-start = (bf16[512,640]{1,0:T(8,128)(2,1)}, bf16[512,640]{1,0:T(8,128)(2,1)S(1)}, u32[]{:S(2)}) copy-start(bf16[512,640]{1,0:T(8,128)(2,1)S(1)} %collective-permute-done.7.refs_1_) | copy-start | bytes 1966084
  231.5 45.8 %collective-permute-start.4 = (bf16[512,640]{1,0:T(8,128)(2,1)S(1)}, bf16[512,640]{1,0:T(8,128)(2,1)S(1)}, u32[]{:S(2)}, u32[]{:S(2)}) collective-permute-start(bf16[512,640]{1,0:T(8,128)(2,1)S(1)} %collective-permute-done.3.refs_1_), channel_id=1, source_target_pairs={{0,2},{2,0},{4,6},{6,4},{1,3},{3,1},{5,7},{7,5},{8,10},{10,8},{12,... | collective-permute-start | bytes 1966088 | tf_op jit(solution)/shard_map/ppermute | solution.py:299
  254.4 3.1 %copy-start.4 = (bf16[256,640]{1,0:T(8,128)(2,1)S(1)}, bf16[256,640]{1,0:T(8,128)(2,1)}, u32[]{:S(2)}) copy-start(bf16[256,640]{1,0:T(8,128)(2,1)} %copy-done.3) | copy-start | bytes 983044
  254.4 20.4 %collective-permute-start.9 = (bf16[384,640]{1,0:T(8,128)(2,1)}, bf16[384,640]{1,0:T(8,128)(2,1)S(1)}, u32[]{:S(2)}, u32[]{:S(2)}) collective-permute-start(bf16[384,640]{1,0:T(8,128)(2,1)} %slice.9), channel_id=1, source_target_pairs={{0,2},{2,0},{4,6},{6,4},{1,3},{3,1},{5,7},{7,5},{8,10},{10,8},{12,... | collective-permute-start | bytes 1474568 | tf_op jit(solution)/shard_map/ppermute | solution.py:299
  255.4 21.2 %collective-permute-start.8 = (bf16[128,640]{1,0:T(8,128)(2,1)S(1)}, bf16[128,640]{1,0:T(8,128)(2,1)S(1)}, u32[]{:S(2)}, u32[]{:S(2)}) collective-permute-start(bf16[128,640]{1,0:T(8,128)(2,1)S(1)} %slice.8), channel_id=1, source_target_pairs={{0,2},{2,0},{4,6},{6,4},{1,3},{3,1},{5,7},{7,5},{8,10},{10,8},{12,... | collective-permute-start | bytes 491528 | tf_op jit(solution)/shard_map/ppermute | solution.py:299
  277.3 0.8 copy-start.1
